TPU v7x, 32 devices: a whole 2x2x4 slice. The times are simulated.
32 devices in a mesh: dp: 8 (over y, x, core), fsdp: 4 (over z).
Axes of the slice: x: 2, y: 2, z: 4, core: 2. Of those that a mesh axis runs over, the one named last changes fastest.
Arguments:
- tokens: bfloat16 [19200, 1024], P(('dp', 'fsdp')), may hold values from -6 to 6
- cotangent: bfloat16 [19200, 1024], P(('dp', 'fsdp')), may hold values from -6 to 6
- crop_group: int32 [8], P('dp'), may hold values from 0 to 1, as said below
- group_tokens: int32 [2], replicated, may hold values from 1000 to 7999
- qkv_weight: float32 [1024, 3072], P('fsdp'), may hold values from -0.1875 to 0.1875
- query_bias: float32 [1024], P('fsdp'), may hold values from -2 to 2
- value_bias: float32 [1024], P('fsdp'), may hold values from -2 to 2
- out_weight: float32 [1024, 1024], P('fsdp'), may hold values from -0.375 to 0.375
- out_bias: float32 [1024], P('fsdp'), may hold values from -2 to 2
- attn_gain: float32 [1024], P('fsdp'), may hold values from 0.5 to 1.5
- attn_shift: float32 [1024], P('fsdp'), may hold values from -2 to 2
- mlp_gain: float32 [1024], P('fsdp'), may hold values from 0.5 to 1.5
- mlp_shift: float32 [1024], P('fsdp'), may hold values from -2 to 2
- up_weight: float32 [1024, 4096], P('fsdp'), may hold values from -0.1875 to 0.1875
- up_bias: float32 [4096], P('fsdp'), may hold values from -2 to 2
- down_weight: float32 [4096, 1024], P('fsdp'), may hold values from -0.09375 to 0.09375
- down_bias: float32 [1024], P('fsdp'), may hold values from -2 to 2
Outputs:
- mixed_out: bfloat16 [19200, 1024], P(('dp', 'fsdp'))
- grad_tokens: bfloat16 [19200, 1024], P(('dp', 'fsdp'))
- grad_qkv_weight: float32 [1024, 3072], P('fsdp')
- grad_query_bias: float32 [1024], P('fsdp')
- grad_value_bias: float32 [1024], P('fsdp')
- grad_out_weight: float32 [1024, 1024], P('fsdp')
- grad_out_bias: float32 [1024], P('fsdp')
- grad_attn_gain: float32 [1024], P('fsdp')
- grad_attn_shift: float32 [1024], P('fsdp')
- grad_mlp_gain: float32 [1024], P('fsdp')
- grad_mlp_shift: float32 [1024], P('fsdp')
- grad_up_weight: float32 [1024, 4096], P('fsdp')
- grad_up_bias: float32 [4096], P('fsdp')
- grad_down_weight: float32 [4096, 1024], P('fsdp')
- grad_down_bias: float32 [1024], P('fsdp')
Inputs may be any that keep to these rules, and one draw needn't show every extreme that they name: `crop_group`: exactly 5 entries are 1 and the others 0.
All inputs are finite; a program needn't handle non-finite values.
Results may differ from a plain program's by a relative error of at most 0.02.
Values may be sent and summed in bfloat16 or wider, within the bound.
A program may use at most 192 MiB of HBM per device.

v0:
```python
import functools

import jax
import jax.numpy as jnp
from jax import lax
from jax.sharding import PartitionSpec as P


D = 1024
HEADS = 16
HEAD_DIM = 64
GLEN = 50
LLEN = 10


EPSILON = 1e-06
BIG_NEGATIVE = -1000000000.0
ROOT_HALF = 0.7071067811865476
INV_ROOT_TAU = 0.3989422804014327


def normalize(values):
    middle = jnp.mean(values, axis=-1, keepdims=True)
    centered = values - middle
    inverse = lax.rsqrt(jnp.mean(centered * centered, axis=-1, keepdims=True) + EPSILON)
    return (centered * inverse, inverse)


def norm_back(grad_out, gain, scaled, inverse):
    grad_scaled = grad_out * gain
    return inverse * (
        grad_scaled
        - jnp.mean(grad_scaled, axis=-1, keepdims=True)
        - scaled * jnp.mean(grad_scaled * scaled, axis=-1, keepdims=True)
    )


def by_crops(values, crop):
    return values.reshape(values.shape[0] // crop, crop, HEADS, HEAD_DIM)


def crop_scores(queries, key_rows):
    factor = HEAD_DIM ** (-0.5)
    return (
        jnp.einsum("cqhd,ckhd->chqk", queries, key_rows, preferred_element_type=jnp.float32)
        * factor
    )


def crop_mask(crop):
    segment = lax.iota(jnp.int32, GLEN) // crop
    return segment[:, None] == segment[None, :]


def attend_crops(queries, key_rows, value_rows, crop):
    length = queries.shape[0]
    crop_q, crop_k, crop_v = (
        by_crops(queries, GLEN),
        by_crops(key_rows, GLEN),
        by_crops(value_rows, GLEN),
    )
    scores = jnp.where(crop_mask(crop), crop_scores(crop_q, crop_k), BIG_NEGATIVE)
    highest = jnp.max(scores, axis=-1, keepdims=True)
    exponent = jnp.exp(scores - highest)
    summed = jnp.sum(exponent, axis=-1, keepdims=True)
    attention = (exponent / summed).astype(jnp.bfloat16)
    context = jnp.einsum("chqk,ckhd->cqhd", attention, crop_v, preferred_element_type=jnp.float32)
    logsum = (highest + jnp.log(summed))[..., 0]
    return (
        context.reshape(length, HEADS * HEAD_DIM),
        jnp.transpose(logsum, (0, 2, 1)).reshape(length, HEADS),
    )


def attend_crops_back(queries, key_rows, value_rows, logsum, grad_context, crop):
    length = queries.shape[0]
    factor = HEAD_DIM ** (-0.5)
    crop_q, crop_k, crop_v = (
        by_crops(queries, GLEN),
        by_crops(key_rows, GLEN),
        by_crops(value_rows, GLEN),
    )
    crop_g = by_crops(grad_context, GLEN)
    crop_l = jnp.transpose(logsum.reshape(length // GLEN, GLEN, HEADS), (0, 2, 1))
    scores = jnp.where(crop_mask(crop), crop_scores(crop_q, crop_k), BIG_NEGATIVE)
    probs = jnp.exp(scores - crop_l[..., None])
    probs_low = probs.astype(jnp.bfloat16)
    grad_values = jnp.einsum(
        "chqk,cqhd->ckhd", probs_low, crop_g, preferred_element_type=jnp.float32
    )
    grad_probs = jnp.einsum("cqhd,ckhd->chqk", crop_g, crop_v, preferred_element_type=jnp.float32)
    delta = jnp.sum(probs * grad_probs, axis=-1, keepdims=True)
    grad_scores = (probs * (grad_probs - delta)).astype(jnp.bfloat16)
    grad_queries = (
        jnp.einsum("chqk,ckhd->cqhd", grad_scores, crop_k, preferred_element_type=jnp.float32)
        * factor
    )
    grad_keys = (
        jnp.einsum("chqk,cqhd->ckhd", grad_scores, crop_q, preferred_element_type=jnp.float32)
        * factor
    )
    width = HEADS * HEAD_DIM
    return jnp.concatenate(
        [
            grad_queries.reshape(length, width),
            grad_keys.reshape(length, width),
            grad_values.reshape(length, width),
        ],
        axis=1,
    ).astype(jnp.bfloat16)


def xor_pairs(n, mask):
    return [(i, i ^ mask) for i in range(n)]


def exchange(leaves, held, bit, d, n_dp):
    got = lax.ppermute(leaves, "dp", xor_pairs(n_dp, 1 << bit))
    pos = sum(1 for b in held if b > bit)
    mine = ((d >> bit) & 1) == 0
    out = [
        jnp.where(mine, jnp.stack([a, g], axis=pos), jnp.stack([g, a], axis=pos))
        for a, g in zip(leaves, got)
    ]
    return out, sorted(held + [bit], reverse=True)


def split_bit(leaves, held, bit, d, n_dp, lead):
    axis = lead + held.index(bit)
    mine = (d >> bit) & 1
    send = [lax.dynamic_index_in_dim(a, 1 - mine, axis, keepdims=False) for a in leaves]
    keep = [lax.dynamic_index_in_dim(a, mine, axis, keepdims=False) for a in leaves]
    got = lax.ppermute([v.astype(jnp.bfloat16) for v in send], "dp", xor_pairs(n_dp, 1 << bit))
    return [k.astype(jnp.float32) + g.astype(jnp.float32) for k, g in zip(keep, got)], [b for b in held if b != bit]


def chip_bits(n_dp):
    return list(range(1, n_dp.bit_length() - 1))


def gather_chain(shard, vec, n_dp, n_fsdp):
    d = lax.axis_index("dp")
    f = lax.axis_index("fsdp")
    rows, cols = shard.shape
    pieces = shard.reshape(n_dp, 2, rows // (2 * n_dp), cols)
    own = lax.dynamic_index_in_dim(pieces, d, 0, keepdims=False)
    down = [(i, (i - 1) % n_fsdp) for i in range(n_fsdp)]
    ring, vring = [], []
    buf = [own] + ([vec] if vec is not None else [])
    for _ in range(1, n_fsdp):
        buf = lax.ppermute(buf, "fsdp", down)
        ring.append(buf[0])
        if vec is not None:
            vring.append(buf[1])
    vecs = None
    if vec is not None:
        vecs = jnp.roll(jnp.stack([vec] + vring, axis=0), f, axis=0)
    if n_fsdp == 1:
        return shard, vecs
    zrel = jnp.stack(ring, axis=0)
    halves = []
    for h in range(2):
        order = chip_bits(n_dp)
        order = order if h == 0 else order[::-1]
        leaves, held = [zrel[:, h]], []
        for bit in order:
            leaves, held = exchange(leaves, held, bit, d, n_dp)
        halves.append(leaves[0])
    both = jnp.stack(halves, axis=-3)
    held = chip_bits(n_dp)[::-1]
    if n_dp > 1:
        (both,), held = exchange([both], held, 0, d, n_dp)
    plane = both.reshape((n_dp, n_fsdp - 1) + both.shape[-3:])
    rel = jnp.concatenate([pieces[None], jnp.swapaxes(plane, 0, 1)], axis=0)
    return jnp.roll(rel, f, axis=0).reshape(n_fsdp * rows, cols), vecs


def reduce_chain(grads, n_dp, n_fsdp):
    d = lax.axis_index("dp")
    f = lax.axis_index("fsdp")
    bits = n_dp.bit_length() - 1
    leaves = [
        g.astype(jnp.bfloat16).reshape((n_fsdp,) + (2,) * bits + (2, g.shape[0] // (n_fsdp * 2 * n_dp), g.shape[1]))
        for g in grads
    ]
    held = list(range(bits - 1, -1, -1))
    if bits > 0:
        leaves, held = split_bit(leaves, held, 0, d, n_dp, 1)
    finals = []
    for h in range(2):
        order = chip_bits(n_dp)
        order = order[::-1] if h == 0 else order
        part = [lax.index_in_dim(a, h, 1 + len(held), keepdims=False) for a in leaves]
        hb = list(held)
        for bit in order:
            part, hb = split_bit(part, hb, bit, d, n_dp, 1)
        finals.append(part)
    acc = [jnp.stack([finals[0][i], finals[1][i]], axis=1) for i in range(len(grads))]
    down = [(i, (i - 1) % n_fsdp) for i in range(n_fsdp)]
    if n_fsdp == 1:
        send = [a[0].astype(jnp.bfloat16) for a in acc]
    else:
        send = [lax.dynamic_index_in_dim(a, (f + 1) % n_fsdp, 0, keepdims=False).astype(jnp.bfloat16) for a in acc]
    for step in range(1, n_fsdp):
        got = lax.ppermute(send, "fsdp", down)
        chunk = (f + 1 + step) % n_fsdp
        send = [
            (g.astype(jnp.float32) + lax.dynamic_index_in_dim(a, chunk, 0, keepdims=False)).astype(jnp.bfloat16)
            for g, a in zip(got, acc)
        ]
    halves = []
    for h in range(2):
        order = chip_bits(n_dp)
        order = order if h == 0 else order[::-1]
        part, hb = [v[h] for v in send], []
        for bit in order:
            part, hb = exchange(part, hb, bit, d, n_dp)
        halves.append(part)
    both = [jnp.stack([halves[0][i], halves[1][i]], axis=len(hb)) for i in range(len(grads))]
    if n_dp > 1:
        both, hb = exchange(both, hb, 0, d, n_dp)
    return [b.reshape(g.shape[0] // n_fsdp, g.shape[1]).astype(jnp.float32) for b, g in zip(both, grads)]


def gather_weights_native(shards):
    return [lax.all_gather(s, "fsdp", axis=0, tiled=True) for s in shards]


def reduce_weights_native(grads):
    return [
        lax.psum(lax.psum_scatter(g, "fsdp", scatter_dimension=0, tiled=True), "dp").astype(jnp.float32)
        for g in grads
    ]


def unpack_vectors(packed, sizes, n_fsdp):
    rows = packed.reshape(n_fsdp, -1)
    out = []
    offset = 0
    for size in sizes:
        width = size // n_fsdp
        out.append(rows[:, offset : offset + width].reshape(size))
        offset += width
    return out


def column_sums(values):
    return jnp.sum(values.astype(jnp.float32), axis=0)


def local_body(
    tokens,
    cotangent,
    crop_group,
    group_tokens,
    qkv_weight,
    query_bias,
    value_bias,
    out_weight,
    out_bias,
    attn_gain,
    attn_shift,
    mlp_gain,
    mlp_shift,
    up_weight,
    up_bias,
    down_weight,
    down_bias,
    n_dp,
    n_fsdp,
):
    small = n_dp * n_fsdp <= 64
    vectors = (query_bias, value_bias, out_bias, attn_gain, attn_shift, mlp_gain, mlp_shift, up_bias, down_bias)
    sizes = [v.shape[0] * n_fsdp for v in vectors]
    vec_local = jnp.concatenate([v.astype(jnp.bfloat16) for v in vectors])
    low = [w.astype(jnp.bfloat16) for w in (qkv_weight, out_weight, up_weight, down_weight)]
    if small:
        qkv_low, vec_rows = gather_chain(low[0], vec_local, n_dp, n_fsdp)
        out_low, _ = gather_chain(low[1], None, n_dp, n_fsdp)
        up_low, _ = gather_chain(low[2], None, n_dp, n_fsdp)
        down_low, _ = gather_chain(low[3], None, n_dp, n_fsdp)
    else:
        qkv_low, out_low, up_low, down_low = gather_weights_native(low)
        vec_rows = lax.all_gather(vec_local, "fsdp", axis=0, tiled=False)
    (
        query_add,
        value_add,
        out_add,
        gain_one,
        shift_one,
        gain_two,
        shift_two,
        up_add,
        down_add,
    ) = [v.astype(jnp.float32) for v in unpack_vectors(vec_rows, sizes, n_fsdp)]
    is_global = crop_group[0] == 1
    totals = (group_tokens[0] + group_tokens[1]).astype(jnp.float32)
    loss_share = jnp.where(is_global, group_tokens[1], group_tokens[0]).astype(jnp.float32) / totals
    inputs = tokens.astype(jnp.float32)
    scaled_one, inverse_one = normalize(inputs)
    normed_one = (scaled_one * gain_one + shift_one).astype(jnp.bfloat16)
    projected = jnp.dot(normed_one, qkv_low, preferred_element_type=jnp.float32)
    projected = projected + jnp.concatenate([query_add, jnp.zeros_like(query_add), value_add])
    projected_low = projected.astype(jnp.bfloat16)
    queries = projected_low[:, :D]
    key_rows = projected_low[:, D : 2 * D]
    value_rows = projected_low[:, 2 * D :]
    crop = jnp.where(is_global, GLEN, LLEN)
    context, logsum = attend_crops(queries, key_rows, value_rows, crop)
    context_low = context.astype(jnp.bfloat16)
    middle = inputs + (jnp.dot(context_low, out_low, preferred_element_type=jnp.float32) + out_add)
    scaled_two, inverse_two = normalize(middle)
    normed_two = (scaled_two * gain_two + shift_two).astype(jnp.bfloat16)
    preacts = jnp.dot(normed_two, up_low, preferred_element_type=jnp.float32) + up_add
    error_part = 1.0 + jax.scipy.special.erf(preacts * ROOT_HALF)
    activated = (0.5 * preacts * error_part).astype(jnp.bfloat16)
    mixed_out = (
        middle + (jnp.dot(activated, down_low, preferred_element_type=jnp.float32) + down_add)
    ).astype(jnp.bfloat16)
    upstream = cotangent.astype(jnp.float32) * loss_share
    upstream_low = upstream.astype(jnp.bfloat16)
    grad_down_weight = jnp.dot(activated.T, upstream_low, preferred_element_type=jnp.float32)
    grad_down_bias = column_sums(upstream_low)
    grad_activated = jnp.dot(upstream_low, down_low.T, preferred_element_type=jnp.float32)
    slope = 0.5 * error_part + preacts * jnp.exp(-0.5 * preacts * preacts) * INV_ROOT_TAU
    grad_preacts = (grad_activated * slope).astype(jnp.bfloat16)
    grad_up_weight = jnp.dot(normed_two.T, grad_preacts, preferred_element_type=jnp.float32)
    grad_up_bias = column_sums(grad_preacts)
    grad_normed_two = jnp.dot(grad_preacts, up_low.T, preferred_element_type=jnp.float32)
    grad_mlp_gain = jnp.sum(grad_normed_two * scaled_two, axis=0)
    grad_mlp_shift = jnp.sum(grad_normed_two, axis=0)
    grad_middle = upstream + norm_back(grad_normed_two, gain_two, scaled_two, inverse_two)
    grad_branch = grad_middle.astype(jnp.bfloat16)
    grad_out_weight = jnp.dot(context_low.T, grad_branch, preferred_element_type=jnp.float32)
    grad_out_bias = column_sums(grad_branch)
    grad_context = jnp.dot(grad_branch, out_low.T, preferred_element_type=jnp.float32).astype(
        jnp.bfloat16
    )
    grad_projected = attend_crops_back(queries, key_rows, value_rows, logsum, grad_context, crop)
    grad_qkv_weight = jnp.dot(normed_one.T, grad_projected, preferred_element_type=jnp.float32)
    grad_query_bias = column_sums(grad_projected[:, :D])
    grad_value_bias = column_sums(grad_projected[:, 2 * D :])
    grad_normed_one = jnp.dot(grad_projected, qkv_low.T, preferred_element_type=jnp.float32)
    grad_attn_gain = jnp.sum(grad_normed_one * scaled_one, axis=0)
    grad_attn_shift = jnp.sum(grad_normed_one, axis=0)
    grad_tokens = (
        grad_middle + norm_back(grad_normed_one, gain_one, scaled_one, inverse_one)
    ).astype(jnp.bfloat16)
    grad_vectors = (
        grad_query_bias,
        grad_value_bias,
        grad_out_bias,
        grad_attn_gain,
        grad_attn_shift,
        grad_mlp_gain,
        grad_mlp_shift,
        grad_up_bias,
        grad_down_bias,
    )
    vec_grads = jnp.concatenate(
        [g.astype(jnp.bfloat16).reshape(n_fsdp, -1) for g in grad_vectors], axis=1
    )
    if small:
        (grad_down_shard,) = reduce_chain([grad_down_weight], n_dp, n_fsdp)
        (grad_up_shard,) = reduce_chain([grad_up_weight], n_dp, n_fsdp)
        (grad_out_shard,) = reduce_chain([grad_out_weight], n_dp, n_fsdp)
        grad_qkv_shard, vec_flat = reduce_chain(
            [grad_qkv_weight, vec_grads.reshape(n_fsdp * 2 * n_dp, -1)], n_dp, n_fsdp
        )
    else:
        grad_qkv_shard, grad_out_shard, grad_up_shard, grad_down_shard = reduce_weights_native(
            [w.astype(jnp.bfloat16) for w in (grad_qkv_weight, grad_out_weight, grad_up_weight, grad_down_weight)],
        )
        (vec_flat,) = reduce_weights_native([vec_grads])
    vec_out = unpack_vectors(vec_flat.reshape(1, -1), [s // n_fsdp for s in sizes], 1)
    return (
        mixed_out,
        grad_tokens,
        grad_qkv_shard,
        vec_out[0],
        vec_out[1],
        grad_out_shard,
        vec_out[2],
        vec_out[3],
        vec_out[4],
        vec_out[5],
        vec_out[6],
        grad_up_shard,
        vec_out[7],
        grad_down_shard,
        vec_out[8],
    )


def solution(mesh):
    placed = (
        P(("dp", "fsdp"), None),
        P(("dp", "fsdp"), None),
        P("dp"),
        P(),
        P("fsdp", None),
        P("fsdp"),
        P("fsdp"),
        P("fsdp", None),
        P("fsdp"),
        P("fsdp"),
        P("fsdp"),
        P("fsdp"),
        P("fsdp"),
        P("fsdp", None),
        P("fsdp"),
        P("fsdp", None),
        P("fsdp"),
    )
    n_dp = mesh.shape["dp"]
    n_fsdp = mesh.shape["fsdp"]
    return jax.shard_map(
        functools.partial(local_body, n_dp=n_dp, n_fsdp=n_fsdp),
        mesh=mesh,
        in_specs=placed,
        out_specs=(
            P(("dp", "fsdp"), None),
            P(("dp", "fsdp"), None),
            P("fsdp", None),
            P("fsdp"),
            P("fsdp"),
            P("fsdp", None),
            P("fsdp"),
            P("fsdp"),
            P("fsdp"),
            P("fsdp"),
            P("fsdp"),
            P("fsdp", None),
            P("fsdp"),
            P("fsdp", None),
            P("fsdp"),
        ),
        check_vma=False,
    )
```

profile of v0, /device:TPU:0, one launch (start us, length us, event | category | flops | bytes accessed | tf_op | source)
XLA Modules:
  0.0 662.2 jit_solution(5380769989371825510)
XLA Ops:
  29.7 6.8 %collective-permute-done.1 = bf16[3072]{0:T(1024)(128)(2,1)S(1)} collective-permute-done((bf16[3072]{0:T(1024)(128)(2,1)S(1)}, bf16[3072]{0:T(1024)(128)(2,1)S(1)}, u32[]{:S(2)}, u32[]{:S(2)}) %collective-permute-start.1) | collective-permute-done | bytes 6176 | tf_op jit(solution)/shard_map/ppermute | solution.py:151
  88.5 7.2 %collective-permute-done.22 = bf16[3,16,4096]{2,1,0:T(8,128)(2,1)S(1)} collective-permute-done((bf16[3,16,4096]{2,1,0:T(8,128)(2,1)S(1)}, bf16[3,16,4096]{2,1,0:T(8,128)(2,1)S(1)}, u32[]{:S(2)}, u32[]{:S(2)}) %collective-permute-start.22) | collective-permute-done | bytes 393248 | tf_op jit(solution)/shard_map/ppermute | solution.py:118
  97.7 6.4 collective-permute-done.30
  106.3 10.5 %collective-permute-done.9 = bf16[2,3,16,3072]{3,2,1,0:T(8,128)(2,1)S(1)} collective-permute-done((bf16[2,3,16,3072]{3,2,1,0:T(8,128)(2,1)S(1)}, bf16[2,3,16,3072]{3,2,1,0:T(8,128)(2,1)S(1)}, u32[]{:S(2)}, u32[]{:S(2)}) %collective-permute-start.9) | collective-permute-done | bytes 589856 | tf_op jit(solution)/shard_map/ppermute | solution.py:118
  122.3 11.3 %collective-permute-done.25 = bf16[2,3,16,4096]{3,2,1,0:T(8,128)(2,1)S(1)} collective-permute-done((bf16[2,3,16,4096]{3,2,1,0:T(8,128)(2,1)S(1)}, bf16[2,3,16,4096]{3,2,1,0:T(8,128)(2,1)S(1)}, u32[]{:S(2)}, u32[]{:S(2)}) %collective-permute-start.25) | collective-permute-done | bytes 786464 | tf_op jit(solution)/shard_map/ppermute | solution.py:118
  137.3 10.2 %collective-permute-done.33 = bf16[2,3,64,1024]{3,2,1,0:T(8,128)(2,1)S(1)} collective-permute-done((bf16[2,3,64,1024]{3,2,1,0:T(8,128)(2,1)S(1)}, bf16[2,3,64,1024]{3,2,1,0:T(8,128)(2,1)S(1)}, u32[]{:S(2)}, u32[]{:S(2)}) %collective-permute-start.33) | collective-permute-done | bytes 786464 | tf_op jit(solution)/shard_map/ppermute | solution.py:118
  204.8 6.5 fusion.11
  211.3 7.9 %copy.185 = bf16[4,8,2,16,4096]{4,3,2,1,0:T(8,128)(2,1)} copy(bf16[4,8,2,16,4096]{4,3,2,0,1:T(8,128)(2,1)} %fusion.11) | data formatting | bytes 16777216 | tf_op jit(solution)/shard_map/jit(_roll_dynamic)/dynamic_slice | solution.py:175
  223.3 6.5 fusion.8
  229.8 8.5 %copy.189 = bf16[4,8,2,64,1024]{4,3,2,1,0:T(8,128)(2,1)} copy(bf16[4,8,2,64,1024]{4,3,2,0,1:T(8,128)(2,1)} %fusion.8) | data formatting | bytes 16777216 | tf_op jit(solution)/shard_map/jit(_roll_dynamic)/dynamic_slice | solution.py:175
  238.3 12.0 %multiply_convert_fusion = (bf16[600,4096]{1,0:T(8,128)(2,1)}, f32[600,4096]{1,0:T(8,128)}) fusion(f32[4096]{0:T(1024)S(1)} %bitcast.729, bf16[1024,4096]{1,0:T(8,128)(2,1)} %bitcast.635, f32[600,1024]{1,0:T(8,128)S(1)} %copy-done.14, f32[1024]{0:T(1024)S(1)} %bitcast.744, f32[1024]{0:T(1024)S(1)} %bitcast.719, f32[600]{0:T(1024)S(1)} %add_rsqrt_fusion, ...), kind=kOutput, calls=%fused_computation.19 | convolution fusion | flops 5050982400 | bytes 25621184 | tf_op jit(solution)/shard_map/dot_general | solution.py:314
  250.4 13.8 %fusion.226 = (bf16[4096]{0:T(1024)(128)(2,1)S(1)}, bf16[600,4096]{1,0:T(8,128)(2,1)}) fusion(f32[600,4096]{1,0:T(8,128)} %get-tuple-element.134, f32[4096]{0:T(1024)S(1)} %bitcast.730, bf16[4096,1024]{1,0:T(8,128)(2,1)S(1)} %bitcast.631, bf16[600,1024]{1,0:T(8,128)(2,1)S(1)} %copy-done.33, f32[]{:T(128)} %bitcast.114), kind=kOutput, calls=%fused_computation.527 | convolution fusion | flops 5064495104 | bytes 24387588 | tf_op jit(solution)/shard_map/dot_general | solution.py:324
  264.2 10.1 %multiply_reduce_fusion.1 = (bf16[1024]{0:T(1024)(128)(2,1)S(1)}, f32[600]{0:T(1024)S(1)}, f32[600]{0:T(1024)S(1)}, bf16[1024]{0:T(1024)(128)(2,1)S(1)}, f32[600,1024]{1,0:T(8,128)S(1)}) fusion(f32[600,1024]{1,0:T(8,128)S(1)} %copy-done.14, f32[600]{0:T(1024)S(1)} %add_rsqrt_fusion, f32[600]{0:T(1024)S(1)} %broadcast_multiply_fusion.4, ...), kind=kOutput, calls=%fused_computation.120 | convolution fusion | flops 5038691328 | bytes 18236800 | tf_op jit(solution)/shard_map/dot_general | solution.py:329
  281.0 9.6 %convolution_convert_fusion = bf16[1024,4096]{1,0:T(8,128)(2,1)} fusion(bf16[600,4096]{1,0:T(8,128)(2,1)S(1)} %bitcast.761, f32[600,1024]{1,0:T(8,128)S(1)} %copy-done.14, f32[1024]{0:T(1024)S(1)} %bitcast.745, f32[1024]{0:T(1024)S(1)} %bitcast.722, f32[600]{0:T(1024)S(1)} %add_rsqrt_fusion, f32[600]{0:T(1024)S(1)} %broadcast_multiply_fusion.4), kind=kOutput, calls=%fused_computation.29 | convolution fusion | flops 5040431104 | bytes 15774400 | tf_op jit(solution)/shard_map/dot_general | solution.py:327
  293.4 6.6 fusion.225
  332.6 9.8 %fusion.48 = (bf16[1024]{0:T(1024)(128)(2,1)S(1)}, f32[600]{0:T(1024)S(1)}, f32[600]{0:T(1024)S(1)}, bf16[1024]{0:T(1024)(128)(2,1)S(1)}, f32[600,1024]{1,0:T(8,128)}) fusion(bf16[600,1024]{1,0:T(8,128)(2,1)S(1)} %copy-done.6, f32[600]{0:T(1024)S(1)} %add_rsqrt_fusion.1, f32[600]{0:T(1024)S(1)} %broadcast_multiply_fusion.5, f32[1024]{0:T(1024)S(1)} %bitcast.724, ...), kind=kOutput, calls=%fused_computation.118 | convolution fusion | flops 3781014528 | bytes 13682048 | tf_op jit(solution)/shard_map/dot_general | solution.py:343
  342.4 7.5 %convolution_convert_fusion.2 = bf16[1024,3072]{1,0:T(8,128)(2,1)} fusion(bf16[600,3072]{1,0:T(8,128)(2,1)S(1)} %copy-done.36, bf16[600,1024]{1,0:T(8,128)(2,1)S(1)} %copy-done.6, f32[1024]{0:T(1024)S(1)} %bitcast.743, f32[1024]{0:T(1024)S(1)} %bitcast.725, f32[600]{0:T(1024)S(1)} %add_rsqrt_fusion.1, f32[600]{0:T(1024)S(1)} %broadcast_multiply_fusion.5), kind=kOutput, calls=%fused_computation.38 | convolution fusion | flops 3781705728 | bytes 11219648 | tf_op jit(solution)/shard_map/dot_general | solution.py:340
  350.0 9.3 %convolution_convert_fusion.1 = bf16[4096,1024]{1,0:T(8,128)(2,1)} fusion(bf16[600,4096]{1,0:T(8,128)(2,1)S(1)} %bitcast.763, bf16[600,1024]{1,0:T(8,128)(2,1)S(1)} %copy-done.34, f32[]{:T(128)} %bitcast.114), kind=kOutput, calls=%fused_computation.30 | convolution fusion | flops 5039202304 | bytes 14532612 | tf_op jit(solution)/shard_map/dot_general | solution.py:322
  461.5 8.7 %collective-permute-done.36 = bf16[4,2,16,3072]{3,2,0,1:T(8,128)(2,1)S(1)} collective-permute-done((bf16[4,2,16,3072]{3,2,0,1:T(8,128)(2,1)S(1)}, bf16[4,2,16,3072]{3,2,0,1:T(8,128)(2,1)S(1)}, u32[]{:S(2)}, u32[]{:S(2)}) %collective-permute-start.36) | collective-permute-done | bytes 786464 | tf_op jit(solution)/shard_map/ppermute | solution.py:133
  470.7 9.2 %collective-permute-done.38 = bf16[4,2,16,3072]{3,2,1,0:T(8,128)(2,1)S(1)} collective-permute-done((bf16[4,2,16,3072]{3,2,1,0:T(8,128)(2,1)S(1)}, bf16[4,2,16,3072]{3,2,1,0:T(8,128)(2,1)S(1)}, u32[]{:S(2)}, u32[]{:S(2)}) %collective-permute-start.38) | collective-permute-done | bytes 786464 | tf_op jit(solution)/shard_map/ppermute | solution.py:133
  521.4 25.4 %collective-permute-done.45 = bf16[16,3072]{1,0:T(8,128)(2,1)S(1)} collective-permute-done((bf16[16,3072]{1,0:T(8,128)(2,1)S(1)}, bf16[16,3072]{1,0:T(8,128)(2,1)S(1)}, u32[]{:S(2)}, u32[]{:S(2)}) %collective-permute-start.45) | collective-permute-done | bytes 98336 | tf_op jit(solution)/shard_map/ppermute | solution.py:118
  553.5 6.4 collective-permute-done.46
  568.1 17.8 %collective-permute-done.90 = bf16[4,2,64,1024]{3,2,1,0:T(8,128)(2,1)S(1)} collective-permute-done((bf16[4,2,64,1024]{3,2,1,0:T(8,128)(2,1)S(1)}, bf16[4,2,64,1024]{3,2,1,0:T(8,128)(2,1)S(1)}, u32[]{:S(2)}, u32[]{:S(2)}) %collective-permute-start.90) | collective-permute-done | bytes 1048608 | tf_op jit(solution)/shard_map/ppermute | solution.py:133
  587.6 9.5 %collective-permute-done.76 = bf16[4,16,4096]{2,1,0:T(8,128)(2,1)S(1)} collective-permute-done((bf16[4,16,4096]{2,1,0:T(8,128)(2,1)S(1)}, bf16[4,16,4096]{2,1,0:T(8,128)(2,1)S(1)}, u32[]{:S(2)}, u32[]{:S(2)}) %collective-permute-start.76) | collective-permute-done | bytes 524320 | tf_op jit(solution)/shard_map/ppermute | solution.py:133
  (591 shorter events, 418.2 us)
Async XLA Ops:
  15.0 26.6 %collective-permute-start.11 = (bf16[2,16,1024]{2,1,0:T(8,128)(2,1)S(1)}, bf16[2,16,1024]{2,1,0:T(8,128)(2,1)S(1)}, u32[]{:S(2)}, u32[]{:S(2)}) collective-permute-start(bf16[2,16,1024]{2,1,0:T(8,128)(2,1)S(1)} %dynamic-slice_bitcast_fusion.7), channel_id=1, source_target_pairs={{0,3},{1,0},{2,1},{3,2},{4,7},{5,4},{6,5},{7,6},{8,11},{9,8},{10,9... | collective-permute-start | bytes 196616 | tf_op jit(solution)/shard_map/ppermute | solution.py:151
  19.1 36.4 %collective-permute-start.3 = (bf16[2,16,3072]{2,1,0:T(8,128)(2,1)S(1)}, bf16[2,16,3072]{2,1,0:T(8,128)(2,1)S(1)}, u32[]{:S(2)}, u32[]{:S(2)}) collective-permute-start(bf16[2,16,3072]{2,1,0:T(8,128)(2,1)S(1)} %dynamic-slice_bitcast_fusion.6), channel_id=1, source_target_pairs={{0,3},{1,0},{2,1},{3,2},{4,7},{5,4},{6,5},{7,6},{8,11},{9,8},{10,9... | collective-permute-start | bytes 589832 | tf_op jit(solution)/shard_map/ppermute | solution.py:151
  21.2 38.5 %collective-permute-start.19 = (bf16[2,16,4096]{2,1,0:T(8,128)(2,1)S(1)}, bf16[2,16,4096]{2,1,0:T(8,128)(2,1)S(1)}, u32[]{:S(2)}, u32[]{:S(2)}) collective-permute-start(bf16[2,16,4096]{2,1,0:T(8,128)(2,1)S(1)} %dynamic-slice_bitcast_fusion.5), channel_id=1, source_target_pairs={{0,3},{1,0},{2,1},{3,2},{4,7},{5,4},{6,5},{7,6},{8,11},{9,8},{10,9... | collective-permute-start | bytes 786440 | tf_op jit(solution)/shard_map/ppermute | solution.py:151
  23.7 36.1 %collective-permute-start.27 = (bf16[2,64,1024]{2,1,0:T(8,128)(2,1)S(1)}, bf16[2,64,1024]{2,1,0:T(8,128)(2,1)S(1)}, u32[]{:S(2)}, u32[]{:S(2)}) collective-permute-start(bf16[2,64,1024]{2,1,0:T(8,128)(2,1)S(1)} %dynamic-slice_bitcast_fusion.4), channel_id=1, source_target_pairs={{0,3},{1,0},{2,1},{3,2},{4,7},{5,4},{6,5},{7,6},{8,11},{9,8},{10,9... | collective-permute-start | bytes 786440 | tf_op jit(solution)/shard_map/ppermute | solution.py:151
  69.6 49.6 %collective-permute-start.18 = (bf16[2,2,3,2,16,1024]{5,4,3,2,1,0:T(8,128)(2,1)S(1)}, bf16[2,2,3,2,16,1024]{5,4,3,2,1,0:T(8,128)(2,1)S(1)}, u32[]{:S(2)}, u32[]{:S(2)}) collective-permute-start(bf16[2,2,3,2,16,1024]{5,4,3,2,1,0:T(8,128)(2,1)S(1)} %get-tuple-element.62), channel_id=1, source_target_pairs={{0,4},{4,0},{8,12},{12,8},{16,20},{20,16},{24,28},{28,24},{1,5},{5... | collective-permute-start | bytes 2359304 | tf_op jit(solution)/shard_map/ppermute | solution.py:118
  104.2 29.5 %collective-permute-start.25 = (bf16[2,3,16,4096]{3,2,1,0:T(8,128)(2,1)S(1)}, bf16[2,3,16,4096]{3,2,1,0:T(8,128)(2,1)S(1)}, u32[]{:S(2)}, u32[]{:S(2)}) collective-permute-start(bf16[2,3,16,4096]{3,2,1,0:T(8,128)(2,1)S(1)} %maximum_select_fusion.16), channel_id=1, source_target_pairs={{0,8},{4,12},{8,0},{12,4},{16,24},{20,28},{24,16},{28,20},{1,9},{5... | collective-permute-start | bytes 2359304 | tf_op jit(solution)/shard_map/ppermute | solution.py:118
  105.5 29.5 %collective-permute-start.23 = (bf16[2,3,16,4096]{3,2,1,0:T(8,128)(2,1)S(1)}, bf16[2,3,16,4096]{3,2,1,0:T(8,128)(2,1)S(1)}, u32[]{:S(2)}, u32[]{:S(2)}) collective-permute-start(bf16[2,3,16,4096]{3,2,1,0:T(8,128)(2,1)S(1)} %maximum_select_fusion.14), channel_id=1, source_target_pairs={{0,16},{4,20},{8,24},{12,28},{16,0},{20,4},{24,8},{28,12},{1,17},{... | collective-permute-start | bytes 2359304 | tf_op jit(solution)/shard_map/ppermute | solution.py:118
  116.8 30.8 %collective-permute-start.33 = (bf16[2,3,64,1024]{3,2,1,0:T(8,128)(2,1)S(1)}, bf16[2,3,64,1024]{3,2,1,0:T(8,128)(2,1)S(1)}, u32[]{:S(2)}, u32[]{:S(2)}) collective-permute-start(bf16[2,3,64,1024]{3,2,1,0:T(8,128)(2,1)S(1)} %maximum_select_fusion.20), channel_id=1, source_target_pairs={{0,8},{4,12},{8,0},{12,4},{16,24},{20,28},{24,16},{28,20},{1,9},{5... | collective-permute-start | bytes 2359304 | tf_op jit(solution)/shard_map/ppermute | solution.py:118
  118.2 31.7 %collective-permute-start.31 = (bf16[2,3,64,1024]{3,2,1,0:T(8,128)(2,1)S(1)}, bf16[2,3,64,1024]{3,2,1,0:T(8,128)(2,1)S(1)}, u32[]{:S(2)}, u32[]{:S(2)}) collective-permute-start(bf16[2,3,64,1024]{3,2,1,0:T(8,128)(2,1)S(1)} %maximum_select_fusion.18), channel_id=1, source_target_pairs={{0,16},{4,20},{8,24},{12,28},{16,0},{20,4},{24,8},{28,12},{1,17},{... | collective-permute-start | bytes 2359304 | tf_op jit(solution)/shard_map/ppermute | solution.py:118
  119.2 34.1 %collective-permute-start.10 = (bf16[2,2,3,2,16,3072]{5,4,3,2,1,0:T(8,128)(2,1)S(1)}, bf16[2,2,3,2,16,3072]{5,4,3,2,1,0:T(8,128)(2,1)S(1)}, u32[]{:S(2)}, u32[]{:S(2)}) collective-permute-start(bf16[2,2,3,2,16,3072]{5,4,3,2,1,0:T(8,128)(2,1)S(1)} %get-tuple-element.39), channel_id=1, source_target_pairs={{0,4},{4,0},{8,12},{12,8},{16,20},{20,16},{24,28},{28,24},{1,5},{5... | collective-permute-start | bytes 7077896 | tf_op jit(solution)/shard_map/ppermute | solution.py:118
  137.3 62.5 %collective-permute-start.26 = (bf16[2,2,3,2,16,4096]{5,4,3,2,1,0:T(8,128)(2,1)}, bf16[2,2,3,2,16,4096]{5,4,3,2,1,0:T(8,128)(2,1)}, u32[]{:S(2)}, u32[]{:S(2)}) collective-permute-start(bf16[2,2,3,2,16,4096]{5,4,3,2,1,0:T(8,128)(2,1)} %get-tuple-element.37), channel_id=1, source_target_pairs={{0,4},{4,0},{8,12},{12,8},{16,20},{20,16},{24,28},{28,24},{1,5},{5... | collective-permute-start | bytes 9437192 | tf_op jit(solution)/shard_map/ppermute | solution.py:118
  153.3 66.0 %collective-permute-start.34 = (bf16[2,2,3,2,64,1024]{5,4,3,2,1,0:T(8,128)(2,1)}, bf16[2,2,3,2,64,1024]{5,4,3,2,1,0:T(8,128)(2,1)}, u32[]{:S(2)}, u32[]{:S(2)}) collective-permute-start(bf16[2,2,3,2,64,1024]{5,4,3,2,1,0:T(8,128)(2,1)} %get-tuple-element.35), channel_id=1, source_target_pairs={{0,4},{4,0},{8,12},{12,8},{16,20},{20,16},{24,28},{28,24},{1,5},{5... | collective-permute-start | bytes 9437192 | tf_op jit(solution)/shard_map/ppermute | solution.py:118
  366.9 42.3 %collective-permute-start.61 = (bf16[4,2,2,2,16,1024]{5,4,3,2,1,0:T(8,128)(2,1)}, bf16[4,2,2,2,16,1024]{5,4,3,2,1,0:T(8,128)(2,1)}, u32[]{:S(2)}, u32[]{:S(2)}) collective-permute-start(bf16[4,2,2,2,16,1024]{5,4,3,2,1,0:T(8,128)(2,1)} %dynamic-slice_bitcast_fusion.3), channel_id=1, source_target_pairs={{0,4},{4,0},{8,12},{12,8},{16,20},{20,16},{24,28},{28,24},{1,5},{5... | collective-permute-start | bytes 3145736 | tf_op jit(solution)/shard_map/ppermute | solution.py:133
  399.1 54.1 %collective-permute-start.35 = (bf16[4,2,2,2,16,3072]{5,4,3,2,1,0:T(8,128)(2,1)}, bf16[4,2,2,2,16,3072]{5,4,3,2,1,0:T(8,128)(2,1)}, u32[]{:S(2)}, u32[]{:S(2)}) collective-permute-start(bf16[4,2,2,2,16,3072]{5,4,3,2,1,0:T(8,128)(2,1)} %dynamic-slice_bitcast_fusion.2), channel_id=1, source_target_pairs={{0,4},{4,0},{8,12},{12,8},{16,20},{20,16},{24,28},{28,24},{1,5},{5... | collective-permute-start | bytes 9437192 | tf_op jit(solution)/shard_map/ppermute | solution.py:133
  403.5 79.2 %collective-permute-start.74 = (bf16[4,2,2,2,16,4096]{5,4,3,2,1,0:T(8,128)(2,1)}, bf16[4,2,2,2,16,4096]{5,4,3,2,1,0:T(8,128)(2,1)}, u32[]{:S(2)}, u32[]{:S(2)}) collective-permute-start(bf16[4,2,2,2,16,4096]{5,4,3,2,1,0:T(8,128)(2,1)} %dynamic-slice_bitcast_fusion.1), channel_id=1, source_target_pairs={{0,4},{4,0},{8,12},{12,8},{16,20},{20,16},{24,28},{28,24},{1,5},{5... | collective-permute-start | bytes 12582920 | tf_op jit(solution)/shard_map/ppermute | solution.py:133
  403.5 101.4 %collective-permute-start.87 = (bf16[4,2,2,2,64,1024]{5,4,3,2,1,0:T(8,128)(2,1)}, bf16[4,2,2,2,64,1024]{5,4,3,2,1,0:T(8,128)(2,1)}, u32[]{:S(2)}, u32[]{:S(2)}) collective-permute-start(bf16[4,2,2,2,64,1024]{5,4,3,2,1,0:T(8,128)(2,1)} %dynamic-slice_bitcast_fusion), channel_id=1, source_target_pairs={{0,4},{4,0},{8,12},{12,8},{16,20},{20,16},{24,28},{28,24},{1,5},{5... | collective-permute-start | bytes 12582920 | tf_op jit(solution)/shard_map/ppermute | solution.py:133
  459.3 192.9 %collective-permute-start.73 = (bf16[2,2,2,16,1024]{4,3,0,2,1:T(8,128)(2,1)}, bf16[2,2,2,16,1024]{4,3,0,2,1:T(8,128)(2,1)}, u32[]{:S(2)}, u32[]{:S(2)}) collective-permute-start(bf16[2,2,2,16,1024]{4,3,0,2,1:T(8,128)(2,1)} %get-tuple-element.82), channel_id=1, source_target_pairs={{0,4},{4,0},{8,12},{12,8},{16,20},{20,16},{24,28},{28,24},{1,5},{5... | collective-permute-start | bytes 786440 | tf_op jit(solution)/shard_map/ppermute | solution.py:118
  498.4 62.9 %collective-permute-start.75 = (bf16[4,2,16,4096]{3,2,0,1:T(8,128)(2,1)}, bf16[4,2,16,4096]{3,2,0,1:T(8,128)(2,1)}, u32[]{:S(2)}, u32[]{:S(2)}) collective-permute-start(bf16[4,2,16,4096]{3,2,0,1:T(8,128)(2,1)} %fusion.79), channel_id=1, source_target_pairs={{0,16},{4,20},{8,24},{12,28},{16,0},{20,4},{24,8},{28,12},{1,17},{... | collective-permute-start | bytes 3145736 | tf_op jit(solution)/shard_map/ppermute | solution.py:133
  499.7 63.7 %collective-permute-start.77 = (bf16[4,2,16,4096]{3,2,1,0:T(8,128)(2,1)}, bf16[4,2,16,4096]{3,2,1,0:T(8,128)(2,1)}, u32[]{:S(2)}, u32[]{:S(2)}) collective-permute-start(bf16[4,2,16,4096]{3,2,1,0:T(8,128)(2,1)} %fusion.77), channel_id=1, source_target_pairs={{0,8},{4,12},{8,0},{12,4},{16,24},{20,28},{24,16},{28,20},{1,9},{5... | collective-permute-start | bytes 3145736 | tf_op jit(solution)/shard_map/ppermute | solution.py:133
  518.1 48.3 %collective-permute-start.88 = (bf16[4,2,64,1024]{3,2,0,1:T(8,128)(2,1)S(1)}, bf16[4,2,64,1024]{3,2,0,1:T(8,128)(2,1)S(1)}, u32[]{:S(2)}, u32[]{:S(2)}) collective-permute-start(bf16[4,2,64,1024]{3,2,0,1:T(8,128)(2,1)S(1)} %fusion.80), channel_id=1, source_target_pairs={{0,16},{4,20},{8,24},{12,28},{16,0},{20,4},{24,8},{28,12},{1,17},{... | collective-permute-start | bytes 3145736 | tf_op jit(solution)/shard_map/ppermute | solution.py:133
  561.3 48.8 %collective-permute-start.44 = (bf16[2,16,3072]{2,1,0:T(8,128)(2,1)S(1)}, bf16[2,16,3072]{2,1,0:T(8,128)(2,1)S(1)}, u32[]{:S(2)}, u32[]{:S(2)}) collective-permute-start(bf16[2,16,3072]{2,1,0:T(8,128)(2,1)S(1)} %maximum_select_fusion.47), channel_id=1, source_target_pairs={{0,16},{4,20},{8,24},{12,28},{16,0},{20,4},{24,8},{28,12},{1,17},{... | collective-permute-start | bytes 589832 | tf_op jit(solution)/shard_map/ppermute | solution.py:118
  563.5 33.7 %collective-permute-start.76 = (bf16[4,16,4096]{2,1,0:T(8,128)(2,1)S(1)}, bf16[4,16,4096]{2,1,0:T(8,128)(2,1)S(1)}, u32[]{:S(2)}, u32[]{:S(2)}) collective-permute-start(bf16[4,16,4096]{2,1,0:T(8,128)(2,1)S(1)} %fusion.98), channel_id=1, source_target_pairs={{0,8},{4,12},{8,0},{12,4},{16,24},{20,28},{24,16},{28,20},{1,9},{5... | collective-permute-start | bytes 1572872 | tf_op jit(solution)/shard_map/ppermute | solution.py:133
  566.4 31.6 %collective-permute-start.78 = (bf16[4,16,4096]{2,1,0:T(8,128)(2,1)S(1)}, bf16[4,16,4096]{2,1,0:T(8,128)(2,1)S(1)}, u32[]{:S(2)}, u32[]{:S(2)}) collective-permute-start(bf16[4,16,4096]{2,1,0:T(8,128)(2,1)S(1)} %fusion.99), channel_id=1, source_target_pairs={{0,16},{4,20},{8,24},{12,28},{16,0},{20,4},{24,8},{28,12},{1,17},{... | collective-permute-start | bytes 1572872 | tf_op jit(solution)/shard_map/ppermute | solution.py:133
  622.6 31.9 %collective-permute-start.47 = (bf16[2,2,2,16,3072]{4,3,0,2,1:T(8,128)(2,1)S(1)}, bf16[2,2,2,16,3072]{4,3,0,2,1:T(8,128)(2,1)S(1)}, u32[]{:S(2)}, u32[]{:S(2)}) collective-permute-start(bf16[2,2,2,16,3072]{4,3,0,2,1:T(8,128)(2,1)S(1)} %get-tuple-element.48), channel_id=1, source_target_pairs={{0,4},{4,0},{8,12},{12,8},{16,20},{20,16},{24,28},{28,24},{1,5},{5... | collective-permute-start | bytes 2359304 | tf_op jit(solution)/shard_map/ppermute | solution.py:118
  (127 other events, 1124.4 us)
where the time goes:
time: 669 us; the launch traced here: 662 us
  waiting for transfers between devices  219 us (33%)
  starting transfers between devices  131 us (20%)
  matrix products  113 us (17%)
  local copies, waits for them, and re-layouts  112 us (17%)
  other arithmetic  81.6 us (12%)
    ppermute x45, waiting for transfers between devices, exchange(): got = lax.ppermute(leaves, 'dp', xor_pairs(n_dp, 1 << bit))  106 us
    ppermute x25, waiting for transfers between devices, split_bit(): lax.ppermute([v.astype(jnp.bfloat16) for v in send], 'dp', xor_pairs(n_dp...  70.8 us
    ppermute x15, starting transfers between devices, reduce_chain(): got = lax.ppermute(send, 'fsdp', down)  45.4 us
    ppermute x15, starting transfers between devices, gather_chain(): buf = lax.ppermute(buf, 'fsdp', down)  35 us
    ppermute x45, starting transfers between devices, exchange(): got = lax.ppermute(leaves, 'dp', xor_pairs(n_dp, 1 << bit))  28.7 us
    ppermute x15, waiting for transfers between devices, reduce_chain(): got = lax.ppermute(send, 'fsdp', down)  22.6 us
    ppermute x25, starting transfers between devices, split_bit(): lax.ppermute([v.astype(jnp.bfloat16) for v in send], 'dp', xor_pairs(n_dp...  21.6 us
    ppermute x15, waiting for transfers between devices, gather_chain(): buf = lax.ppermute(buf, 'fsdp', down)  19.6 us
  transfers between devices with their start and end apart: 100, of which 55 were waited for; matrix products, arithmetic and copies ran while one was open for 21% of the time, Pallas kernels for 0%

commit v1 on v0

--- a/solution.py
+++ b/solution.py
@@ -114,9 +114,9 @@
     return [(i, i ^ mask) for i in range(n)]
 
 
-def exchange(leaves, held, bit, d, n_dp):
+def exchange(leaves, held, bit, d, n_dp, lead=0):
     got = lax.ppermute(leaves, "dp", xor_pairs(n_dp, 1 << bit))
-    pos = sum(1 for b in held if b > bit)
+    pos = lead + sum(1 for b in held if b > bit)
     mine = ((d >> bit) & 1) == 0
     out = [
         jnp.where(mine, jnp.stack([a, g], axis=pos), jnp.stack([g, a], axis=pos))
@@ -164,14 +164,14 @@
         order = order if h == 0 else order[::-1]
         leaves, held = [zrel[:, h]], []
         for bit in order:
-            leaves, held = exchange(leaves, held, bit, d, n_dp)
+            leaves, held = exchange(leaves, held, bit, d, n_dp, 1)
         halves.append(leaves[0])
     both = jnp.stack(halves, axis=-3)
     held = chip_bits(n_dp)[::-1]
     if n_dp > 1:
-        (both,), held = exchange([both], held, 0, d, n_dp)
-    plane = both.reshape((n_dp, n_fsdp - 1) + both.shape[-3:])
-    rel = jnp.concatenate([pieces[None], jnp.swapaxes(plane, 0, 1)], axis=0)
+        (both,), held = exchange([both], held, 0, d, n_dp, 1)
+    plane = both.reshape((n_fsdp - 1, n_dp) + both.shape[-3:])
+    rel = jnp.concatenate([pieces[None], plane], axis=0)
     return jnp.roll(rel, f, axis=0).reshape(n_fsdp * rows, cols), vecs
 
 

time: 669 us -> 648 us (0.969)
  local copies, waits for them, and re-layouts: 112 us -> 91.7 us
    dynamic_slice x4 -> x0, local copies, waits for them, and re-layouts: 18.6 us -> none  [gather_chain(): return (jnp.roll(rel, f, axis=0).reshape(n_fsdp * rows, cols), vecs)]
    select_n x40 -> x36, other arithmetic: 12.3 us -> 13.4 us  [exchange(): jnp.where(mine, jnp.stack([a, g], axis=pos), jnp.stack([g, a], axis=pos))]
    unnamed x134 -> x132, local copies, waits for them, and re-layouts: 16 us -> 15.2 us
  transfers between devices with their start and end apart: 100 -> 100, of which waited for: 55 -> 53; matrix products, arithmetic and copies ran while one was open for 21% -> 20% of each run, Pallas kernels for 0% -> 0%
where the time goes in v1:
time: 648 us; the launch traced here: 640 us
  waiting for transfers between devices  214 us (33%)
  starting transfers between devices  134 us (21%)
  matrix products  111 us (17%)
  local copies, waits for them, and re-layouts  91.7 us (14%)
  other arithmetic  82.4 us (13%)
    ppermute x45, waiting for transfers between devices, exchange(): got = lax.ppermute(leaves, 'dp', xor_pairs(n_dp, 1 << bit))  103 us
    ppermute x25, waiting for transfers between devices, split_bit(): lax.ppermute([v.astype(jnp.bfloat16) for v in send], 'dp', xor_pairs(n_dp...  69.3 us
    ppermute x15, starting transfers between devices, reduce_chain(): got = lax.ppermute(send, 'fsdp', down)  45.2 us
    ppermute x15, starting transfers between devices, gather_chain(): buf = lax.ppermute(buf, 'fsdp', down)  34.9 us
    ppermute x45, starting transfers between devices, exchange(): got = lax.ppermute(leaves, 'dp', xor_pairs(n_dp, 1 << bit))  31.8 us
    ppermute x15, waiting for transfers between devices, reduce_chain(): got = lax.ppermute(send, 'fsdp', down)  21.9 us
    ppermute x25, starting transfers between devices, split_bit(): lax.ppermute([v.astype(jnp.bfloat16) for v in send], 'dp', xor_pairs(n_dp...  21.7 us
    add x15, other arithmetic, split_bit(): k.astype(jnp.float32) + g.astype(jnp.float32)  20.4 us
  transfers between devices with their start and end apart: 100, of which 53 were waited for; matrix products, arithmetic and copies ran while one was open for 20% of the time, Pallas kernels for 0%

profile of v1, /device:TPU:0, one launch (start us, length us, event | category | flops | bytes accessed | tf_op | source)
XLA Modules:
  0.0 639.9 jit_solution(9527018874704846265)
XLA Ops:
  29.7 6.7 %collective-permute-done.1 = bf16[3072]{0:T(1024)(128)(2,1)S(1)} collective-permute-done((bf16[3072]{0:T(1024)(128)(2,1)S(1)}, bf16[3072]{0:T(1024)(128)(2,1)S(1)}, u32[]{:S(2)}, u32[]{:S(2)}) %collective-permute-start.1) | collective-permute-done | bytes 6176 | tf_op jit(solution)/shard_map/ppermute | solution.py:151
  88.5 12.5 %collective-permute-done.30 = bf16[3,64,1024]{2,1,0:T(8,128)(2,1)S(1)} collective-permute-done((bf16[3,64,1024]{2,1,0:T(8,128)(2,1)S(1)}, bf16[3,64,1024]{2,1,0:T(8,128)(2,1)S(1)}, u32[]{:S(2)}, u32[]{:S(2)}) %collective-permute-start.30) | collective-permute-done | bytes 393248 | tf_op jit(solution)/shard_map/ppermute | solution.py:118
  106.7 10.5 %collective-permute-done.9 = bf16[3,2,16,3072]{3,2,1,0:T(8,128)(2,1)S(1)} collective-permute-done((bf16[3,2,16,3072]{3,2,1,0:T(8,128)(2,1)S(1)}, bf16[3,2,16,3072]{3,2,1,0:T(8,128)(2,1)S(1)}, u32[]{:S(2)}, u32[]{:S(2)}) %collective-permute-start.9) | collective-permute-done | bytes 589856 | tf_op jit(solution)/shard_map/ppermute | solution.py:118
  122.6 11.5 %collective-permute-done.25 = bf16[3,2,16,4096]{3,2,1,0:T(8,128)(2,1)S(1)} collective-permute-done((bf16[3,2,16,4096]{3,2,1,0:T(8,128)(2,1)S(1)}, bf16[3,2,16,4096]{3,2,1,0:T(8,128)(2,1)S(1)}, u32[]{:S(2)}, u32[]{:S(2)}) %collective-permute-start.25) | collective-permute-done | bytes 786464 | tf_op jit(solution)/shard_map/ppermute | solution.py:118
  137.0 10.3 %collective-permute-done.33 = bf16[3,2,64,1024]{3,2,1,0:T(8,128)(2,1)S(1)} collective-permute-done((bf16[3,2,64,1024]{3,2,1,0:T(8,128)(2,1)S(1)}, bf16[3,2,64,1024]{3,2,1,0:T(8,128)(2,1)S(1)}, u32[]{:S(2)}, u32[]{:S(2)}) %collective-permute-start.33) | collective-permute-done | bytes 786464 | tf_op jit(solution)/shard_map/ppermute | solution.py:118
  203.1 5.2 fusion.11
  208.3 6.3 maximum_select_fusion.1
  220.0 10.8 %multiply_convert_fusion = (bf16[600,4096]{1,0:T(8,128)(2,1)}, f32[600,4096]{1,0:T(8,128)}) fusion(f32[4096]{0:T(1024)S(1)} %bitcast.699, bf16[1024,4096]{1,0:T(8,128)(2,1)S(1)} %bitcast.601, f32[600,1024]{1,0:T(8,128)S(1)} %get-tuple-element.136, f32[1024]{0:T(1024)S(1)} %bitcast.714, f32[1024]{0:T(1024)S(1)} %bitcast.689, f32[600]{0:T(1024)S(1)} %add_rsqrt_fusion, ...), kind=kOutput, calls=%fused_computation.19 | convolution fusion | flops 5050982400 | bytes 25621184 | tf_op jit(solution)/shard_map/dot_general | solution.py:314
  230.8 13.0 %fusion.218 = (bf16[4096]{0:T(1024)(128)(2,1)S(1)}, bf16[600,4096]{1,0:T(8,128)(2,1)S(1)}) fusion(f32[600,4096]{1,0:T(8,128)} %get-tuple-element.138, f32[4096]{0:T(1024)S(1)} %bitcast.700, bf16[4096,1024]{1,0:T(8,128)(2,1)S(1)} %bitcast.597, bf16[600,1024]{1,0:T(8,128)(2,1)S(1)} %copy-done.33, f32[]{:T(128)} %bitcast.98), kind=kOutput, calls=%fused_computation.523 | convolution fusion | flops 5064495104 | bytes 24387588 | tf_op jit(solution)/shard_map/dot_general | solution.py:324
  243.7 10.6 %multiply_reduce_fusion.1 = (bf16[1024]{0:T(1024)(128)(2,1)S(1)}, f32[600]{0:T(1024)S(1)}, f32[600]{0:T(1024)S(1)}, bf16[1024]{0:T(1024)(128)(2,1)S(1)}, f32[600,1024]{1,0:T(8,128)S(1)}) fusion(f32[600,1024]{1,0:T(8,128)S(1)} %get-tuple-element.136, f32[600]{0:T(1024)S(1)} %add_rsqrt_fusion, f32[600]{0:T(1024)S(1)} %broadcast_multiply_fusion.4, ...), kind=kOutput, calls=%fused_computation.120 | convolution fusion | flops 5038691328 | bytes 18236800 | tf_op jit(solution)/shard_map/dot_general | solution.py:329
  261.1 9.8 %convolution_convert_fusion = bf16[1024,4096]{1,0:T(8,128)(2,1)} fusion(bf16[600,4096]{1,0:T(8,128)(2,1)S(1)} %bitcast.731, f32[600,1024]{1,0:T(8,128)S(1)} %get-tuple-element.136, f32[1024]{0:T(1024)S(1)} %bitcast.715, f32[1024]{0:T(1024)S(1)} %bitcast.692, f32[600]{0:T(1024)S(1)} %add_rsqrt_fusion, f32[600]{0:T(1024)S(1)} %broadcast_multiply_fusion.4), kind=kOutput, calls=%fused_computation.29 | convolution fusion | flops 5040431104 | bytes 15774400 | tf_op jit(solution)/shard_map/dot_general | solution.py:327
  273.7 6.6 %fusion.217 = (bf16[16,64]{1,0:T(8,128)(2,1)S(1)}, bf16[12,50,16,64]{3,1,2,0:T(8,128)(2,1)}) fusion(f32[12,16,50,50]{2,3,1,0:T(8,128)} %copy-done, f32[12,16,50]{2,1,0:T(8,128)S(1)} %log_add_fusion, bf16[12,50,16,64]{3,2,1,0:T(8,128)(2,1)} %reshape.3812), kind=kOutput, calls=%fused_computation.522 | convolution fusion | flops 63627776 | bytes 4418048 | tf_op jit(solution)/shard_map/chqk,cqhd->ckhd/dot_general | solution.py:88
  312.7 9.9 %fusion.48 = (bf16[1024]{0:T(1024)(128)(2,1)S(1)}, f32[600]{0:T(1024)S(1)}, f32[600]{0:T(1024)S(1)}, bf16[1024]{0:T(1024)(128)(2,1)S(1)}, f32[600,1024]{1,0:T(8,128)}) fusion(bf16[600,1024]{1,0:T(8,128)(2,1)S(1)} %copy-done.6, f32[600]{0:T(1024)S(1)} %add_rsqrt_fusion.1, f32[600]{0:T(1024)S(1)} %broadcast_multiply_fusion.5, f32[1024]{0:T(1024)S(1)} %bitcast.694, ...), kind=kOutput, calls=%fused_computation.118 | convolution fusion | flops 3781014528 | bytes 13682048 | tf_op jit(solution)/shard_map/dot_general | solution.py:343
  322.6 7.5 %convolution_convert_fusion.2 = bf16[1024,3072]{1,0:T(8,128)(2,1)} fusion(bf16[600,3072]{1,0:T(8,128)(2,1)S(1)} %copy-done.36, bf16[600,1024]{1,0:T(8,128)(2,1)S(1)} %copy-done.6, f32[1024]{0:T(1024)S(1)} %bitcast.713, f32[1024]{0:T(1024)S(1)} %bitcast.695, f32[600]{0:T(1024)S(1)} %add_rsqrt_fusion.1, f32[600]{0:T(1024)S(1)} %broadcast_multiply_fusion.5), kind=kOutput, calls=%fused_computation.38 | convolution fusion | flops 3781705728 | bytes 11219648 | tf_op jit(solution)/shard_map/dot_general | solution.py:340
  330.1 9.3 %convolution_convert_fusion.1 = bf16[4096,1024]{1,0:T(8,128)(2,1)} fusion(bf16[600,4096]{1,0:T(8,128)(2,1)S(1)} %bitcast.733, bf16[600,1024]{1,0:T(8,128)(2,1)S(1)} %copy-done.34, f32[]{:T(128)} %bitcast.98), kind=kOutput, calls=%fused_computation.30 | convolution fusion | flops 5039202304 | bytes 14532612 | tf_op jit(solution)/shard_map/dot_general | solution.py:322
  339.5 6.4 add_convert_fusion.1
  441.1 8.8 %collective-permute-done.36 = bf16[4,2,16,3072]{3,2,0,1:T(8,128)(2,1)S(1)} collective-permute-done((bf16[4,2,16,3072]{3,2,0,1:T(8,128)(2,1)S(1)}, bf16[4,2,16,3072]{3,2,0,1:T(8,128)(2,1)S(1)}, u32[]{:S(2)}, u32[]{:S(2)}) %collective-permute-start.36) | collective-permute-done | bytes 786464 | tf_op jit(solution)/shard_map/ppermute | solution.py:133
  450.2 9.2 %collective-permute-done.38 = bf16[4,2,16,3072]{3,2,1,0:T(8,128)(2,1)S(1)} collective-permute-done((bf16[4,2,16,3072]{3,2,1,0:T(8,128)(2,1)S(1)}, bf16[4,2,16,3072]{3,2,1,0:T(8,128)(2,1)S(1)}, u32[]{:S(2)}, u32[]{:S(2)}) %collective-permute-start.38) | collective-permute-done | bytes 786464 | tf_op jit(solution)/shard_map/ppermute | solution.py:133
  482.4 5.6 convert_add_fusion
  499.2 25.2 %collective-permute-done.45 = bf16[16,3072]{1,0:T(8,128)(2,1)S(1)} collective-permute-done((bf16[16,3072]{1,0:T(8,128)(2,1)S(1)}, bf16[16,3072]{1,0:T(8,128)(2,1)S(1)}, u32[]{:S(2)}, u32[]{:S(2)}) %collective-permute-start.45) | collective-permute-done | bytes 98336 | tf_op jit(solution)/shard_map/ppermute | solution.py:118
  531.0 6.4 collective-permute-done.46
  545.7 17.8 %collective-permute-done.90 = bf16[4,2,64,1024]{3,2,1,0:T(8,128)(2,1)S(1)} collective-permute-done((bf16[4,2,64,1024]{3,2,1,0:T(8,128)(2,1)S(1)}, bf16[4,2,64,1024]{3,2,1,0:T(8,128)(2,1)S(1)}, u32[]{:S(2)}, u32[]{:S(2)}) %collective-permute-start.90) | collective-permute-done | bytes 1048608 | tf_op jit(solution)/shard_map/ppermute | solution.py:133
  565.2 9.5 %collective-permute-done.76 = bf16[4,16,4096]{2,1,0:T(8,128)(2,1)S(1)} collective-permute-done((bf16[4,16,4096]{2,1,0:T(8,128)(2,1)S(1)}, bf16[4,16,4096]{2,1,0:T(8,128)(2,1)S(1)}, u32[]{:S(2)}, u32[]{:S(2)}) %collective-permute-start.76) | collective-permute-done | bytes 524320 | tf_op jit(solution)/shard_map/ppermute | solution.py:133
  587.5 5.8 collective-permute-done.92
  (580 shorter events, 398.5 us)
Async XLA Ops:
  15.0 26.6 %collective-permute-start.11 = (bf16[2,16,1024]{2,1,0:T(8,128)(2,1)S(1)}, bf16[2,16,1024]{2,1,0:T(8,128)(2,1)S(1)}, u32[]{:S(2)}, u32[]{:S(2)}) collective-permute-start(bf16[2,16,1024]{2,1,0:T(8,128)(2,1)S(1)} %dynamic-slice_bitcast_fusion.7), channel_id=1, source_target_pairs={{0,3},{1,0},{2,1},{3,2},{4,7},{5,4},{6,5},{7,6},{8,11},{9,8},{10,9... | collective-permute-start | bytes 196616 | tf_op jit(solution)/shard_map/ppermute | solution.py:151
  19.1 36.4 %collective-permute-start.3 = (bf16[2,16,3072]{2,1,0:T(8,128)(2,1)S(1)}, bf16[2,16,3072]{2,1,0:T(8,128)(2,1)S(1)}, u32[]{:S(2)}, u32[]{:S(2)}) collective-permute-start(bf16[2,16,3072]{2,1,0:T(8,128)(2,1)S(1)} %dynamic-slice_bitcast_fusion.6), channel_id=1, source_target_pairs={{0,3},{1,0},{2,1},{3,2},{4,7},{5,4},{6,5},{7,6},{8,11},{9,8},{10,9... | collective-permute-start | bytes 589832 | tf_op jit(solution)/shard_map/ppermute | solution.py:151
  21.2 38.5 %collective-permute-start.19 = (bf16[2,16,4096]{2,1,0:T(8,128)(2,1)S(1)}, bf16[2,16,4096]{2,1,0:T(8,128)(2,1)S(1)}, u32[]{:S(2)}, u32[]{:S(2)}) collective-permute-start(bf16[2,16,4096]{2,1,0:T(8,128)(2,1)S(1)} %dynamic-slice_bitcast_fusion.5), channel_id=1, source_target_pairs={{0,3},{1,0},{2,1},{3,2},{4,7},{5,4},{6,5},{7,6},{8,11},{9,8},{10,9... | collective-permute-start | bytes 786440 | tf_op jit(solution)/shard_map/ppermute | solution.py:151
  23.7 36.1 %collective-permute-start.27 = (bf16[2,64,1024]{2,1,0:T(8,128)(2,1)S(1)}, bf16[2,64,1024]{2,1,0:T(8,128)(2,1)S(1)}, u32[]{:S(2)}, u32[]{:S(2)}) collective-permute-start(bf16[2,64,1024]{2,1,0:T(8,128)(2,1)S(1)} %dynamic-slice_bitcast_fusion.4), channel_id=1, source_target_pairs={{0,3},{1,0},{2,1},{3,2},{4,7},{5,4},{6,5},{7,6},{8,11},{9,8},{10,9... | collective-permute-start | bytes 786440 | tf_op jit(solution)/shard_map/ppermute | solution.py:151
  69.5 49.7 %collective-permute-start.18 = (bf16[3,2,2,2,16,1024]{5,4,3,2,1,0:T(8,128)(2,1)S(1)}, bf16[3,2,2,2,16,1024]{5,4,3,2,1,0:T(8,128)(2,1)S(1)}, u32[]{:S(2)}, u32[]{:S(2)}) collective-permute-start(bf16[3,2,2,2,16,1024]{5,4,3,2,1,0:T(8,128)(2,1)S(1)} %get-tuple-element.64), channel_id=1, source_target_pairs={{0,4},{4,0},{8,12},{12,8},{16,20},{20,16},{24,28},{28,24},{1,5},{5... | collective-permute-start | bytes 2359304 | tf_op jit(solution)/shard_map/ppermute | solution.py:118
  101.9 32.2 %collective-permute-start.25 = (bf16[3,2,16,4096]{3,2,1,0:T(8,128)(2,1)S(1)}, bf16[3,2,16,4096]{3,2,1,0:T(8,128)(2,1)S(1)}, u32[]{:S(2)}, u32[]{:S(2)}) collective-permute-start(bf16[3,2,16,4096]{3,2,1,0:T(8,128)(2,1)S(1)} %maximum_select_fusion.16), channel_id=1, source_target_pairs={{0,8},{4,12},{8,0},{12,4},{16,24},{20,28},{24,16},{28,20},{1,9},{5... | collective-permute-start | bytes 2359304 | tf_op jit(solution)/shard_map/ppermute | solution.py:118
  105.5 29.5 %collective-permute-start.23 = (bf16[3,2,16,4096]{3,2,1,0:T(8,128)(2,1)S(1)}, bf16[3,2,16,4096]{3,2,1,0:T(8,128)(2,1)S(1)}, u32[]{:S(2)}, u32[]{:S(2)}) collective-permute-start(bf16[3,2,16,4096]{3,2,1,0:T(8,128)(2,1)S(1)} %maximum_select_fusion.14), channel_id=1, source_target_pairs={{0,16},{4,20},{8,24},{12,28},{16,0},{20,4},{24,8},{28,12},{1,17},{... | collective-permute-start | bytes 2359304 | tf_op jit(solution)/shard_map/ppermute | solution.py:118
  117.2 30.1 %collective-permute-start.33 = (bf16[3,2,64,1024]{3,2,1,0:T(8,128)(2,1)S(1)}, bf16[3,2,64,1024]{3,2,1,0:T(8,128)(2,1)S(1)}, u32[]{:S(2)}, u32[]{:S(2)}) collective-permute-start(bf16[3,2,64,1024]{3,2,1,0:T(8,128)(2,1)S(1)} %maximum_select_fusion.20), channel_id=1, source_target_pairs={{0,8},{4,12},{8,0},{12,4},{16,24},{20,28},{24,16},{28,20},{1,9},{5... | collective-permute-start | bytes 2359304 | tf_op jit(solution)/shard_map/ppermute | solution.py:118
  119.0 34.0 %collective-permute-start.10 = (bf16[3,2,2,2,16,3072]{5,4,3,2,1,0:T(8,128)(2,1)S(1)}, bf16[3,2,2,2,16,3072]{5,4,3,2,1,0:T(8,128)(2,1)S(1)}, u32[]{:S(2)}, u32[]{:S(2)}) collective-permute-start(bf16[3,2,2,2,16,3072]{5,4,3,2,1,0:T(8,128)(2,1)S(1)} %get-tuple-element.39), channel_id=1, source_target_pairs={{0,4},{4,0},{8,12},{12,8},{16,20},{20,16},{24,28},{28,24},{1,5},{5... | collective-permute-start | bytes 7077896 | tf_op jit(solution)/shard_map/ppermute | solution.py:118
  119.2 30.6 %collective-permute-start.31 = (bf16[3,2,64,1024]{3,2,1,0:T(8,128)(2,1)S(1)}, bf16[3,2,64,1024]{3,2,1,0:T(8,128)(2,1)S(1)}, u32[]{:S(2)}, u32[]{:S(2)}) collective-permute-start(bf16[3,2,64,1024]{3,2,1,0:T(8,128)(2,1)S(1)} %maximum_select_fusion.18), channel_id=1, source_target_pairs={{0,16},{4,20},{8,24},{12,28},{16,0},{20,4},{24,8},{28,12},{1,17},{... | collective-permute-start | bytes 2359304 | tf_op jit(solution)/shard_map/ppermute | solution.py:118
  137.0 61.6 %collective-permute-start.26 = (bf16[3,2,2,2,16,4096]{5,4,3,2,1,0:T(8,128)(2,1)}, bf16[3,2,2,2,16,4096]{5,4,3,2,1,0:T(8,128)(2,1)}, u32[]{:S(2)}, u32[]{:S(2)}) collective-permute-start(bf16[3,2,2,2,16,4096]{5,4,3,2,1,0:T(8,128)(2,1)} %get-tuple-element.37), channel_id=1, source_target_pairs={{0,4},{4,0},{8,12},{12,8},{16,20},{20,16},{24,28},{28,24},{1,5},{5... | collective-permute-start | bytes 9437192 | tf_op jit(solution)/shard_map/ppermute | solution.py:118
  153.0 55.3 %collective-permute-start.34 = (bf16[3,2,2,2,64,1024]{5,4,3,2,1,0:T(8,128)(2,1)}, bf16[3,2,2,2,64,1024]{5,4,3,2,1,0:T(8,128)(2,1)}, u32[]{:S(2)}, u32[]{:S(2)}) collective-permute-start(bf16[3,2,2,2,64,1024]{5,4,3,2,1,0:T(8,128)(2,1)} %get-tuple-element.35), channel_id=1, source_target_pairs={{0,4},{4,0},{8,12},{12,8},{16,20},{20,16},{24,28},{28,24},{1,5},{5... | collective-permute-start | bytes 9437192 | tf_op jit(solution)/shard_map/ppermute | solution.py:118
  347.0 42.4 %collective-permute-start.61 = (bf16[4,2,2,2,16,1024]{5,4,3,2,1,0:T(8,128)(2,1)}, bf16[4,2,2,2,16,1024]{5,4,3,2,1,0:T(8,128)(2,1)}, u32[]{:S(2)}, u32[]{:S(2)}) collective-permute-start(bf16[4,2,2,2,16,1024]{5,4,3,2,1,0:T(8,128)(2,1)} %dynamic-slice_bitcast_fusion.3), channel_id=1, source_target_pairs={{0,4},{4,0},{8,12},{12,8},{16,20},{20,16},{24,28},{28,24},{1,5},{5... | collective-permute-start | bytes 3145736 | tf_op jit(solution)/shard_map/ppermute | solution.py:133
  379.3 53.6 %collective-permute-start.35 = (bf16[4,2,2,2,16,3072]{5,4,3,2,1,0:T(8,128)(2,1)}, bf16[4,2,2,2,16,3072]{5,4,3,2,1,0:T(8,128)(2,1)}, u32[]{:S(2)}, u32[]{:S(2)}) collective-permute-start(bf16[4,2,2,2,16,3072]{5,4,3,2,1,0:T(8,128)(2,1)} %dynamic-slice_bitcast_fusion.2), channel_id=1, source_target_pairs={{0,4},{4,0},{8,12},{12,8},{16,20},{20,16},{24,28},{28,24},{1,5},{5... | collective-permute-start | bytes 9437192 | tf_op jit(solution)/shard_map/ppermute | solution.py:133
  383.6 78.1 %collective-permute-start.74 = (bf16[4,2,2,2,16,4096]{5,4,3,2,1,0:T(8,128)(2,1)}, bf16[4,2,2,2,16,4096]{5,4,3,2,1,0:T(8,128)(2,1)}, u32[]{:S(2)}, u32[]{:S(2)}) collective-permute-start(bf16[4,2,2,2,16,4096]{5,4,3,2,1,0:T(8,128)(2,1)} %dynamic-slice_bitcast_fusion.1), channel_id=1, source_target_pairs={{0,4},{4,0},{8,12},{12,8},{16,20},{20,16},{24,28},{28,24},{1,5},{5... | collective-permute-start | bytes 12582920 | tf_op jit(solution)/shard_map/ppermute | solution.py:133
  383.6 98.8 %collective-permute-start.87 = (bf16[4,2,2,2,64,1024]{5,4,3,2,1,0:T(8,128)(2,1)}, bf16[4,2,2,2,64,1024]{5,4,3,2,1,0:T(8,128)(2,1)}, u32[]{:S(2)}, u32[]{:S(2)}) collective-permute-start(bf16[4,2,2,2,64,1024]{5,4,3,2,1,0:T(8,128)(2,1)} %dynamic-slice_bitcast_fusion), channel_id=1, source_target_pairs={{0,4},{4,0},{8,12},{12,8},{16,20},{20,16},{24,28},{28,24},{1,5},{5... | collective-permute-start | bytes 12582920 | tf_op jit(solution)/shard_map/ppermute | solution.py:133
  438.9 190.8 %collective-permute-start.73 = (bf16[2,2,2,16,1024]{4,3,0,2,1:T(8,128)(2,1)}, bf16[2,2,2,16,1024]{4,3,0,2,1:T(8,128)(2,1)}, u32[]{:S(2)}, u32[]{:S(2)}) collective-permute-start(bf16[2,2,2,16,1024]{4,3,0,2,1:T(8,128)(2,1)} %get-tuple-element.85), channel_id=1, source_target_pairs={{0,4},{4,0},{8,12},{12,8},{16,20},{20,16},{24,28},{28,24},{1,5},{5... | collective-permute-start | bytes 786440 | tf_op jit(solution)/shard_map/ppermute | solution.py:118
  475.9 62.9 %collective-permute-start.75 = (bf16[4,2,16,4096]{3,2,0,1:T(8,128)(2,1)}, bf16[4,2,16,4096]{3,2,0,1:T(8,128)(2,1)}, u32[]{:S(2)}, u32[]{:S(2)}) collective-permute-start(bf16[4,2,16,4096]{3,2,0,1:T(8,128)(2,1)} %fusion.76), channel_id=1, source_target_pairs={{0,16},{4,20},{8,24},{12,28},{16,0},{20,4},{24,8},{28,12},{1,17},{... | collective-permute-start | bytes 3145736 | tf_op jit(solution)/shard_map/ppermute | solution.py:133
  477.3 63.8 %collective-permute-start.77 = (bf16[4,2,16,4096]{3,2,1,0:T(8,128)(2,1)}, bf16[4,2,16,4096]{3,2,1,0:T(8,128)(2,1)}, u32[]{:S(2)}, u32[]{:S(2)}) collective-permute-start(bf16[4,2,16,4096]{3,2,1,0:T(8,128)(2,1)} %fusion.74), channel_id=1, source_target_pairs={{0,8},{4,12},{8,0},{12,4},{16,24},{20,28},{24,16},{28,20},{1,9},{5... | collective-permute-start | bytes 3145736 | tf_op jit(solution)/shard_map/ppermute | solution.py:133
  495.8 48.2 %collective-permute-start.88 = (bf16[4,2,64,1024]{3,2,0,1:T(8,128)(2,1)S(1)}, bf16[4,2,64,1024]{3,2,0,1:T(8,128)(2,1)S(1)}, u32[]{:S(2)}, u32[]{:S(2)}) collective-permute-start(bf16[4,2,64,1024]{3,2,0,1:T(8,128)(2,1)S(1)} %fusion.77), channel_id=1, source_target_pairs={{0,16},{4,20},{8,24},{12,28},{16,0},{20,4},{24,8},{28,12},{1,17},{... | collective-permute-start | bytes 3145736 | tf_op jit(solution)/shard_map/ppermute | solution.py:133
  538.8 48.7 %collective-permute-start.44 = (bf16[2,16,3072]{2,1,0:T(8,128)(2,1)S(1)}, bf16[2,16,3072]{2,1,0:T(8,128)(2,1)S(1)}, u32[]{:S(2)}, u32[]{:S(2)}) collective-permute-start(bf16[2,16,3072]{2,1,0:T(8,128)(2,1)S(1)} %maximum_select_fusion.47), channel_id=1, source_target_pairs={{0,16},{4,20},{8,24},{12,28},{16,0},{20,4},{24,8},{28,12},{1,17},{... | collective-permute-start | bytes 589832 | tf_op jit(solution)/shard_map/ppermute | solution.py:118
  541.2 33.5 %collective-permute-start.76 = (bf16[4,16,4096]{2,1,0:T(8,128)(2,1)S(1)}, bf16[4,16,4096]{2,1,0:T(8,128)(2,1)S(1)}, u32[]{:S(2)}, u32[]{:S(2)}) collective-permute-start(bf16[4,16,4096]{2,1,0:T(8,128)(2,1)S(1)} %fusion.92), channel_id=1, source_target_pairs={{0,8},{4,12},{8,0},{12,4},{16,24},{20,28},{24,16},{28,20},{1,9},{5... | collective-permute-start | bytes 1572872 | tf_op jit(solution)/shard_map/ppermute | solution.py:133
  544.0 31.6 %collective-permute-start.78 = (bf16[4,16,4096]{2,1,0:T(8,128)(2,1)S(1)}, bf16[4,16,4096]{2,1,0:T(8,128)(2,1)S(1)}, u32[]{:S(2)}, u32[]{:S(2)}) collective-permute-start(bf16[4,16,4096]{2,1,0:T(8,128)(2,1)S(1)} %fusion.93), channel_id=1, source_target_pairs={{0,16},{4,20},{8,24},{12,28},{16,0},{20,4},{24,8},{28,12},{1,17},{... | collective-permute-start | bytes 1572872 | tf_op jit(solution)/shard_map/ppermute | solution.py:133
  600.2 31.8 %collective-permute-start.47 = (bf16[2,2,2,16,3072]{4,3,0,2,1:T(8,128)(2,1)S(1)}, bf16[2,2,2,16,3072]{4,3,0,2,1:T(8,128)(2,1)S(1)}, u32[]{:S(2)}, u32[]{:S(2)}) collective-permute-start(bf16[2,2,2,16,3072]{4,3,0,2,1:T(8,128)(2,1)S(1)} %get-tuple-element.48), channel_id=1, source_target_pairs={{0,4},{4,0},{8,12},{12,8},{16,20},{20,16},{24,28},{28,24},{1,5},{5... | collective-permute-start | bytes 2359304 | tf_op jit(solution)/shard_map/ppermute | solution.py:118
  (126 other events, 1147.2 us)

commit v2 on v1

--- a/solution.py
+++ b/solution.py
@@ -208,15 +208,10 @@
             (g.astype(jnp.float32) + lax.dynamic_index_in_dim(a, chunk, 0, keepdims=False)).astype(jnp.bfloat16)
             for g, a in zip(got, acc)
         ]
-    halves = []
-    for h in range(2):
-        order = chip_bits(n_dp)
-        order = order if h == 0 else order[::-1]
-        part, hb = [v[h] for v in send], []
-        for bit in order:
-            part, hb = exchange(part, hb, bit, d, n_dp)
-        halves.append(part)
-    both = [jnp.stack([halves[0][i], halves[1][i]], axis=len(hb)) for i in range(len(grads))]
+    part, hb = send, []
+    for bit in chip_bits(n_dp):
+        part, hb = exchange(part, hb, bit, d, n_dp)
+    both = part
     if n_dp > 1:
         both, hb = exchange(both, hb, 0, d, n_dp)
     return [b.reshape(g.shape[0] // n_fsdp, g.shape[1]).astype(jnp.float32) for b, g in zip(both, grads)]
@@ -364,9 +359,22 @@
         (grad_down_shard,) = reduce_chain([grad_down_weight], n_dp, n_fsdp)
         (grad_up_shard,) = reduce_chain([grad_up_weight], n_dp, n_fsdp)
         (grad_out_shard,) = reduce_chain([grad_out_weight], n_dp, n_fsdp)
-        grad_qkv_shard, vec_flat = reduce_chain(
-            [grad_qkv_weight, vec_grads.reshape(n_fsdp * 2 * n_dp, -1)], n_dp, n_fsdp
-        )
+        rows = grad_qkv_weight.shape[0] // (n_fsdp * 2 * n_dp)
+        slot = vec_grads.shape[1] // (2 * n_dp)
+        if slot % rows == 0:
+            qkv_view = grad_qkv_weight.astype(jnp.bfloat16).reshape(n_fsdp, n_dp, 2, rows, -1)
+            vec_view = vec_grads.reshape(n_fsdp, n_dp, 2, rows, slot // rows)
+            pad = -(slot // rows) % 128
+            vec_view = jnp.pad(vec_view, ((0, 0),) * 4 + ((0, pad),))
+            joined = jnp.concatenate([qkv_view, vec_view], axis=-1)
+            (both_shard,) = reduce_chain([joined.reshape(grad_qkv_weight.shape[0], -1)], n_dp, n_fsdp)
+            cols = grad_qkv_weight.shape[1]
+            grad_qkv_shard = both_shard[:, :cols]
+            vec_flat = both_shard[:, cols : cols + slot // rows].reshape(-1)
+        else:
+            grad_qkv_shard, vec_flat = reduce_chain(
+                [grad_qkv_weight, vec_grads.reshape(n_fsdp * 2 * n_dp, -1)], n_dp, n_fsdp
+            )
     else:
         grad_qkv_shard, grad_out_shard, grad_up_shard, grad_down_shard = reduce_weights_native(
             [w.astype(jnp.bfloat16) for w in (grad_qkv_weight, grad_out_weight, grad_up_weight, grad_down_weight)],

time: 648 us -> 587 us (0.906)
  waiting for transfers between devices: 214 us -> 172 us
  starting transfers between devices: 134 us -> 111 us
    ppermute x45 -> x32, waiting for transfers between devices: 103 us -> 77.7 us  [exchange(): got = lax.ppermute(leaves, 'dp', xor_pairs(n_dp, 1 << bit))]
    ppermute x15 -> x12, waiting for transfers between devices: 21.9 us -> 11.5 us  [reduce_chain(): got = lax.ppermute(send, 'fsdp', down)]
    ppermute x25 -> x20, starting transfers between devices: 21.7 us -> 13.9 us  [split_bit(): lax.ppermute([v.astype(jnp.bfloat16) for v in send], 'dp', xor_pairs(n_dp...]
    ppermute x45 -> x32, starting transfers between devices: 31.8 us -> 24.1 us  [exchange(): got = lax.ppermute(leaves, 'dp', xor_pairs(n_dp, 1 << bit))]
    ppermute x15 -> x12, starting transfers between devices: 45.2 us -> 38.3 us  [reduce_chain(): got = lax.ppermute(send, 'fsdp', down)]
    ppermute x25 -> x20, waiting for transfers between devices: 69.3 us -> 63.5 us  [split_bit(): lax.ppermute([v.astype(jnp.bfloat16) for v in send], 'dp', xor_pairs(n_dp...]
    unnamed x132 -> x137, local copies, waits for them, and re-layouts: 15.2 us -> 16.2 us
    select_n x36 -> x32, other arithmetic: 13.4 us -> 14.3 us  [exchange(): jnp.where(mine, jnp.stack([a, g], axis=pos), jnp.stack([g, a], axis=pos))]
  transfers between devices with their start and end apart: 100 -> 79, of which waited for: 53 -> 40; matrix products, arithmetic and copies ran while one was open for 20% -> 28% of each run, Pallas kernels for 0% -> 0%
where the time goes in v2:
time: 587 us; the launch traced here: 578 us
  waiting for transfers between devices  172 us (29%)
  matrix products  115 us (20%)
  starting transfers between devices  111 us (19%)
  local copies, waits for them, and re-layouts  90.9 us (15%)
  other arithmetic  82.8 us (14%)
  between operations  6.2 us (1%)
    ppermute x32, waiting for transfers between devices, exchange(): got = lax.ppermute(leaves, 'dp', xor_pairs(n_dp, 1 << bit))  77.7 us
    ppermute x20, waiting for transfers between devices, split_bit(): lax.ppermute([v.astype(jnp.bfloat16) for v in send], 'dp', xor_pairs(n_dp...  63.5 us
    ppermute x12, starting transfers between devices, reduce_chain(): got = lax.ppermute(send, 'fsdp', down)  38.3 us
    ppermute x15, starting transfers between devices, gather_chain(): buf = lax.ppermute(buf, 'fsdp', down)  34.9 us
    ppermute x32, starting transfers between devices, exchange(): got = lax.ppermute(leaves, 'dp', xor_pairs(n_dp, 1 << bit))  24.1 us
    ppermute x15, waiting for transfers between devices, gather_chain(): buf = lax.ppermute(buf, 'fsdp', down)  19.8 us
    add x12, other arithmetic, split_bit(): k.astype(jnp.float32) + g.astype(jnp.float32)  19.5 us
    concatenate x4, other arithmetic, gather_chain(): return (jnp.roll(rel, f, axis=0).reshape(n_fsdp * rows, cols), vecs)  16.8 us
  transfers between devices with their start and end apart: 79, of which 40 were waited for; matrix products, arithmetic and copies ran while one was open for 28% of the time, Pallas kernels for 0%

profile of v2, /device:TPU:0, one launch (start us, length us, event | category | flops | bytes accessed | tf_op | source)
XLA Modules:
  0.0 578.3 jit_solution(4418886509020071019)
XLA Ops:
  8.6 5.1 collective-permute-start
  29.7 6.8 %collective-permute-done.1 = bf16[3072]{0:T(1024)(128)(2,1)S(1)} collective-permute-done((bf16[3072]{0:T(1024)(128)(2,1)S(1)}, bf16[3072]{0:T(1024)(128)(2,1)S(1)}, u32[]{:S(2)}, u32[]{:S(2)}) %collective-permute-start.1) | collective-permute-done | bytes 6176 | tf_op jit(solution)/shard_map/ppermute | solution.py:151
  88.5 12.5 %collective-permute-done.30 = bf16[3,64,1024]{2,1,0:T(8,128)(2,1)S(1)} collective-permute-done((bf16[3,64,1024]{2,1,0:T(8,128)(2,1)S(1)}, bf16[3,64,1024]{2,1,0:T(8,128)(2,1)S(1)}, u32[]{:S(2)}, u32[]{:S(2)}) %collective-permute-start.30) | collective-permute-done | bytes 393248 | tf_op jit(solution)/shard_map/ppermute | solution.py:118
  106.7 10.5 %collective-permute-done.9 = bf16[3,2,16,3072]{3,2,1,0:T(8,128)(2,1)S(1)} collective-permute-done((bf16[3,2,16,3072]{3,2,1,0:T(8,128)(2,1)S(1)}, bf16[3,2,16,3072]{3,2,1,0:T(8,128)(2,1)S(1)}, u32[]{:S(2)}, u32[]{:S(2)}) %collective-permute-start.9) | collective-permute-done | bytes 589856 | tf_op jit(solution)/shard_map/ppermute | solution.py:118
  122.7 11.4 %collective-permute-done.25 = bf16[3,2,16,4096]{3,2,1,0:T(8,128)(2,1)S(1)} collective-permute-done((bf16[3,2,16,4096]{3,2,1,0:T(8,128)(2,1)S(1)}, bf16[3,2,16,4096]{3,2,1,0:T(8,128)(2,1)S(1)}, u32[]{:S(2)}, u32[]{:S(2)}) %collective-permute-start.25) | collective-permute-done | bytes 786464 | tf_op jit(solution)/shard_map/ppermute | solution.py:118
  137.0 10.3 %collective-permute-done.33 = bf16[3,2,64,1024]{3,2,1,0:T(8,128)(2,1)S(1)} collective-permute-done((bf16[3,2,64,1024]{3,2,1,0:T(8,128)(2,1)S(1)}, bf16[3,2,64,1024]{3,2,1,0:T(8,128)(2,1)S(1)}, u32[]{:S(2)}, u32[]{:S(2)}) %collective-permute-start.33) | collective-permute-done | bytes 786464 | tf_op jit(solution)/shard_map/ppermute | solution.py:118
  203.2 5.2 fusion.11
  208.4 6.3 %maximum_select_fusion.1 = bf16[3,2,2,2,2,64,1024]{6,5,4,3,2,1,0:T(8,128)(2,1)S(1)} fusion(bf16[3,2,2,1,2,64,1024]{6,5,4,3,2,1,0:T(8,128)(2,1)} %bitcast.95, bf16[3,2,2,1,2,64,1024]{6,5,4,3,2,1,0:T(8,128)(2,1)S(1)} %copy-done.4, pred[]{:T(512)S(6)} %eq.43), kind=kLoop, calls=%fused_computation.39 | loop fusion | flops 9437184 | bytes 12582913 | tf_op jit(solution)/shard_map/jit(_where)/select_n | solution.py:122
  214.9 5.1 fusion.8
  220.1 10.9 %multiply_convert_fusion = (bf16[600,4096]{1,0:T(8,128)(2,1)}, f32[600,4096]{1,0:T(8,128)}) fusion(f32[4096]{0:T(1024)S(1)} %bitcast.590, bf16[1024,4096]{1,0:T(8,128)(2,1)S(1)} %bitcast.486, f32[600,1024]{1,0:T(8,128)S(1)} %get-tuple-element.94, f32[1024]{0:T(1024)S(1)} %bitcast.597, f32[1024]{0:T(1024)S(1)} %bitcast.582, f32[600]{0:T(1024)S(1)} %add_rsqrt_fusion, ...), kind=kOutput, calls=%fused_computation.19 | convolution fusion | flops 5050982400 | bytes 25621184 | tf_op jit(solution)/shard_map/dot_general | solution.py:309
  231.0 12.9 %fusion.191 = (bf16[4096]{0:T(1024)(128)(2,1)S(1)}, bf16[600,4096]{1,0:T(8,128)(2,1)S(1)}) fusion(f32[600,4096]{1,0:T(8,128)} %get-tuple-element.96, f32[4096]{0:T(1024)S(1)} %bitcast.591, bf16[4096,1024]{1,0:T(8,128)(2,1)S(1)} %bitcast.482, bf16[600,1024]{1,0:T(8,128)(2,1)S(1)} %copy-done.36, f32[]{:T(128)} %bitcast.98), kind=kOutput, calls=%fused_computation.427 | convolution fusion | flops 5064495104 | bytes 24387588 | tf_op jit(solution)/shard_map/dot_general | solution.py:319
  243.9 10.6 %multiply_reduce_fusion.1 = (bf16[1024]{0:T(1024)(128)(2,1)S(1)}, f32[600]{0:T(1024)S(1)}, f32[600]{0:T(1024)S(1)}, bf16[1024]{0:T(1024)(128)(2,1)S(1)}, f32[600,1024]{1,0:T(8,128)S(1)}) fusion(f32[600,1024]{1,0:T(8,128)S(1)} %get-tuple-element.94, f32[600]{0:T(1024)S(1)} %add_rsqrt_fusion, f32[600]{0:T(1024)S(1)} %broadcast_multiply_fusion.4, ...), kind=kOutput, calls=%fused_computation.127 | convolution fusion | flops 5038691328 | bytes 18236800 | tf_op jit(solution)/shard_map/dot_general | solution.py:324
  261.2 9.8 %convolution_convert_fusion = bf16[1024,4096]{1,0:T(8,128)(2,1)} fusion(bf16[600,4096]{1,0:T(8,128)(2,1)S(1)} %bitcast.610, f32[600,1024]{1,0:T(8,128)S(1)} %get-tuple-element.94, f32[1024]{0:T(1024)S(1)} %bitcast.598, f32[1024]{0:T(1024)S(1)} %bitcast.585, f32[600]{0:T(1024)S(1)} %add_rsqrt_fusion, f32[600]{0:T(1024)S(1)} %broadcast_multiply_fusion.4), kind=kOutput, calls=%fused_computation.31 | convolution fusion | flops 5040431104 | bytes 15774400 | tf_op jit(solution)/shard_map/dot_general | solution.py:322
  273.8 6.6 %fusion.190 = (bf16[16,64]{1,0:T(8,128)(2,1)S(1)}, bf16[12,50,16,64]{3,1,2,0:T(8,128)(2,1)}) fusion(f32[12,16,50,50]{2,3,1,0:T(8,128)} %copy-done, f32[12,16,50]{2,1,0:T(8,128)S(1)} %log_add_fusion, bf16[12,50,16,64]{3,2,1,0:T(8,128)(2,1)} %reshape.2519), kind=kOutput, calls=%fused_computation.426 | convolution fusion | flops 63627776 | bytes 4418048 | tf_op jit(solution)/shard_map/chqk,cqhd->ckhd/dot_general | solution.py:88
  289.9 12.6 %convolution_convert_fusion.1 = bf16[4096,1024]{1,0:T(8,128)(2,1)} fusion(bf16[600,4096]{1,0:T(8,128)(2,1)} %get-tuple-element.95, bf16[600,1024]{1,0:T(8,128)(2,1)S(1)} %copy-done.37, f32[]{:T(128)} %bitcast.98), kind=kOutput, calls=%fused_computation.32 | convolution fusion | flops 5039202304 | bytes 14532612 | tf_op jit(solution)/shard_map/dot_general | solution.py:317
  302.6 6.4 %add_convert_fusion.1 = bf16[600,1024]{1,0:T(8,128)(2,1)} fusion(f32[600,1024]{1,0:T(8,128)S(1)} %copy-done.15, bf16[600,4096]{1,0:T(8,128)(2,1)S(1)} %bitcast.612, bf16[4096,1024]{1,0:T(8,128)(2,1)S(1)} %bitcast.485, f32[1024]{0:T(1024)S(1)} %bitcast.596), kind=kOutput, calls=%fused_computation.132 | convolution fusion | flops 5035008000 | bytes 16994304 | tf_op jit(solution)/shard_map/dot_general | solution.py:313
  336.2 9.7 %fusion.52 = (bf16[1024]{0:T(1024)(128)(2,1)S(1)}, f32[600]{0:T(1024)S(1)}, f32[600]{0:T(1024)S(1)}, bf16[1024]{0:T(1024)(128)(2,1)S(1)}, f32[600,1024]{1,0:T(8,128)}) fusion(bf16[600,1024]{1,0:T(8,128)(2,1)S(1)} %copy-done.7, f32[600]{0:T(1024)S(1)} %add_rsqrt_fusion.1, f32[600]{0:T(1024)S(1)} %broadcast_multiply_fusion.5, f32[1024]{0:T(1024)S(1)} %bitcast.587, ...), kind=kOutput, calls=%fused_computation.125 | convolution fusion | flops 3781014528 | bytes 13682048 | tf_op jit(solution)/shard_map/dot_general | solution.py:338
  346.7 7.9 %convolution_convert_fusion.2 = bf16[1024,3072]{1,0:T(8,128)(2,1)S(1)} fusion(bf16[600,3072]{1,0:T(8,128)(2,1)} %constant_dynamic-update-slice_fusion, bf16[600,1024]{1,0:T(8,128)(2,1)S(1)} %copy-done.7, f32[1024]{0:T(1024)S(1)} %bitcast.595, f32[1024]{0:T(1024)S(1)} %bitcast.588, f32[600]{0:T(1024)S(1)} %add_rsqrt_fusion.1, ...), kind=kOutput, calls=%fused_computation.42 | convolution fusion | flops 3781705728 | bytes 11219648 | tf_op jit(solution)/shard_map/dot_general | solution.py:335
  410.8 15.2 %collective-permute-done.36 = bf16[4,2,16,3200]{3,2,0,1:T(8,128)(2,1)S(1)} collective-permute-done((bf16[4,2,16,3200]{3,2,0,1:T(8,128)(2,1)S(1)}, bf16[4,2,16,3200]{3,2,0,1:T(8,128)(2,1)S(1)}, u32[]{:S(2)}, u32[]{:S(2)}) %collective-permute-start.36) | collective-permute-done | bytes 819232 | tf_op jit(solution)/shard_map/ppermute | solution.py:133
  449.5 5.6 convert_add_fusion
  480.2 16.6 %collective-permute-done.69 = bf16[4,2,64,1024]{3,2,0,1:T(8,128)(2,1)S(1)} collective-permute-done((bf16[4,2,64,1024]{3,2,0,1:T(8,128)(2,1)S(1)}, bf16[4,2,64,1024]{3,2,0,1:T(8,128)(2,1)S(1)}, u32[]{:S(2)}, u32[]{:S(2)}) %collective-permute-start.69) | collective-permute-done | bytes 1048608 | tf_op jit(solution)/shard_map/ppermute | solution.py:133
  505.4 5.9 %collective-permute-done.59 = bf16[4,16,4096]{2,1,0:T(8,128)(2,1)S(1)} collective-permute-done((bf16[4,16,4096]{2,1,0:T(8,128)(2,1)S(1)}, bf16[4,16,4096]{2,1,0:T(8,128)(2,1)S(1)}, u32[]{:S(2)}, u32[]{:S(2)}) %collective-permute-start.59) | collective-permute-done | bytes 524320 | tf_op jit(solution)/shard_map/ppermute | solution.py:133
  553.6 9.7 %collective-permute-done.66 = bf16[2,2,16,4096]{3,2,1,0:T(8,128)(2,1)S(1)} collective-permute-done((bf16[2,2,16,4096]{3,2,1,0:T(8,128)(2,1)S(1)}, bf16[2,2,16,4096]{3,2,1,0:T(8,128)(2,1)S(1)}, u32[]{:S(2)}, u32[]{:S(2)}) %collective-permute-start.66) | collective-permute-done | bytes 524320 | tf_op jit(solution)/shard_map/ppermute | solution.py:118
  563.7 8.2 %collective-permute-done.77 = bf16[2,2,64,1024]{3,2,1,0:T(8,128)(2,1)S(1)} collective-permute-done((bf16[2,2,64,1024]{3,2,1,0:T(8,128)(2,1)S(1)}, bf16[2,2,64,1024]{3,2,1,0:T(8,128)(2,1)S(1)}, u32[]{:S(2)}, u32[]{:S(2)}) %collective-permute-start.77) | collective-permute-done | bytes 524320 | tf_op jit(solution)/shard_map/ppermute | solution.py:118
  (500 shorter events, 350.6 us)
Async XLA Ops:
  15.0 26.6 %collective-permute-start.11 = (bf16[2,16,1024]{2,1,0:T(8,128)(2,1)S(1)}, bf16[2,16,1024]{2,1,0:T(8,128)(2,1)S(1)}, u32[]{:S(2)}, u32[]{:S(2)}) collective-permute-start(bf16[2,16,1024]{2,1,0:T(8,128)(2,1)S(1)} %dynamic-slice_bitcast_fusion.6), channel_id=1, source_target_pairs={{0,3},{1,0},{2,1},{3,2},{4,7},{5,4},{6,5},{7,6},{8,11},{9,8},{10,9... | collective-permute-start | bytes 196616 | tf_op jit(solution)/shard_map/ppermute | solution.py:151
  19.1 36.4 %collective-permute-start.3 = (bf16[2,16,3072]{2,1,0:T(8,128)(2,1)S(1)}, bf16[2,16,3072]{2,1,0:T(8,128)(2,1)S(1)}, u32[]{:S(2)}, u32[]{:S(2)}) collective-permute-start(bf16[2,16,3072]{2,1,0:T(8,128)(2,1)S(1)} %dynamic-slice_bitcast_fusion.5), channel_id=1, source_target_pairs={{0,3},{1,0},{2,1},{3,2},{4,7},{5,4},{6,5},{7,6},{8,11},{9,8},{10,9... | collective-permute-start | bytes 589832 | tf_op jit(solution)/shard_map/ppermute | solution.py:151
  21.2 38.5 %collective-permute-start.19 = (bf16[2,16,4096]{2,1,0:T(8,128)(2,1)S(1)}, bf16[2,16,4096]{2,1,0:T(8,128)(2,1)S(1)}, u32[]{:S(2)}, u32[]{:S(2)}) collective-permute-start(bf16[2,16,4096]{2,1,0:T(8,128)(2,1)S(1)} %dynamic-slice_bitcast_fusion.4), channel_id=1, source_target_pairs={{0,3},{1,0},{2,1},{3,2},{4,7},{5,4},{6,5},{7,6},{8,11},{9,8},{10,9... | collective-permute-start | bytes 786440 | tf_op jit(solution)/shard_map/ppermute | solution.py:151
  23.7 36.1 %collective-permute-start.27 = (bf16[2,64,1024]{2,1,0:T(8,128)(2,1)S(1)}, bf16[2,64,1024]{2,1,0:T(8,128)(2,1)S(1)}, u32[]{:S(2)}, u32[]{:S(2)}) collective-permute-start(bf16[2,64,1024]{2,1,0:T(8,128)(2,1)S(1)} %dynamic-slice_bitcast_fusion.3), channel_id=1, source_target_pairs={{0,3},{1,0},{2,1},{3,2},{4,7},{5,4},{6,5},{7,6},{8,11},{9,8},{10,9... | collective-permute-start | bytes 786440 | tf_op jit(solution)/shard_map/ppermute | solution.py:151
  69.5 49.7 %collective-permute-start.18 = (bf16[3,2,2,2,16,1024]{5,4,3,2,1,0:T(8,128)(2,1)S(1)}, bf16[3,2,2,2,16,1024]{5,4,3,2,1,0:T(8,128)(2,1)S(1)}, u32[]{:S(2)}, u32[]{:S(2)}) collective-permute-start(bf16[3,2,2,2,16,1024]{5,4,3,2,1,0:T(8,128)(2,1)S(1)} %get-tuple-element.58), channel_id=1, source_target_pairs={{0,4},{4,0},{8,12},{12,8},{16,20},{20,16},{24,28},{28,24},{1,5},{5... | collective-permute-start | bytes 2359304 | tf_op jit(solution)/shard_map/ppermute | solution.py:118
  101.9 32.2 %collective-permute-start.25 = (bf16[3,2,16,4096]{3,2,1,0:T(8,128)(2,1)S(1)}, bf16[3,2,16,4096]{3,2,1,0:T(8,128)(2,1)S(1)}, u32[]{:S(2)}, u32[]{:S(2)}) collective-permute-start(bf16[3,2,16,4096]{3,2,1,0:T(8,128)(2,1)S(1)} %maximum_select_fusion.22), channel_id=1, source_target_pairs={{0,8},{4,12},{8,0},{12,4},{16,24},{20,28},{24,16},{28,20},{1,9},{5... | collective-permute-start | bytes 2359304 | tf_op jit(solution)/shard_map/ppermute | solution.py:118
  105.5 29.5 %collective-permute-start.23 = (bf16[3,2,16,4096]{3,2,1,0:T(8,128)(2,1)S(1)}, bf16[3,2,16,4096]{3,2,1,0:T(8,128)(2,1)S(1)}, u32[]{:S(2)}, u32[]{:S(2)}) collective-permute-start(bf16[3,2,16,4096]{3,2,1,0:T(8,128)(2,1)S(1)} %maximum_select_fusion.20), channel_id=1, source_target_pairs={{0,16},{4,20},{8,24},{12,28},{16,0},{20,4},{24,8},{28,12},{1,17},{... | collective-permute-start | bytes 2359304 | tf_op jit(solution)/shard_map/ppermute | solution.py:118
  117.2 30.1 %collective-permute-start.33 = (bf16[3,2,64,1024]{3,2,1,0:T(8,128)(2,1)S(1)}, bf16[3,2,64,1024]{3,2,1,0:T(8,128)(2,1)S(1)}, u32[]{:S(2)}, u32[]{:S(2)}) collective-permute-start(bf16[3,2,64,1024]{3,2,1,0:T(8,128)(2,1)S(1)} %maximum_select_fusion.26), channel_id=1, source_target_pairs={{0,8},{4,12},{8,0},{12,4},{16,24},{20,28},{24,16},{28,20},{1,9},{5... | collective-permute-start | bytes 2359304 | tf_op jit(solution)/shard_map/ppermute | solution.py:118
  119.0 34.0 %collective-permute-start.10 = (bf16[3,2,2,2,16,3072]{5,4,3,2,1,0:T(8,128)(2,1)S(1)}, bf16[3,2,2,2,16,3072]{5,4,3,2,1,0:T(8,128)(2,1)S(1)}, u32[]{:S(2)}, u32[]{:S(2)}) collective-permute-start(bf16[3,2,2,2,16,3072]{5,4,3,2,1,0:T(8,128)(2,1)S(1)} %get-tuple-element.39), channel_id=1, source_target_pairs={{0,4},{4,0},{8,12},{12,8},{16,20},{20,16},{24,28},{28,24},{1,5},{5... | collective-permute-start | bytes 7077896 | tf_op jit(solution)/shard_map/ppermute | solution.py:118
  119.2 30.6 %collective-permute-start.31 = (bf16[3,2,64,1024]{3,2,1,0:T(8,128)(2,1)S(1)}, bf16[3,2,64,1024]{3,2,1,0:T(8,128)(2,1)S(1)}, u32[]{:S(2)}, u32[]{:S(2)}) collective-permute-start(bf16[3,2,64,1024]{3,2,1,0:T(8,128)(2,1)S(1)} %maximum_select_fusion.24), channel_id=1, source_target_pairs={{0,16},{4,20},{8,24},{12,28},{16,0},{20,4},{24,8},{28,12},{1,17},{... | collective-permute-start | bytes 2359304 | tf_op jit(solution)/shard_map/ppermute | solution.py:118
  137.0 61.7 %collective-permute-start.26 = (bf16[3,2,2,2,16,4096]{5,4,3,2,1,0:T(8,128)(2,1)}, bf16[3,2,2,2,16,4096]{5,4,3,2,1,0:T(8,128)(2,1)}, u32[]{:S(2)}, u32[]{:S(2)}) collective-permute-start(bf16[3,2,2,2,16,4096]{5,4,3,2,1,0:T(8,128)(2,1)} %get-tuple-element.37), channel_id=1, source_target_pairs={{0,4},{4,0},{8,12},{12,8},{16,20},{20,16},{24,28},{28,24},{1,5},{5... | collective-permute-start | bytes 9437192 | tf_op jit(solution)/shard_map/ppermute | solution.py:118
  153.0 55.4 %collective-permute-start.34 = (bf16[3,2,2,2,64,1024]{5,4,3,2,1,0:T(8,128)(2,1)}, bf16[3,2,2,2,64,1024]{5,4,3,2,1,0:T(8,128)(2,1)}, u32[]{:S(2)}, u32[]{:S(2)}) collective-permute-start(bf16[3,2,2,2,64,1024]{5,4,3,2,1,0:T(8,128)(2,1)} %get-tuple-element.35), channel_id=1, source_target_pairs={{0,4},{4,0},{8,12},{12,8},{16,20},{20,16},{24,28},{28,24},{1,5},{5... | collective-permute-start | bytes 9437192 | tf_op jit(solution)/shard_map/ppermute | solution.py:118
  311.3 43.3 %collective-permute-start.46 = (bf16[4,2,2,2,16,1024]{5,4,3,2,1,0:T(8,128)(2,1)}, bf16[4,2,2,2,16,1024]{5,4,3,2,1,0:T(8,128)(2,1)}, u32[]{:S(2)}, u32[]{:S(2)}) collective-permute-start(bf16[4,2,2,2,16,1024]{5,4,3,2,1,0:T(8,128)(2,1)} %dynamic-slice_bitcast_fusion.2), channel_id=1, source_target_pairs={{0,4},{4,0},{8,12},{12,8},{16,20},{20,16},{24,28},{28,24},{1,5},{5... | collective-permute-start | bytes 3145736 | tf_op jit(solution)/shard_map/ppermute | solution.py:133
  359.0 42.6 %collective-permute-start.35 = (bf16[4,2,2,2,16,3200]{5,4,3,2,1,0:T(8,128)(2,1)}, bf16[4,2,2,2,16,3200]{5,4,3,2,1,0:T(8,128)(2,1)}, u32[]{:S(2)}, u32[]{:S(2)}) collective-permute-start(bf16[4,2,2,2,16,3200]{5,4,3,2,1,0:T(8,128)(2,1)} %fusion.18), channel_id=1, source_target_pairs={{0,4},{4,0},{8,12},{12,8},{16,20},{20,16},{24,28},{28,24},{1,5},{5... | collective-permute-start | bytes 9830408 | tf_op jit(solution)/shard_map/ppermute | solution.py:133
  395.5 38.5 %collective-permute-start.57 = (bf16[4,2,2,2,16,4096]{5,4,3,2,1,0:T(8,128)(2,1)S(1)}, bf16[4,2,2,2,16,4096]{5,4,3,2,1,0:T(8,128)(2,1)}, u32[]{:S(2)}, u32[]{:S(2)}) collective-permute-start(bf16[4,2,2,2,16,4096]{5,4,3,2,1,0:T(8,128)(2,1)S(1)} %copy-done.29), channel_id=1, source_target_pairs={{0,4},{4,0},{8,12},{12,8},{16,20},{20,16},{24,28},{28,24},{1,5},{5... | collective-permute-start | bytes 12582920 | tf_op jit(solution)/shard_map/ppermute | solution.py:133
  395.5 54.0 %collective-permute-start.68 = (bf16[4,2,2,2,64,1024]{5,4,3,2,1,0:T(8,128)(2,1)}, bf16[4,2,2,2,64,1024]{5,4,3,2,1,0:T(8,128)(2,1)}, u32[]{:S(2)}, u32[]{:S(2)}) collective-permute-start(bf16[4,2,2,2,64,1024]{5,4,3,2,1,0:T(8,128)(2,1)} %dynamic-slice_bitcast_fusion), channel_id=1, source_target_pairs={{0,4},{4,0},{8,12},{12,8},{16,20},{20,16},{24,28},{28,24},{1,5},{5... | collective-permute-start | bytes 12582920 | tf_op jit(solution)/shard_map/ppermute | solution.py:133
  440.2 36.6 %collective-permute-start.58 = (bf16[4,2,16,4096]{3,2,0,1:T(8,128)(2,1)S(1)}, bf16[4,2,16,4096]{3,2,0,1:T(8,128)(2,1)}, u32[]{:S(2)}, u32[]{:S(2)}) collective-permute-start(bf16[4,2,16,4096]{3,2,0,1:T(8,128)(2,1)S(1)} %fusion.80), channel_id=1, source_target_pairs={{0,16},{4,20},{8,24},{12,28},{16,0},{20,4},{24,8},{28,12},{1,17},{... | collective-permute-start | bytes 3145736 | tf_op jit(solution)/shard_map/ppermute | solution.py:133
  440.8 37.6 %collective-permute-start.60 = (bf16[4,2,16,4096]{3,2,1,0:T(8,128)(2,1)S(1)}, bf16[4,2,16,4096]{3,2,1,0:T(8,128)(2,1)}, u32[]{:S(2)}, u32[]{:S(2)}) collective-permute-start(bf16[4,2,16,4096]{3,2,1,0:T(8,128)(2,1)S(1)} %fusion.78), channel_id=1, source_target_pairs={{0,8},{4,12},{8,0},{12,4},{16,24},{20,28},{24,16},{28,20},{1,9},{5... | collective-permute-start | bytes 3145736 | tf_op jit(solution)/shard_map/ppermute | solution.py:133
  469.0 27.8 %collective-permute-start.69 = (bf16[4,2,64,1024]{3,2,0,1:T(8,128)(2,1)S(1)}, bf16[4,2,64,1024]{3,2,0,1:T(8,128)(2,1)S(1)}, u32[]{:S(2)}, u32[]{:S(2)}) collective-permute-start(bf16[4,2,64,1024]{3,2,0,1:T(8,128)(2,1)S(1)} %fusion.81), channel_id=1, source_target_pairs={{0,16},{4,20},{8,24},{12,28},{16,0},{20,4},{24,8},{28,12},{1,17},{... | collective-permute-start | bytes 3145736 | tf_op jit(solution)/shard_map/ppermute | solution.py:133
  474.6 26.1 %collective-permute-start.71 = (bf16[4,2,64,1024]{3,2,1,0:T(8,128)(2,1)S(1)}, bf16[4,2,64,1024]{3,2,1,0:T(8,128)(2,1)S(1)}, u32[]{:S(2)}, u32[]{:S(2)}) collective-permute-start(bf16[4,2,64,1024]{3,2,1,0:T(8,128)(2,1)S(1)} %fusion.79), channel_id=1, source_target_pairs={{0,8},{4,12},{8,0},{12,4},{16,24},{20,28},{24,16},{28,20},{1,9},{5... | collective-permute-start | bytes 3145736 | tf_op jit(solution)/shard_map/ppermute | solution.py:133
  474.7 30.3 %collective-permute-start.43 = (bf16[2,16,3200]{2,1,0:T(8,128)(2,1)S(1)}, bf16[2,16,3200]{2,1,0:T(8,128)(2,1)S(1)}, u32[]{:S(2)}, u32[]{:S(2)}) collective-permute-start(bf16[2,16,3200]{2,1,0:T(8,128)(2,1)S(1)} %fusion.135), channel_id=1, source_target_pairs={{0,8},{4,12},{8,0},{12,4},{16,24},{20,28},{24,16},{28,20},{1,9},{5... | collective-permute-start | bytes 614408 | tf_op jit(solution)/shard_map/ppermute | solution.py:118
  478.3 32.9 %collective-permute-start.59 = (bf16[4,16,4096]{2,1,0:T(8,128)(2,1)S(1)}, bf16[4,16,4096]{2,1,0:T(8,128)(2,1)S(1)}, u32[]{:S(2)}, u32[]{:S(2)}) collective-permute-start(bf16[4,16,4096]{2,1,0:T(8,128)(2,1)S(1)} %fusion.96), channel_id=1, source_target_pairs={{0,8},{4,12},{8,0},{12,4},{16,24},{20,28},{24,16},{28,20},{1,9},{5... | collective-permute-start | bytes 1572872 | tf_op jit(solution)/shard_map/ppermute | solution.py:133
  480.2 31.2 %collective-permute-start.61 = (bf16[4,16,4096]{2,1,0:T(8,128)(2,1)S(1)}, bf16[4,16,4096]{2,1,0:T(8,128)(2,1)S(1)}, u32[]{:S(2)}, u32[]{:S(2)}) collective-permute-start(bf16[4,16,4096]{2,1,0:T(8,128)(2,1)S(1)} %fusion.97), channel_id=1, source_target_pairs={{0,16},{4,20},{8,24},{12,28},{16,0},{20,4},{24,8},{28,12},{1,17},{... | collective-permute-start | bytes 1572872 | tf_op jit(solution)/shard_map/ppermute | solution.py:133
  522.1 22.4 %collective-permute-start.45 = (bf16[2,2,2,16,3200]{4,3,2,1,0:T(8,128)(2,1)S(1)}, bf16[2,2,2,16,3200]{4,3,2,1,0:T(8,128)(2,1)S(1)}, u32[]{:S(2)}, u32[]{:S(2)}) collective-permute-start(bf16[2,2,2,16,3200]{4,3,2,1,0:T(8,128)(2,1)S(1)} %maximum_select_fusion.18), channel_id=1, source_target_pairs={{0,4},{4,0},{8,12},{12,8},{16,20},{20,16},{24,28},{28,24},{1,5},{5... | collective-permute-start | bytes 2457608 | tf_op jit(solution)/shard_map/ppermute | solution.py:118
  (110 other events, 1188.8 us)

commit v3 on v2

--- a/solution.py
+++ b/solution.py
@@ -356,8 +356,15 @@
         [g.astype(jnp.bfloat16).reshape(n_fsdp, -1) for g in grad_vectors], axis=1
     )
     if small:
-        (grad_down_shard,) = reduce_chain([grad_down_weight], n_dp, n_fsdp)
-        (grad_up_shard,) = reduce_chain([grad_up_weight], n_dp, n_fsdp)
+        width = grad_down_weight.shape[1]
+        up_view = grad_up_weight.astype(jnp.bfloat16).reshape(n_fsdp, n_dp, 2, -1, width)
+        down_view = grad_down_weight.astype(jnp.bfloat16).reshape(n_fsdp, n_dp, 2, -1, width)
+        split = up_view.shape[3]
+        mlp = jnp.concatenate([up_view, down_view], axis=3)
+        (mlp_shard,) = reduce_chain([mlp.reshape(-1, width)], n_dp, n_fsdp)
+        mlp_shard = mlp_shard.reshape(n_dp, 2, -1, width)
+        grad_up_shard = mlp_shard[:, :, :split].reshape(grad_up_weight.shape[0] // n_fsdp, -1)
+        grad_down_shard = mlp_shard[:, :, split:].reshape(grad_down_weight.shape[0] // n_fsdp, -1)
         (grad_out_shard,) = reduce_chain([grad_out_weight], n_dp, n_fsdp)
         rows = grad_qkv_weight.shape[0] // (n_fsdp * 2 * n_dp)
         slot = vec_grads.shape[1] // (2 * n_dp)

time: 587 us -> 651 us (1.11)
  waiting for transfers between devices: 172 us -> 217 us
  local copies, waits for them, and re-layouts: 90.9 us -> 117 us
  starting transfers between devices: 111 us -> 92.2 us
  other arithmetic: 82.8 us -> 93.8 us
    ppermute x12 -> x9, waiting for transfers between devices: 11.5 us -> 34.9 us  [reduce_chain(): got = lax.ppermute(send, 'fsdp', down)]
    ppermute x20 -> x15, waiting for transfers between devices: 63.5 us -> 78.4 us  [split_bit(): lax.ppermute([v.astype(jnp.bfloat16) for v in send], 'dp', xor_pairs(n_dp...]
    ppermute x12 -> x9, starting transfers between devices: 38.3 us -> 24.2 us  [reduce_chain(): got = lax.ppermute(send, 'fsdp', down)]
    concatenate x0 -> x1, local copies, waits for them, and re-layouts: none -> 14.1 us  [local_body(): mlp = jnp.concatenate([up_view, down_view], axis=3)]
    unnamed x137 -> x134, local copies, waits for them, and re-layouts: 16.2 us -> 26.7 us
    squeeze x3 -> x1, local copies, waits for them, and re-layouts: 7.61 us -> 1.08 us  [split_bit(): lax.dynamic_index_in_dim(a, 1 - mine, axis, keepdims=False)]
    ppermute x32 -> x29, waiting for transfers between devices: 77.7 us -> 83.7 us  [exchange(): got = lax.ppermute(leaves, 'dp', xor_pairs(n_dp, 1 << bit))]
    ppermute x32 -> x29, starting transfers between devices: 24.1 us -> 18.9 us  [exchange(): got = lax.ppermute(leaves, 'dp', xor_pairs(n_dp, 1 << bit))]
  transfers between devices with their start and end apart: 79 -> 68, of which waited for: 40 -> 35; matrix products, arithmetic and copies ran while one was open for 28% -> 25% of each run, Pallas kernels for 0% -> 0%
where the time goes in v3:
time: 651 us; the launch traced here: 642 us
  waiting for transfers between devices  217 us (33%)
  local copies, waits for them, and re-layouts  117 us (18%)
  matrix products  116 us (18%)
  other arithmetic  93.8 us (14%)
  starting transfers between devices  92.2 us (14%)
    ppermute x29, waiting for transfers between devices, exchange(): got = lax.ppermute(leaves, 'dp', xor_pairs(n_dp, 1 << bit))  83.7 us
    ppermute x15, waiting for transfers between devices, split_bit(): lax.ppermute([v.astype(jnp.bfloat16) for v in send], 'dp', xor_pairs(n_dp...  78.4 us
    ppermute x9, waiting for transfers between devices, reduce_chain(): got = lax.ppermute(send, 'fsdp', down)  34.9 us
    ppermute x15, starting transfers between devices, gather_chain(): buf = lax.ppermute(buf, 'fsdp', down)  34.8 us
    unnamed x134, local copies, waits for them, and re-layouts  26.7 us
    ppermute x9, starting transfers between devices, reduce_chain(): got = lax.ppermute(send, 'fsdp', down)  24.2 us
    ppermute x15, waiting for transfers between devices, gather_chain(): buf = lax.ppermute(buf, 'fsdp', down)  19.9 us
    select_n x29, other arithmetic, exchange(): jnp.where(mine, jnp.stack([a, g], axis=pos), jnp.stack([g, a], axis=pos))  19.4 us
  transfers between devices with their start and end apart: 68, of which 35 were waited for; matrix products, arithmetic and copies ran while one was open for 25% of the time, Pallas kernels for 0%

profile of v3, /device:TPU:0, one launch (start us, length us, event | category | flops | bytes accessed | tf_op | source)
XLA Modules:
  0.0 641.8 jit_solution(14861320825940011773)
XLA Ops:
  29.6 6.8 %collective-permute-done.1 = bf16[3072]{0:T(1024)(128)(2,1)S(1)} collective-permute-done((bf16[3072]{0:T(1024)(128)(2,1)S(1)}, bf16[3072]{0:T(1024)(128)(2,1)S(1)}, u32[]{:S(2)}, u32[]{:S(2)}) %collective-permute-start.1) | collective-permute-done | bytes 6176 | tf_op jit(solution)/shard_map/ppermute | solution.py:151
  88.4 12.5 %collective-permute-done.30 = bf16[3,64,1024]{2,1,0:T(8,128)(2,1)S(1)} collective-permute-done((bf16[3,64,1024]{2,1,0:T(8,128)(2,1)S(1)}, bf16[3,64,1024]{2,1,0:T(8,128)(2,1)S(1)}, u32[]{:S(2)}, u32[]{:S(2)}) %collective-permute-start.30) | collective-permute-done | bytes 393248 | tf_op jit(solution)/shard_map/ppermute | solution.py:118
  106.6 10.5 %collective-permute-done.9 = bf16[3,2,16,3072]{3,2,1,0:T(8,128)(2,1)S(1)} collective-permute-done((bf16[3,2,16,3072]{3,2,1,0:T(8,128)(2,1)S(1)}, bf16[3,2,16,3072]{3,2,1,0:T(8,128)(2,1)S(1)}, u32[]{:S(2)}, u32[]{:S(2)}) %collective-permute-start.9) | collective-permute-done | bytes 589856 | tf_op jit(solution)/shard_map/ppermute | solution.py:118
  122.4 11.6 %collective-permute-done.25 = bf16[3,2,16,4096]{3,2,1,0:T(8,128)(2,1)S(1)} collective-permute-done((bf16[3,2,16,4096]{3,2,1,0:T(8,128)(2,1)S(1)}, bf16[3,2,16,4096]{3,2,1,0:T(8,128)(2,1)S(1)}, u32[]{:S(2)}, u32[]{:S(2)}) %collective-permute-start.25) | collective-permute-done | bytes 786464 | tf_op jit(solution)/shard_map/ppermute | solution.py:118
  137.0 10.3 %collective-permute-done.33 = bf16[3,2,64,1024]{3,2,1,0:T(8,128)(2,1)S(1)} collective-permute-done((bf16[3,2,64,1024]{3,2,1,0:T(8,128)(2,1)S(1)}, bf16[3,2,64,1024]{3,2,1,0:T(8,128)(2,1)S(1)}, u32[]{:S(2)}, u32[]{:S(2)}) %collective-permute-start.33) | collective-permute-done | bytes 786464 | tf_op jit(solution)/shard_map/ppermute | solution.py:118
  219.9 11.0 %multiply_convert_fusion = (bf16[600,4096]{1,0:T(8,128)(2,1)}, f32[600,4096]{1,0:T(8,128)}) fusion(f32[4096]{0:T(1024)S(1)} %bitcast.532, bf16[1024,4096]{1,0:T(8,128)(2,1)S(1)} %bitcast.439, f32[600,1024]{1,0:T(8,128)S(1)} %get-tuple-element.96, f32[1024]{0:T(1024)S(1)} %bitcast.539, f32[1024]{0:T(1024)S(1)} %bitcast.524, f32[600]{0:T(1024)S(1)} %add_rsqrt_fusion, ...), kind=kOutput, calls=%fused_computation.24 | convolution fusion | flops 5050982400 | bytes 25621184 | tf_op jit(solution)/shard_map/dot_general | solution.py:309
  230.8 13.0 %fusion.169 = (bf16[4096]{0:T(1024)(128)(2,1)S(1)}, bf16[600,4096]{1,0:T(8,128)(2,1)S(1)}) fusion(f32[600,4096]{1,0:T(8,128)} %get-tuple-element.98, f32[4096]{0:T(1024)S(1)} %bitcast.533, bf16[4096,1024]{1,0:T(8,128)(2,1)S(1)} %bitcast.437, bf16[600,1024]{1,0:T(8,128)(2,1)S(1)} %copy-done.35, f32[]{:T(128)} %bitcast.98), kind=kOutput, calls=%fused_computation.385 | convolution fusion | flops 5064495104 | bytes 24387588 | tf_op jit(solution)/shard_map/dot_general | solution.py:319
  243.8 10.6 %multiply_reduce_fusion.1 = (bf16[1024]{0:T(1024)(128)(2,1)S(1)}, f32[600]{0:T(1024)S(1)}, f32[600]{0:T(1024)S(1)}, bf16[1024]{0:T(1024)(128)(2,1)S(1)}, f32[600,1024]{1,0:T(8,128)S(1)}) fusion(f32[600,1024]{1,0:T(8,128)S(1)} %get-tuple-element.96, f32[600]{0:T(1024)S(1)} %add_rsqrt_fusion, f32[600]{0:T(1024)S(1)} %broadcast_multiply_fusion.4, ...), kind=kOutput, calls=%fused_computation.130 | convolution fusion | flops 5038691328 | bytes 18236800 | tf_op jit(solution)/shard_map/dot_general | solution.py:324
  261.1 9.8 %convolution_convert_fusion = bf16[1024,4096]{1,0:T(8,128)(2,1)} fusion(bf16[600,4096]{1,0:T(8,128)(2,1)S(1)} %bitcast.552, f32[600,1024]{1,0:T(8,128)S(1)} %get-tuple-element.96, f32[1024]{0:T(1024)S(1)} %bitcast.540, f32[1024]{0:T(1024)S(1)} %bitcast.527, f32[600]{0:T(1024)S(1)} %add_rsqrt_fusion, f32[600]{0:T(1024)S(1)} %broadcast_multiply_fusion.4), kind=kOutput, calls=%fused_computation.38 | convolution fusion | flops 5040431104 | bytes 15774400 | tf_op jit(solution)/shard_map/dot_general | solution.py:322
  273.7 6.6 %fusion.168 = (bf16[16,64]{1,0:T(8,128)(2,1)S(1)}, bf16[12,50,16,64]{3,1,2,0:T(8,128)(2,1)}) fusion(f32[12,16,50,50]{2,3,1,0:T(8,128)} %copy-done, f32[12,16,50]{2,1,0:T(8,128)S(1)} %log_add_fusion, bf16[12,50,16,64]{3,2,1,0:T(8,128)(2,1)} %reshape.2330), kind=kOutput, calls=%fused_computation.384 | convolution fusion | flops 63627776 | bytes 4418048 | tf_op jit(solution)/shard_map/chqk,cqhd->ckhd/dot_general | solution.py:88
  312.4 9.8 %fusion.54 = (bf16[1024]{0:T(1024)(128)(2,1)S(1)}, f32[600]{0:T(1024)S(1)}, f32[600]{0:T(1024)S(1)}, bf16[1024]{0:T(1024)(128)(2,1)S(1)}, f32[600,1024]{1,0:T(8,128)}) fusion(bf16[600,1024]{1,0:T(8,128)(2,1)S(1)} %copy-done.5, f32[600]{0:T(1024)S(1)} %add_rsqrt_fusion.1, f32[600]{0:T(1024)S(1)} %broadcast_multiply_fusion.5, f32[1024]{0:T(1024)S(1)} %bitcast.529, ...), kind=kOutput, calls=%fused_computation.128 | convolution fusion | flops 3781014528 | bytes 13682048 | tf_op jit(solution)/shard_map/dot_general | solution.py:338
  322.3 7.6 %convolution_convert_fusion.2 = bf16[1024,3072]{1,0:T(8,128)(2,1)} fusion(bf16[600,3072]{1,0:T(8,128)(2,1)S(1)} %copy-done.37, bf16[600,1024]{1,0:T(8,128)(2,1)S(1)} %copy-done.5, f32[1024]{0:T(1024)S(1)} %bitcast.538, f32[1024]{0:T(1024)S(1)} %bitcast.530, f32[600]{0:T(1024)S(1)} %add_rsqrt_fusion.1, f32[600]{0:T(1024)S(1)} %broadcast_multiply_fusion.5), kind=kOutput, calls=%fused_computation.57 | convolution fusion | flops 3781705728 | bytes 11219648 | tf_op jit(solution)/shard_map/dot_general | solution.py:335
  329.9 14.1 %concatenate.576 = bf16[4,2,2,2,2,64,1024]{6,5,4,3,2,1,0:T(8,128)(2,1)} reshape(bf16[1024,4096]{1,0:T(8,128)(2,1)} %convolution_convert_fusion) | data formatting | bytes 16777216 | tf_op jit(solution)/shard_map/concatenate | solution.py:363
  352.3 10.1 %convolution_convert_fusion.1 = bf16[4096,1024]{1,0:T(8,128)(2,1)S(1)} fusion(bf16[600,4096]{1,0:T(8,128)(2,1)} %get-tuple-element.97, bf16[600,1024]{1,0:T(8,128)(2,1)S(1)} %copy-done.36, f32[]{:T(128)} %bitcast.98), kind=kOutput, calls=%fused_computation.39 | convolution fusion | flops 5039202304 | bytes 14532612 | tf_op jit(solution)/shard_map/dot_general | solution.py:317
  371.1 8.2 %copy.195 = bf16[4,2,2,1,2,128,1024]{6,5,0,1,4,2,3:T(8,128)(2,1)} copy(bf16[4,2,2,1,2,128,1024]{6,5,4,3,2,1,0:T(8,128)(2,1)} %get-tuple-element.28) | data formatting | bytes 16777216
  381.8 7.0 %collective-permute-done.49 = bf16[4,2,16,1024]{3,2,1,0:T(8,128)(2,1)S(1)} collective-permute-done((bf16[4,2,16,1024]{3,2,1,0:T(8,128)(2,1)S(1)}, bf16[4,2,16,1024]{3,2,1,0:T(8,128)(2,1)S(1)}, u32[]{:S(2)}, u32[]{:S(2)}) %collective-permute-start.49) | collective-permute-done | bytes 262176 | tf_op jit(solution)/shard_map/ppermute | solution.py:133
  396.3 10.1 %add_convert_fusion.1 = bf16[600,1024]{1,0:T(8,128)(2,1)} fusion(f32[600,1024]{1,0:T(8,128)S(1)} %copy-done.15, bf16[600,4096]{1,0:T(8,128)(2,1)} %get-tuple-element.97, bf16[4096,1024]{1,0:T(8,128)(2,1)} %bitcast.438, f32[1024]{0:T(1024)S(1)} %bitcast.536), kind=kOutput, calls=%fused_computation.135 | convolution fusion | flops 5035008000 | bytes 16994304 | tf_op jit(solution)/shard_map/dot_general | solution.py:313
  436.6 8.0 %convert_add_fusion = f32[4,2,2,2,128,1024]{5,4,0,1,3,2:T(8,128)S(1)} fusion(bf16[4,2,2,2,128,1024]{5,4,0,1,3,2:T(8,128)(2,1)} %copy-done.22, bf16[4,2,2,1,2,128,1024]{6,5,4,3,2,1,0:T(8,128)(2,1)} %get-tuple-element.27), kind=kLoop, calls=%fused_computation.12 | loop fusion | flops 12582912 | bytes 33554432 | tf_op jit(solution)/shard_map/add | solution.py:134
  444.6 6.6 %fusion.158 = (f32[4,2,2,1,128,1024]{5,4,0,1,3,2:T(8,128)}, f32[4,2,2,1,128,1024]{5,4,0,1,3,2:T(8,128)}) fusion(f32[4,2,2,2,128,1024]{5,4,0,1,3,2:T(8,128)S(1)} %convert_add_fusion), kind=kLoop, calls=%fused_computation.374 | loop fusion | bytes 33554432 | tf_op jit(solution)/shard_map/slice | solution.py:193
  462.6 39.8 %collective-permute-done.58 = bf16[4,2,128,1024]{3,2,0,1:T(8,128)(2,1)S(1)} collective-permute-done((bf16[4,2,128,1024]{3,2,0,1:T(8,128)(2,1)S(1)}, bf16[4,2,128,1024]{3,2,0,1:T(8,128)(2,1)S(1)}, u32[]{:S(2)}, u32[]{:S(2)}) %collective-permute-start.58) | collective-permute-done | bytes 2097184 | tf_op jit(solution)/shard_map/ppermute | solution.py:133
  516.1 20.0 %collective-permute-done.59 = bf16[4,128,1024]{2,1,0:T(8,128)(2,1)S(1)} collective-permute-done((bf16[4,128,1024]{2,1,0:T(8,128)(2,1)S(1)}, bf16[4,128,1024]{2,1,0:T(8,128)(2,1)S(1)}, u32[]{:S(2)}, u32[]{:S(2)}) %collective-permute-start.59) | collective-permute-done | bytes 1048608 | tf_op jit(solution)/shard_map/ppermute | solution.py:133
  540.5 12.1 %collective-permute-done.62 = bf16[2,128,1024]{2,1,0:T(8,128)(2,1)S(1)} collective-permute-done((bf16[2,128,1024]{2,1,0:T(8,128)(2,1)S(1)}, bf16[2,128,1024]{2,1,0:T(8,128)(2,1)S(1)}, u32[]{:S(2)}, u32[]{:S(2)}) %collective-permute-start.62) | collective-permute-done | bytes 524320 | tf_op jit(solution)/shard_map/ppermute | solution.py:205
  561.0 8.0 %collective-permute-done.63 = bf16[2,128,1024]{2,1,0:T(8,128)(2,1)S(1)} collective-permute-done((bf16[2,128,1024]{2,1,0:T(8,128)(2,1)S(1)}, bf16[2,128,1024]{2,1,0:T(8,128)(2,1)S(1)}, u32[]{:S(2)}, u32[]{:S(2)}) %collective-permute-start.63) | collective-permute-done | bytes 524320 | tf_op jit(solution)/shard_map/ppermute | solution.py:205
  597.7 17.9 %collective-permute-done.66 = bf16[2,2,128,1024]{3,2,1,0:T(8,128)(2,1)S(1)} collective-permute-done((bf16[2,2,128,1024]{3,2,1,0:T(8,128)(2,1)S(1)}, bf16[2,2,128,1024]{3,2,1,0:T(8,128)(2,1)S(1)}, u32[]{:S(2)}, u32[]{:S(2)}) %collective-permute-start.66) | collective-permute-done | bytes 1048608 | tf_op jit(solution)/shard_map/ppermute | solution.py:118
  (456 shorter events, 354.2 us)
Async XLA Ops:
  15.0 26.5 %collective-permute-start.11 = (bf16[2,16,1024]{2,1,0:T(8,128)(2,1)S(1)}, bf16[2,16,1024]{2,1,0:T(8,128)(2,1)S(1)}, u32[]{:S(2)}, u32[]{:S(2)}) collective-permute-start(bf16[2,16,1024]{2,1,0:T(8,128)(2,1)S(1)} %dynamic-slice_bitcast_fusion.4), channel_id=1, source_target_pairs={{0,3},{1,0},{2,1},{3,2},{4,7},{5,4},{6,5},{7,6},{8,11},{9,8},{10,9... | collective-permute-start | bytes 196616 | tf_op jit(solution)/shard_map/ppermute | solution.py:151
  19.1 36.4 %collective-permute-start.3 = (bf16[2,16,3072]{2,1,0:T(8,128)(2,1)S(1)}, bf16[2,16,3072]{2,1,0:T(8,128)(2,1)S(1)}, u32[]{:S(2)}, u32[]{:S(2)}) collective-permute-start(bf16[2,16,3072]{2,1,0:T(8,128)(2,1)S(1)} %dynamic-slice_bitcast_fusion.3), channel_id=1, source_target_pairs={{0,3},{1,0},{2,1},{3,2},{4,7},{5,4},{6,5},{7,6},{8,11},{9,8},{10,9... | collective-permute-start | bytes 589832 | tf_op jit(solution)/shard_map/ppermute | solution.py:151
  21.1 38.6 %collective-permute-start.19 = (bf16[2,16,4096]{2,1,0:T(8,128)(2,1)S(1)}, bf16[2,16,4096]{2,1,0:T(8,128)(2,1)S(1)}, u32[]{:S(2)}, u32[]{:S(2)}) collective-permute-start(bf16[2,16,4096]{2,1,0:T(8,128)(2,1)S(1)} %dynamic-slice_bitcast_fusion.2), channel_id=1, source_target_pairs={{0,3},{1,0},{2,1},{3,2},{4,7},{5,4},{6,5},{7,6},{8,11},{9,8},{10,9... | collective-permute-start | bytes 786440 | tf_op jit(solution)/shard_map/ppermute | solution.py:151
  23.7 36.1 %collective-permute-start.27 = (bf16[2,64,1024]{2,1,0:T(8,128)(2,1)S(1)}, bf16[2,64,1024]{2,1,0:T(8,128)(2,1)S(1)}, u32[]{:S(2)}, u32[]{:S(2)}) collective-permute-start(bf16[2,64,1024]{2,1,0:T(8,128)(2,1)S(1)} %dynamic-slice_bitcast_fusion.1), channel_id=1, source_target_pairs={{0,3},{1,0},{2,1},{3,2},{4,7},{5,4},{6,5},{7,6},{8,11},{9,8},{10,9... | collective-permute-start | bytes 786440 | tf_op jit(solution)/shard_map/ppermute | solution.py:151
  69.5 49.7 %collective-permute-start.18 = (bf16[3,2,2,2,16,1024]{5,4,3,2,1,0:T(8,128)(2,1)S(1)}, bf16[3,2,2,2,16,1024]{5,4,3,2,1,0:T(8,128)(2,1)S(1)}, u32[]{:S(2)}, u32[]{:S(2)}) collective-permute-start(bf16[3,2,2,2,16,1024]{5,4,3,2,1,0:T(8,128)(2,1)S(1)} %get-tuple-element.60), channel_id=1, source_target_pairs={{0,4},{4,0},{8,12},{12,8},{16,20},{20,16},{24,28},{28,24},{1,5},{5... | collective-permute-start | bytes 2359304 | tf_op jit(solution)/shard_map/ppermute | solution.py:118
  101.8 32.2 %collective-permute-start.25 = (bf16[3,2,16,4096]{3,2,1,0:T(8,128)(2,1)S(1)}, bf16[3,2,16,4096]{3,2,1,0:T(8,128)(2,1)S(1)}, u32[]{:S(2)}, u32[]{:S(2)}) collective-permute-start(bf16[3,2,16,4096]{3,2,1,0:T(8,128)(2,1)S(1)} %maximum_select_fusion.20), channel_id=1, source_target_pairs={{0,8},{4,12},{8,0},{12,4},{16,24},{20,28},{24,16},{28,20},{1,9},{5... | collective-permute-start | bytes 2359304 | tf_op jit(solution)/shard_map/ppermute | solution.py:118
  105.5 29.5 %collective-permute-start.23 = (bf16[3,2,16,4096]{3,2,1,0:T(8,128)(2,1)S(1)}, bf16[3,2,16,4096]{3,2,1,0:T(8,128)(2,1)S(1)}, u32[]{:S(2)}, u32[]{:S(2)}) collective-permute-start(bf16[3,2,16,4096]{3,2,1,0:T(8,128)(2,1)S(1)} %maximum_select_fusion.18), channel_id=1, source_target_pairs={{0,16},{4,20},{8,24},{12,28},{16,0},{20,4},{24,8},{28,12},{1,17},{... | collective-permute-start | bytes 2359304 | tf_op jit(solution)/shard_map/ppermute | solution.py:118
  117.1 30.1 %collective-permute-start.33 = (bf16[3,2,64,1024]{3,2,1,0:T(8,128)(2,1)S(1)}, bf16[3,2,64,1024]{3,2,1,0:T(8,128)(2,1)S(1)}, u32[]{:S(2)}, u32[]{:S(2)}) collective-permute-start(bf16[3,2,64,1024]{3,2,1,0:T(8,128)(2,1)S(1)} %maximum_select_fusion.24), channel_id=1, source_target_pairs={{0,8},{4,12},{8,0},{12,4},{16,24},{20,28},{24,16},{28,20},{1,9},{5... | collective-permute-start | bytes 2359304 | tf_op jit(solution)/shard_map/ppermute | solution.py:118
  118.9 34.1 %collective-permute-start.10 = (bf16[3,2,2,2,16,3072]{5,4,3,2,1,0:T(8,128)(2,1)S(1)}, bf16[3,2,2,2,16,3072]{5,4,3,2,1,0:T(8,128)(2,1)S(1)}, u32[]{:S(2)}, u32[]{:S(2)}) collective-permute-start(bf16[3,2,2,2,16,3072]{5,4,3,2,1,0:T(8,128)(2,1)S(1)} %get-tuple-element.41), channel_id=1, source_target_pairs={{0,4},{4,0},{8,12},{12,8},{16,20},{20,16},{24,28},{28,24},{1,5},{5... | collective-permute-start | bytes 7077896 | tf_op jit(solution)/shard_map/ppermute | solution.py:118
  119.1 30.7 %collective-permute-start.31 = (bf16[3,2,64,1024]{3,2,1,0:T(8,128)(2,1)S(1)}, bf16[3,2,64,1024]{3,2,1,0:T(8,128)(2,1)S(1)}, u32[]{:S(2)}, u32[]{:S(2)}) collective-permute-start(bf16[3,2,64,1024]{3,2,1,0:T(8,128)(2,1)S(1)} %maximum_select_fusion.22), channel_id=1, source_target_pairs={{0,16},{4,20},{8,24},{12,28},{16,0},{20,4},{24,8},{28,12},{1,17},{... | collective-permute-start | bytes 2359304 | tf_op jit(solution)/shard_map/ppermute | solution.py:118
  137.0 61.5 %collective-permute-start.26 = (bf16[3,2,2,2,16,4096]{5,4,3,2,1,0:T(8,128)(2,1)}, bf16[3,2,2,2,16,4096]{5,4,3,2,1,0:T(8,128)(2,1)}, u32[]{:S(2)}, u32[]{:S(2)}) collective-permute-start(bf16[3,2,2,2,16,4096]{5,4,3,2,1,0:T(8,128)(2,1)} %get-tuple-element.39), channel_id=1, source_target_pairs={{0,4},{4,0},{8,12},{12,8},{16,20},{20,16},{24,28},{28,24},{1,5},{5... | collective-permute-start | bytes 9437192 | tf_op jit(solution)/shard_map/ppermute | solution.py:118
  152.9 55.3 %collective-permute-start.34 = (bf16[3,2,2,2,64,1024]{5,4,3,2,1,0:T(8,128)(2,1)}, bf16[3,2,2,2,64,1024]{5,4,3,2,1,0:T(8,128)(2,1)}, u32[]{:S(2)}, u32[]{:S(2)}) collective-permute-start(bf16[3,2,2,2,64,1024]{5,4,3,2,1,0:T(8,128)(2,1)} %get-tuple-element.37), channel_id=1, source_target_pairs={{0,4},{4,0},{8,12},{12,8},{16,20},{20,16},{24,28},{28,24},{1,5},{5... | collective-permute-start | bytes 9437192 | tf_op jit(solution)/shard_map/ppermute | solution.py:118
  352.3 73.3 %collective-permute-start.35 = (bf16[4,2,2,2,16,3200]{5,4,3,2,1,0:T(8,128)(2,1)}, bf16[4,2,2,2,16,3200]{5,4,3,2,1,0:T(8,128)(2,1)}, u32[]{:S(2)}, u32[]{:S(2)}) collective-permute-start(bf16[4,2,2,2,16,3200]{5,4,3,2,1,0:T(8,128)(2,1)} %fusion.20), channel_id=1, source_target_pairs={{0,4},{4,0},{8,12},{12,8},{16,20},{20,16},{24,28},{28,24},{1,5},{5... | collective-permute-start | bytes 9830408 | tf_op jit(solution)/shard_map/ppermute | solution.py:133
  379.3 53.9 %collective-permute-start.57 = (bf16[4,2,2,2,128,1024]{5,4,0,1,3,2:T(8,128)(2,1)}, bf16[4,2,2,2,128,1024]{5,4,0,1,3,2:T(8,128)(2,1)S(1)}, u32[]{:S(2)}, u32[]{:S(2)}) collective-permute-start(bf16[4,2,2,2,128,1024]{5,4,0,1,3,2:T(8,128)(2,1)} %bitcast.441), channel_id=1, source_target_pairs={{0,4},{4,0},{8,12},{12,8},{16,20},{20,16},{24,28},{28,24},{1,5},{5... | collective-permute-start | bytes 25165832 | tf_op jit(solution)/shard_map/ppermute | solution.py:133
  425.5 161.2 %collective-permute-start.56 = (bf16[2,2,2,16,1024]{4,3,2,1,0:T(8,128)(2,1)}, bf16[2,2,2,16,1024]{4,3,2,1,0:T(8,128)(2,1)}, u32[]{:S(2)}, u32[]{:S(2)}) collective-permute-start(bf16[2,2,2,16,1024]{4,3,2,1,0:T(8,128)(2,1)} %maximum_select_fusion.35), channel_id=1, source_target_pairs={{0,4},{4,0},{8,12},{12,8},{16,20},{20,16},{24,28},{28,24},{1,5},{5... | collective-permute-start | bytes 786440 | tf_op jit(solution)/shard_map/ppermute | solution.py:118
  429.1 25.7 %collective-permute-start.36 = (bf16[4,2,16,3200]{3,2,0,1:T(8,128)(2,1)S(1)}, bf16[4,2,16,3200]{3,2,0,1:T(8,128)(2,1)S(1)}, u32[]{:S(2)}, u32[]{:S(2)}) collective-permute-start(bf16[4,2,16,3200]{3,2,0,1:T(8,128)(2,1)S(1)} %fusion.101), channel_id=1, source_target_pairs={{0,16},{4,20},{8,24},{12,28},{16,0},{20,4},{24,8},{28,12},{1,17},{... | collective-permute-start | bytes 2457608 | tf_op jit(solution)/shard_map/ppermute | solution.py:133
  431.7 28.1 %collective-permute-start.38 = (bf16[4,2,16,3200]{3,2,1,0:T(8,128)(2,1)}, bf16[4,2,16,3200]{3,2,1,0:T(8,128)(2,1)}, u32[]{:S(2)}, u32[]{:S(2)}) collective-permute-start(bf16[4,2,16,3200]{3,2,1,0:T(8,128)(2,1)} %fusion.100), channel_id=1, source_target_pairs={{0,8},{4,12},{8,0},{12,4},{16,24},{20,28},{24,16},{28,20},{1,9},{5... | collective-permute-start | bytes 2457608 | tf_op jit(solution)/shard_map/ppermute | solution.py:133
  453.9 48.6 %collective-permute-start.58 = (bf16[4,2,128,1024]{3,2,0,1:T(8,128)(2,1)S(1)}, bf16[4,2,128,1024]{3,2,0,1:T(8,128)(2,1)S(1)}, u32[]{:S(2)}, u32[]{:S(2)}) collective-permute-start(bf16[4,2,128,1024]{3,2,0,1:T(8,128)(2,1)S(1)} %fusion.71), channel_id=1, source_target_pairs={{0,16},{4,20},{8,24},{12,28},{16,0},{20,4},{24,8},{28,12},{1,17},{... | collective-permute-start | bytes 6291464 | tf_op jit(solution)/shard_map/ppermute | solution.py:133
  457.6 48.6 %collective-permute-start.60 = (bf16[4,2,128,1024]{3,2,0,1:T(8,128)(2,1)S(1)}, bf16[4,2,128,1024]{3,2,0,1:T(8,128)(2,1)S(1)}, u32[]{:S(2)}, u32[]{:S(2)}) collective-permute-start(bf16[4,2,128,1024]{3,2,0,1:T(8,128)(2,1)S(1)} %fusion.72), channel_id=1, source_target_pairs={{0,8},{4,12},{8,0},{12,4},{16,24},{20,28},{24,16},{28,20},{1,9},{5... | collective-permute-start | bytes 6291464 | tf_op jit(solution)/shard_map/ppermute | solution.py:133
  458.3 56.8 %collective-permute-start.37 = (bf16[4,16,3200]{2,1,0:T(8,128)(2,1)S(1)}, bf16[4,16,3200]{2,1,0:T(8,128)(2,1)}, u32[]{:S(2)}, u32[]{:S(2)}) collective-permute-start(bf16[4,16,3200]{2,1,0:T(8,128)(2,1)S(1)} %fusion.110), channel_id=1, source_target_pairs={{0,8},{4,12},{8,0},{12,4},{16,24},{20,28},{24,16},{28,20},{1,9},{5... | collective-permute-start | bytes 1228808 | tf_op jit(solution)/shard_map/ppermute | solution.py:133
  461.4 78.9 %collective-permute-start.39 = (bf16[4,16,3200]{2,1,0:T(8,128)(2,1)S(1)}, bf16[4,16,3200]{2,1,0:T(8,128)(2,1)S(1)}, u32[]{:S(2)}, u32[]{:S(2)}) collective-permute-start(bf16[4,16,3200]{2,1,0:T(8,128)(2,1)S(1)} %fusion.111), channel_id=1, source_target_pairs={{0,16},{4,20},{8,24},{12,28},{16,0},{20,4},{24,8},{28,12},{1,17},{... | collective-permute-start | bytes 1228808 | tf_op jit(solution)/shard_map/ppermute | solution.py:133
  503.7 32.5 %collective-permute-start.59 = (bf16[4,128,1024]{2,1,0:T(8,128)(2,1)S(1)}, bf16[4,128,1024]{2,1,0:T(8,128)(2,1)S(1)}, u32[]{:S(2)}, u32[]{:S(2)}) collective-permute-start(bf16[4,128,1024]{2,1,0:T(8,128)(2,1)S(1)} %fusion.81), channel_id=1, source_target_pairs={{0,8},{4,12},{8,0},{12,4},{16,24},{20,28},{24,16},{28,20},{1,9},{5... | collective-permute-start | bytes 3145736 | tf_op jit(solution)/shard_map/ppermute | solution.py:133
  507.4 29.0 %collective-permute-start.61 = (bf16[4,128,1024]{2,1,0:T(8,128)(2,1)S(1)}, bf16[4,128,1024]{2,1,0:T(8,128)(2,1)S(1)}, u32[]{:S(2)}, u32[]{:S(2)}) collective-permute-start(bf16[4,128,1024]{2,1,0:T(8,128)(2,1)S(1)} %fusion.82), channel_id=1, source_target_pairs={{0,16},{4,20},{8,24},{12,28},{16,0},{20,4},{24,8},{28,12},{1,17},{... | collective-permute-start | bytes 3145736 | tf_op jit(solution)/shard_map/ppermute | solution.py:133
  596.2 23.8 %collective-permute-start.44 = (bf16[2,2,16,3200]{3,2,1,0:T(8,128)(2,1)S(1)}, bf16[2,2,16,3200]{3,2,1,0:T(8,128)(2,1)S(1)}, u32[]{:S(2)}, u32[]{:S(2)}) collective-permute-start(bf16[2,2,16,3200]{3,2,1,0:T(8,128)(2,1)S(1)} %maximum_select_fusion.31), channel_id=1, source_target_pairs={{0,16},{4,20},{8,24},{12,28},{16,0},{20,4},{24,8},{28,12},{1,17},{... | collective-permute-start | bytes 1228808 | tf_op jit(solution)/shard_map/ppermute | solution.py:118
  (97 other events, 1118.7 us)

commit v4 on v2

--- a/solution.py
+++ b/solution.py
@@ -270,7 +270,17 @@
     vec_local = jnp.concatenate([v.astype(jnp.bfloat16) for v in vectors])
     low = [w.astype(jnp.bfloat16) for w in (qkv_weight, out_weight, up_weight, down_weight)]
     if small:
-        qkv_low, vec_rows = gather_chain(low[0], vec_local, n_dp, n_fsdp)
+        rows = low[0].shape[0] // (2 * n_dp)
+        slot = vec_local.shape[0] // (2 * n_dp)
+        if slot % rows == 0:
+            cols = low[0].shape[1]
+            vec_view = vec_local.reshape(2 * n_dp * rows, slot // rows)
+            vec_view = jnp.pad(vec_view, ((0, 0), (0, -(slot // rows) % 128)))
+            joined, _ = gather_chain(jnp.concatenate([low[0], vec_view], axis=1), None, n_dp, n_fsdp)
+            qkv_low = joined[:, :cols]
+            vec_rows = joined[:, cols : cols + slot // rows].reshape(n_fsdp, -1)
+        else:
+            qkv_low, vec_rows = gather_chain(low[0], vec_local, n_dp, n_fsdp)
         out_low, _ = gather_chain(low[1], None, n_dp, n_fsdp)
         up_low, _ = gather_chain(low[2], None, n_dp, n_fsdp)
         down_low, _ = gather_chain(low[3], None, n_dp, n_fsdp)

time: 587 us -> 590 us (level)
    ppermute x15 -> x12, starting transfers between devices: 34.9 us -> 29.2 us  [gather_chain(): buf = lax.ppermute(buf, 'fsdp', down)]
    ppermute x15 -> x12, waiting for transfers between devices: 19.8 us -> 23.9 us  [gather_chain(): buf = lax.ppermute(buf, 'fsdp', down)]
    unnamed x137 -> x133, local copies, waits for them, and re-layouts: 16.2 us -> 16.3 us
  transfers between devices with their start and end apart: 79 -> 76, of which waited for: 40 -> 40; matrix products, arithmetic and copies ran while one was open for 28% -> 30% of each run, Pallas kernels for 0% -> 0%
where the time goes in v4:
time: 590 us; the launch traced here: 582 us
  waiting for transfers between devices  173 us (29%)
  matrix products  117 us (20%)
  starting transfers between devices  111 us (19%)
  local copies, waits for them, and re-layouts  91.4 us (15%)
  other arithmetic  83.3 us (14%)
  between operations  6.19 us (1%)
    ppermute x32, waiting for transfers between devices, exchange(): got = lax.ppermute(leaves, 'dp', xor_pairs(n_dp, 1 << bit))  76.6 us
    ppermute x20, waiting for transfers between devices, split_bit(): lax.ppermute([v.astype(jnp.bfloat16) for v in send], 'dp', xor_pairs(n_dp...  61.2 us
    ppermute x12, starting transfers between devices, reduce_chain(): got = lax.ppermute(send, 'fsdp', down)  40.4 us
    ppermute x12, starting transfers between devices, gather_chain(): buf = lax.ppermute(buf, 'fsdp', down)  29.2 us
    ppermute x32, starting transfers between devices, exchange(): got = lax.ppermute(leaves, 'dp', xor_pairs(n_dp, 1 << bit))  25.1 us
    ppermute x12, waiting for transfers between devices, gather_chain(): buf = lax.ppermute(buf, 'fsdp', down)  23.9 us
    add x12, other arithmetic, split_bit(): k.astype(jnp.float32) + g.astype(jnp.float32)  19.5 us
    concatenate x4, other arithmetic, gather_chain(): return (jnp.roll(rel, f, axis=0).reshape(n_fsdp * rows, cols), vecs)  17.3 us
  transfers between devices with their start and end apart: 76, of which 40 were waited for; matrix products, arithmetic and copies ran while one was open for 30% of the time, Pallas kernels for 0%

profile of v4, /device:TPU:0, one launch (start us, length us, event | category | flops | bytes accessed | tf_op | source)
XLA Modules:
  0.0 582.2 jit_solution(16293537405106273188)
XLA Ops:
  2.0 5.1 collective-permute-start.8
  27.6 10.5 %collective-permute-done.9 = bf16[2,16,1024]{2,1,0:T(8,128)(2,1)S(1)} collective-permute-done((bf16[2,16,1024]{2,1,0:T(8,128)(2,1)S(1)}, bf16[2,16,1024]{2,1,0:T(8,128)(2,1)S(1)}, u32[]{:S(2)}, u32[]{:S(2)}) %collective-permute-start.9) | collective-permute-done | bytes 65568 | tf_op jit(solution)/shard_map/ppermute | solution.py:151
  86.0 12.6 %collective-permute-done.27 = bf16[3,64,1024]{2,1,0:T(8,128)(2,1)S(1)} collective-permute-done((bf16[3,64,1024]{2,1,0:T(8,128)(2,1)S(1)}, bf16[3,64,1024]{2,1,0:T(8,128)(2,1)S(1)}, u32[]{:S(2)}, u32[]{:S(2)}) %collective-permute-start.27) | collective-permute-done | bytes 393248 | tf_op jit(solution)/shard_map/ppermute | solution.py:118
  103.6 11.7 %collective-permute-done.6 = bf16[3,2,16,3200]{3,2,1,0:T(8,128)(2,1)S(1)} collective-permute-done((bf16[3,2,16,3200]{3,2,1,0:T(8,128)(2,1)S(1)}, bf16[3,2,16,3200]{3,2,1,0:T(8,128)(2,1)S(1)}, u32[]{:S(2)}, u32[]{:S(2)}) %collective-permute-start.6) | collective-permute-done | bytes 614432 | tf_op jit(solution)/shard_map/ppermute | solution.py:118
  120.7 11.4 %collective-permute-done.22 = bf16[3,2,16,4096]{3,2,1,0:T(8,128)(2,1)S(1)} collective-permute-done((bf16[3,2,16,4096]{3,2,1,0:T(8,128)(2,1)S(1)}, bf16[3,2,16,4096]{3,2,1,0:T(8,128)(2,1)S(1)}, u32[]{:S(2)}, u32[]{:S(2)}) %collective-permute-start.22) | collective-permute-done | bytes 786464 | tf_op jit(solution)/shard_map/ppermute | solution.py:118
  134.9 8.4 %collective-permute-done.30 = bf16[3,2,64,1024]{3,2,1,0:T(8,128)(2,1)S(1)} collective-permute-done((bf16[3,2,64,1024]{3,2,1,0:T(8,128)(2,1)S(1)}, bf16[3,2,64,1024]{3,2,1,0:T(8,128)(2,1)S(1)}, u32[]{:S(2)}, u32[]{:S(2)}) %collective-permute-start.30) | collective-permute-done | bytes 786464 | tf_op jit(solution)/shard_map/ppermute | solution.py:118
  157.5 7.5 %add_convert_fusion = bf16[600,3072]{1,0:T(8,128)(2,1)S(1)} fusion(bf16[1024,3200]{1,0:T(8,128)(2,1)} %bitcast.489, f32[3072]{0:T(1024)S(1)} %pad_maximum_fusion.12, bf16[600,1024]{1,0:T(8,128)(2,1)} %param.17, f32[1024]{0:T(1024)S(1)} %bitcast.593, f32[1024]{0:T(1024)S(1)} %bitcast.585, f32[600]{0:T(1024)S(1)} %add_rsqrt_fusion.1, ...), kind=kOutput, calls=%fused_computation.33 | convolution fusion | flops 3782246400 | bytes 11231936 | tf_op jit(solution)/shard_map/dot_general | solution.py:307
  205.0 5.2 fusion.11
  210.2 6.3 %maximum_select_fusion.1 = bf16[3,2,2,2,2,64,1024]{6,5,4,3,2,1,0:T(8,128)(2,1)S(1)} fusion(bf16[3,2,2,1,2,64,1024]{6,5,4,3,2,1,0:T(8,128)(2,1)} %bitcast.95, bf16[3,2,2,1,2,64,1024]{6,5,4,3,2,1,0:T(8,128)(2,1)S(1)} %copy-done.4, pred[]{:T(512)S(6)} %eq.41), kind=kLoop, calls=%fused_computation.39 | loop fusion | flops 9437184 | bytes 12582913 | tf_op jit(solution)/shard_map/jit(_where)/select_n | solution.py:122
  221.8 10.9 %multiply_convert_fusion = (bf16[600,4096]{1,0:T(8,128)(2,1)}, f32[600,4096]{1,0:T(8,128)}) fusion(f32[4096]{0:T(1024)S(1)} %bitcast.589, bf16[1024,4096]{1,0:T(8,128)(2,1)S(1)} %bitcast.484, f32[600,1024]{1,0:T(8,128)S(1)} %get-tuple-element.94, f32[1024]{0:T(1024)S(1)} %bitcast.596, f32[1024]{0:T(1024)S(1)} %bitcast.581, f32[600]{0:T(1024)S(1)} %add_rsqrt_fusion, ...), kind=kOutput, calls=%fused_computation.19 | convolution fusion | flops 5050982400 | bytes 25621184 | tf_op jit(solution)/shard_map/dot_general | solution.py:319
  232.7 12.9 %fusion.199 = (bf16[4096]{0:T(1024)(128)(2,1)S(1)}, bf16[600,4096]{1,0:T(8,128)(2,1)S(1)}) fusion(f32[600,4096]{1,0:T(8,128)} %get-tuple-element.96, f32[4096]{0:T(1024)S(1)} %bitcast.590, bf16[4096,1024]{1,0:T(8,128)(2,1)S(1)} %bitcast.480, bf16[600,1024]{1,0:T(8,128)(2,1)S(1)} %copy-done.35, f32[]{:T(128)} %bitcast.98), kind=kOutput, calls=%fused_computation.433 | convolution fusion | flops 5064495104 | bytes 24387588 | tf_op jit(solution)/shard_map/dot_general | solution.py:329
  245.7 10.6 %multiply_reduce_fusion.1 = (bf16[1024]{0:T(1024)(128)(2,1)S(1)}, f32[600]{0:T(1024)S(1)}, f32[600]{0:T(1024)S(1)}, bf16[1024]{0:T(1024)(128)(2,1)S(1)}, f32[600,1024]{1,0:T(8,128)S(1)}) fusion(f32[600,1024]{1,0:T(8,128)S(1)} %get-tuple-element.94, f32[600]{0:T(1024)S(1)} %add_rsqrt_fusion, f32[600]{0:T(1024)S(1)} %broadcast_multiply_fusion.4, ...), kind=kOutput, calls=%fused_computation.134 | convolution fusion | flops 5038691328 | bytes 18236800 | tf_op jit(solution)/shard_map/dot_general | solution.py:334
  263.0 9.8 %convolution_convert_fusion = bf16[1024,4096]{1,0:T(8,128)(2,1)} fusion(bf16[600,4096]{1,0:T(8,128)(2,1)S(1)} %bitcast.609, f32[600,1024]{1,0:T(8,128)S(1)} %get-tuple-element.94, f32[1024]{0:T(1024)S(1)} %bitcast.597, f32[1024]{0:T(1024)S(1)} %bitcast.584, f32[600]{0:T(1024)S(1)} %add_rsqrt_fusion, f32[600]{0:T(1024)S(1)} %broadcast_multiply_fusion.4), kind=kOutput, calls=%fused_computation.31 | convolution fusion | flops 5040431104 | bytes 15774400 | tf_op jit(solution)/shard_map/dot_general | solution.py:332
  275.5 6.6 %fusion.198 = (bf16[16,64]{1,0:T(8,128)(2,1)S(1)}, bf16[12,50,16,64]{3,1,2,0:T(8,128)(2,1)}) fusion(f32[12,16,50,50]{2,3,1,0:T(8,128)} %copy-done, f32[12,16,50]{2,1,0:T(8,128)S(1)} %log_add_fusion, bf16[12,50,16,64]{3,2,1,0:T(8,128)(2,1)} %reshape.2527), kind=kOutput, calls=%fused_computation.432 | convolution fusion | flops 63627776 | bytes 4418048 | tf_op jit(solution)/shard_map/chqk,cqhd->ckhd/dot_general | solution.py:88
  291.6 12.6 %convolution_convert_fusion.1 = bf16[4096,1024]{1,0:T(8,128)(2,1)} fusion(bf16[600,4096]{1,0:T(8,128)(2,1)} %get-tuple-element.95, bf16[600,1024]{1,0:T(8,128)(2,1)S(1)} %copy-done.36, f32[]{:T(128)} %bitcast.98), kind=kOutput, calls=%fused_computation.32 | convolution fusion | flops 5039202304 | bytes 14532612 | tf_op jit(solution)/shard_map/dot_general | solution.py:327
  304.3 6.4 %add_convert_fusion.1 = bf16[600,1024]{1,0:T(8,128)(2,1)} fusion(f32[600,1024]{1,0:T(8,128)S(1)} %copy-done.14, bf16[600,4096]{1,0:T(8,128)(2,1)S(1)} %bitcast.611, bf16[4096,1024]{1,0:T(8,128)(2,1)S(1)} %bitcast.483, f32[1024]{0:T(1024)S(1)} %bitcast.595), kind=kOutput, calls=%fused_computation.139 | convolution fusion | flops 5035008000 | bytes 16994304 | tf_op jit(solution)/shard_map/dot_general | solution.py:323
  337.9 9.7 %fusion.59 = (bf16[1024]{0:T(1024)(128)(2,1)S(1)}, f32[600]{0:T(1024)S(1)}, f32[600]{0:T(1024)S(1)}, bf16[1024]{0:T(1024)(128)(2,1)S(1)}, f32[600,1024]{1,0:T(8,128)}) fusion(bf16[600,1024]{1,0:T(8,128)(2,1)S(1)} %copy-done.6, f32[600]{0:T(1024)S(1)} %add_rsqrt_fusion.1, f32[600]{0:T(1024)S(1)} %broadcast_multiply_fusion.5, f32[1024]{0:T(1024)S(1)} %bitcast.586, ...), kind=kOutput, calls=%fused_computation.131 | convolution fusion | flops 3781014528 | bytes 13682048 | tf_op jit(solution)/shard_map/dot_general | solution.py:348
  348.4 7.9 %convolution_convert_fusion.2 = bf16[1024,3072]{1,0:T(8,128)(2,1)S(1)} fusion(bf16[600,3072]{1,0:T(8,128)(2,1)} %constant_dynamic-update-slice_fusion, bf16[600,1024]{1,0:T(8,128)(2,1)S(1)} %copy-done.6, f32[1024]{0:T(1024)S(1)} %bitcast.594, f32[1024]{0:T(1024)S(1)} %bitcast.587, f32[600]{0:T(1024)S(1)} %add_rsqrt_fusion.1, ...), kind=kOutput, calls=%fused_computation.42 | convolution fusion | flops 3781705728 | bytes 11219648 | tf_op jit(solution)/shard_map/dot_general | solution.py:345
  414.7 15.1 %collective-permute-done.33 = bf16[4,2,16,3200]{3,2,0,1:T(8,128)(2,1)S(1)} collective-permute-done((bf16[4,2,16,3200]{3,2,0,1:T(8,128)(2,1)S(1)}, bf16[4,2,16,3200]{3,2,0,1:T(8,128)(2,1)S(1)}, u32[]{:S(2)}, u32[]{:S(2)}) %collective-permute-start.33) | collective-permute-done | bytes 819232 | tf_op jit(solution)/shard_map/ppermute | solution.py:133
  453.3 5.6 convert_add_fusion
  484.0 16.6 %collective-permute-done.66 = bf16[4,2,64,1024]{3,2,0,1:T(8,128)(2,1)S(1)} collective-permute-done((bf16[4,2,64,1024]{3,2,0,1:T(8,128)(2,1)S(1)}, bf16[4,2,64,1024]{3,2,0,1:T(8,128)(2,1)S(1)}, u32[]{:S(2)}, u32[]{:S(2)}) %collective-permute-start.66) | collective-permute-done | bytes 1048608 | tf_op jit(solution)/shard_map/ppermute | solution.py:133
  509.2 5.9 %collective-permute-done.56 = bf16[4,16,4096]{2,1,0:T(8,128)(2,1)S(1)} collective-permute-done((bf16[4,16,4096]{2,1,0:T(8,128)(2,1)S(1)}, bf16[4,16,4096]{2,1,0:T(8,128)(2,1)S(1)}, u32[]{:S(2)}, u32[]{:S(2)}) %collective-permute-start.56) | collective-permute-done | bytes 524320 | tf_op jit(solution)/shard_map/ppermute | solution.py:133
  557.4 9.8 %collective-permute-done.63 = bf16[2,2,16,4096]{3,2,1,0:T(8,128)(2,1)S(1)} collective-permute-done((bf16[2,2,16,4096]{3,2,1,0:T(8,128)(2,1)S(1)}, bf16[2,2,16,4096]{3,2,1,0:T(8,128)(2,1)S(1)}, u32[]{:S(2)}, u32[]{:S(2)}) %collective-permute-start.63) | collective-permute-done | bytes 524320 | tf_op jit(solution)/shard_map/ppermute | solution.py:118
  567.6 8.2 %collective-permute-done.74 = bf16[2,2,64,1024]{3,2,1,0:T(8,128)(2,1)S(1)} collective-permute-done((bf16[2,2,64,1024]{3,2,1,0:T(8,128)(2,1)S(1)}, bf16[2,2,64,1024]{3,2,1,0:T(8,128)(2,1)S(1)}, u32[]{:S(2)}, u32[]{:S(2)}) %collective-permute-start.74) | collective-permute-done | bytes 524320 | tf_op jit(solution)/shard_map/ppermute | solution.py:118
  (489 shorter events, 348.9 us)
Async XLA Ops:
  2.0 22.1 %collective-permute-start.8 = (bf16[2,16,1024]{2,1,0:T(8,128)(2,1)S(1)}, bf16[2,16,1024]{2,1,0:T(8,128)(2,1)S(1)}, u32[]{:S(2)}, u32[]{:S(2)}) collective-permute-start(bf16[2,16,1024]{2,1,0:T(8,128)(2,1)S(1)} %dynamic-slice_bitcast_fusion.6), channel_id=1, source_target_pairs={{0,3},{1,0},{2,1},{3,2},{4,7},{5,4},{6,5},{7,6},{8,11},{9,8},{10,9... | collective-permute-start | bytes 196616 | tf_op jit(solution)/shard_map/ppermute | solution.py:151
  18.9 29.9 %collective-permute-start = (bf16[2,16,3200]{2,1,0:T(8,128)(2,1)S(1)}, bf16[2,16,3200]{2,1,0:T(8,128)(2,1)S(1)}, u32[]{:S(2)}, u32[]{:S(2)}) collective-permute-start(bf16[2,16,3200]{2,1,0:T(8,128)(2,1)S(1)} %dynamic-slice_bitcast_fusion.5), channel_id=1, source_target_pairs={{0,3},{1,0},{2,1},{3,2},{4,7},{5,4},{6,5},{7,6},{8,11},{9,8},{10,9... | collective-permute-start | bytes 614408 | tf_op jit(solution)/shard_map/ppermute | solution.py:151
  21.0 31.9 %collective-permute-start.16 = (bf16[2,16,4096]{2,1,0:T(8,128)(2,1)S(1)}, bf16[2,16,4096]{2,1,0:T(8,128)(2,1)S(1)}, u32[]{:S(2)}, u32[]{:S(2)}) collective-permute-start(bf16[2,16,4096]{2,1,0:T(8,128)(2,1)S(1)} %dynamic-slice_bitcast_fusion.4), channel_id=1, source_target_pairs={{0,3},{1,0},{2,1},{3,2},{4,7},{5,4},{6,5},{7,6},{8,11},{9,8},{10,9... | collective-permute-start | bytes 786440 | tf_op jit(solution)/shard_map/ppermute | solution.py:151
  22.2 30.7 %collective-permute-start.24 = (bf16[2,64,1024]{2,1,0:T(8,128)(2,1)S(1)}, bf16[2,64,1024]{2,1,0:T(8,128)(2,1)S(1)}, u32[]{:S(2)}, u32[]{:S(2)}) collective-permute-start(bf16[2,64,1024]{2,1,0:T(8,128)(2,1)S(1)} %dynamic-slice_bitcast_fusion.3), channel_id=1, source_target_pairs={{0,3},{1,0},{2,1},{3,2},{4,7},{5,4},{6,5},{7,6},{8,11},{9,8},{10,9... | collective-permute-start | bytes 786440 | tf_op jit(solution)/shard_map/ppermute | solution.py:151
  62.8 54.5 %collective-permute-start.15 = (bf16[3,2,2,2,16,1024]{5,4,3,2,1,0:T(8,128)(2,1)S(1)}, bf16[3,2,2,2,16,1024]{5,4,3,2,1,0:T(8,128)(2,1)S(1)}, u32[]{:S(2)}, u32[]{:S(2)}) collective-permute-start(bf16[3,2,2,2,16,1024]{5,4,3,2,1,0:T(8,128)(2,1)S(1)} %get-tuple-element.58), channel_id=1, source_target_pairs={{0,4},{4,0},{8,12},{12,8},{16,20},{20,16},{24,28},{28,24},{1,5},{5... | collective-permute-start | bytes 2359304 | tf_op jit(solution)/shard_map/ppermute | solution.py:118
  99.8 32.3 %collective-permute-start.22 = (bf16[3,2,16,4096]{3,2,1,0:T(8,128)(2,1)S(1)}, bf16[3,2,16,4096]{3,2,1,0:T(8,128)(2,1)S(1)}, u32[]{:S(2)}, u32[]{:S(2)}) collective-permute-start(bf16[3,2,16,4096]{3,2,1,0:T(8,128)(2,1)S(1)} %maximum_select_fusion.22), channel_id=1, source_target_pairs={{0,8},{4,12},{8,0},{12,4},{16,24},{20,28},{24,16},{28,20},{1,9},{5... | collective-permute-start | bytes 2359304 | tf_op jit(solution)/shard_map/ppermute | solution.py:118
  101.6 31.2 %collective-permute-start.20 = (bf16[3,2,16,4096]{3,2,1,0:T(8,128)(2,1)S(1)}, bf16[3,2,16,4096]{3,2,1,0:T(8,128)(2,1)S(1)}, u32[]{:S(2)}, u32[]{:S(2)}) collective-permute-start(bf16[3,2,16,4096]{3,2,1,0:T(8,128)(2,1)S(1)} %maximum_select_fusion.20), channel_id=1, source_target_pairs={{0,16},{4,20},{8,24},{12,28},{16,0},{20,4},{24,8},{28,12},{1,17},{... | collective-permute-start | bytes 2359304 | tf_op jit(solution)/shard_map/ppermute | solution.py:118
  115.3 28.0 %collective-permute-start.30 = (bf16[3,2,64,1024]{3,2,1,0:T(8,128)(2,1)S(1)}, bf16[3,2,64,1024]{3,2,1,0:T(8,128)(2,1)S(1)}, u32[]{:S(2)}, u32[]{:S(2)}) collective-permute-start(bf16[3,2,64,1024]{3,2,1,0:T(8,128)(2,1)S(1)} %maximum_select_fusion.26), channel_id=1, source_target_pairs={{0,8},{4,12},{8,0},{12,4},{16,24},{20,28},{24,16},{28,20},{1,9},{5... | collective-permute-start | bytes 2359304 | tf_op jit(solution)/shard_map/ppermute | solution.py:118
  116.7 31.8 %collective-permute-start.7 = (bf16[3,2,2,2,16,3200]{5,4,3,2,1,0:T(8,128)(2,1)S(1)}, bf16[3,2,2,2,16,3200]{5,4,3,2,1,0:T(8,128)(2,1)S(1)}, u32[]{:S(2)}, u32[]{:S(2)}) collective-permute-start(bf16[3,2,2,2,16,3200]{5,4,3,2,1,0:T(8,128)(2,1)S(1)} %get-tuple-element.39), channel_id=1, source_target_pairs={{0,4},{4,0},{8,12},{12,8},{16,20},{20,16},{24,28},{28,24},{1,5},{5... | collective-permute-start | bytes 7372808 | tf_op jit(solution)/shard_map/ppermute | solution.py:118
  117.3 28.1 %collective-permute-start.28 = (bf16[3,2,64,1024]{3,2,1,0:T(8,128)(2,1)S(1)}, bf16[3,2,64,1024]{3,2,1,0:T(8,128)(2,1)S(1)}, u32[]{:S(2)}, u32[]{:S(2)}) collective-permute-start(bf16[3,2,64,1024]{3,2,1,0:T(8,128)(2,1)S(1)} %maximum_select_fusion.24), channel_id=1, source_target_pairs={{0,16},{4,20},{8,24},{12,28},{16,0},{20,4},{24,8},{28,12},{1,17},{... | collective-permute-start | bytes 2359304 | tf_op jit(solution)/shard_map/ppermute | solution.py:118
  134.9 65.6 %collective-permute-start.23 = (bf16[3,2,2,2,16,4096]{5,4,3,2,1,0:T(8,128)(2,1)}, bf16[3,2,2,2,16,4096]{5,4,3,2,1,0:T(8,128)(2,1)}, u32[]{:S(2)}, u32[]{:S(2)}) collective-permute-start(bf16[3,2,2,2,16,4096]{5,4,3,2,1,0:T(8,128)(2,1)} %get-tuple-element.37), channel_id=1, source_target_pairs={{0,4},{4,0},{8,12},{12,8},{16,20},{20,16},{24,28},{28,24},{1,5},{5... | collective-permute-start | bytes 9437192 | tf_op jit(solution)/shard_map/ppermute | solution.py:118
  148.5 61.7 %collective-permute-start.31 = (bf16[3,2,2,2,64,1024]{5,4,3,2,1,0:T(8,128)(2,1)}, bf16[3,2,2,2,64,1024]{5,4,3,2,1,0:T(8,128)(2,1)}, u32[]{:S(2)}, u32[]{:S(2)}) collective-permute-start(bf16[3,2,2,2,64,1024]{5,4,3,2,1,0:T(8,128)(2,1)} %get-tuple-element.35), channel_id=1, source_target_pairs={{0,4},{4,0},{8,12},{12,8},{16,20},{20,16},{24,28},{28,24},{1,5},{5... | collective-permute-start | bytes 9437192 | tf_op jit(solution)/shard_map/ppermute | solution.py:118
  313.1 43.3 %collective-permute-start.43 = (bf16[4,2,2,2,16,1024]{5,4,3,2,1,0:T(8,128)(2,1)}, bf16[4,2,2,2,16,1024]{5,4,3,2,1,0:T(8,128)(2,1)}, u32[]{:S(2)}, u32[]{:S(2)}) collective-permute-start(bf16[4,2,2,2,16,1024]{5,4,3,2,1,0:T(8,128)(2,1)} %dynamic-slice_bitcast_fusion.2), channel_id=1, source_target_pairs={{0,4},{4,0},{8,12},{12,8},{16,20},{20,16},{24,28},{28,24},{1,5},{5... | collective-permute-start | bytes 3145736 | tf_op jit(solution)/shard_map/ppermute | solution.py:133
  360.8 44.6 %collective-permute-start.32 = (bf16[4,2,2,2,16,3200]{5,4,3,2,1,0:T(8,128)(2,1)}, bf16[4,2,2,2,16,3200]{5,4,3,2,1,0:T(8,128)(2,1)}, u32[]{:S(2)}, u32[]{:S(2)}) collective-permute-start(bf16[4,2,2,2,16,3200]{5,4,3,2,1,0:T(8,128)(2,1)} %fusion.24), channel_id=1, source_target_pairs={{0,4},{4,0},{8,12},{12,8},{16,20},{20,16},{24,28},{28,24},{1,5},{5... | collective-permute-start | bytes 9830408 | tf_op jit(solution)/shard_map/ppermute | solution.py:133
  399.3 38.5 %collective-permute-start.54 = (bf16[4,2,2,2,16,4096]{5,4,3,2,1,0:T(8,128)(2,1)S(1)}, bf16[4,2,2,2,16,4096]{5,4,3,2,1,0:T(8,128)(2,1)}, u32[]{:S(2)}, u32[]{:S(2)}) collective-permute-start(bf16[4,2,2,2,16,4096]{5,4,3,2,1,0:T(8,128)(2,1)S(1)} %copy-done.28), channel_id=1, source_target_pairs={{0,4},{4,0},{8,12},{12,8},{16,20},{20,16},{24,28},{28,24},{1,5},{5... | collective-permute-start | bytes 12582920 | tf_op jit(solution)/shard_map/ppermute | solution.py:133
  399.3 54.0 %collective-permute-start.65 = (bf16[4,2,2,2,64,1024]{5,4,3,2,1,0:T(8,128)(2,1)}, bf16[4,2,2,2,64,1024]{5,4,3,2,1,0:T(8,128)(2,1)}, u32[]{:S(2)}, u32[]{:S(2)}) collective-permute-start(bf16[4,2,2,2,64,1024]{5,4,3,2,1,0:T(8,128)(2,1)} %dynamic-slice_bitcast_fusion), channel_id=1, source_target_pairs={{0,4},{4,0},{8,12},{12,8},{16,20},{20,16},{24,28},{28,24},{1,5},{5... | collective-permute-start | bytes 12582920 | tf_op jit(solution)/shard_map/ppermute | solution.py:133
  444.0 36.6 %collective-permute-start.55 = (bf16[4,2,16,4096]{3,2,0,1:T(8,128)(2,1)S(1)}, bf16[4,2,16,4096]{3,2,0,1:T(8,128)(2,1)}, u32[]{:S(2)}, u32[]{:S(2)}) collective-permute-start(bf16[4,2,16,4096]{3,2,0,1:T(8,128)(2,1)S(1)} %fusion.88), channel_id=1, source_target_pairs={{0,16},{4,20},{8,24},{12,28},{16,0},{20,4},{24,8},{28,12},{1,17},{... | collective-permute-start | bytes 3145736 | tf_op jit(solution)/shard_map/ppermute | solution.py:133
  444.7 37.6 %collective-permute-start.57 = (bf16[4,2,16,4096]{3,2,1,0:T(8,128)(2,1)S(1)}, bf16[4,2,16,4096]{3,2,1,0:T(8,128)(2,1)}, u32[]{:S(2)}, u32[]{:S(2)}) collective-permute-start(bf16[4,2,16,4096]{3,2,1,0:T(8,128)(2,1)S(1)} %fusion.86), channel_id=1, source_target_pairs={{0,8},{4,12},{8,0},{12,4},{16,24},{20,28},{24,16},{28,20},{1,9},{5... | collective-permute-start | bytes 3145736 | tf_op jit(solution)/shard_map/ppermute | solution.py:133
  472.6 28.0 %collective-permute-start.66 = (bf16[4,2,64,1024]{3,2,0,1:T(8,128)(2,1)S(1)}, bf16[4,2,64,1024]{3,2,0,1:T(8,128)(2,1)S(1)}, u32[]{:S(2)}, u32[]{:S(2)}) collective-permute-start(bf16[4,2,64,1024]{3,2,0,1:T(8,128)(2,1)S(1)} %fusion.89), channel_id=1, source_target_pairs={{0,16},{4,20},{8,24},{12,28},{16,0},{20,4},{24,8},{28,12},{1,17},{... | collective-permute-start | bytes 3145736 | tf_op jit(solution)/shard_map/ppermute | solution.py:133
  478.3 26.1 %collective-permute-start.68 = (bf16[4,2,64,1024]{3,2,1,0:T(8,128)(2,1)S(1)}, bf16[4,2,64,1024]{3,2,1,0:T(8,128)(2,1)S(1)}, u32[]{:S(2)}, u32[]{:S(2)}) collective-permute-start(bf16[4,2,64,1024]{3,2,1,0:T(8,128)(2,1)S(1)} %fusion.87), channel_id=1, source_target_pairs={{0,8},{4,12},{8,0},{12,4},{16,24},{20,28},{24,16},{28,20},{1,9},{5... | collective-permute-start | bytes 3145736 | tf_op jit(solution)/shard_map/ppermute | solution.py:133
  478.5 30.3 %collective-permute-start.40 = (bf16[2,16,3200]{2,1,0:T(8,128)(2,1)S(1)}, bf16[2,16,3200]{2,1,0:T(8,128)(2,1)S(1)}, u32[]{:S(2)}, u32[]{:S(2)}) collective-permute-start(bf16[2,16,3200]{2,1,0:T(8,128)(2,1)S(1)} %fusion.143), channel_id=1, source_target_pairs={{0,8},{4,12},{8,0},{12,4},{16,24},{20,28},{24,16},{28,20},{1,9},{5... | collective-permute-start | bytes 614408 | tf_op jit(solution)/shard_map/ppermute | solution.py:118
  482.1 32.9 %collective-permute-start.56 = (bf16[4,16,4096]{2,1,0:T(8,128)(2,1)S(1)}, bf16[4,16,4096]{2,1,0:T(8,128)(2,1)S(1)}, u32[]{:S(2)}, u32[]{:S(2)}) collective-permute-start(bf16[4,16,4096]{2,1,0:T(8,128)(2,1)S(1)} %fusion.104), channel_id=1, source_target_pairs={{0,8},{4,12},{8,0},{12,4},{16,24},{20,28},{24,16},{28,20},{1,9},{5... | collective-permute-start | bytes 1572872 | tf_op jit(solution)/shard_map/ppermute | solution.py:133
  483.9 31.2 %collective-permute-start.58 = (bf16[4,16,4096]{2,1,0:T(8,128)(2,1)S(1)}, bf16[4,16,4096]{2,1,0:T(8,128)(2,1)S(1)}, u32[]{:S(2)}, u32[]{:S(2)}) collective-permute-start(bf16[4,16,4096]{2,1,0:T(8,128)(2,1)S(1)} %fusion.105), channel_id=1, source_target_pairs={{0,16},{4,20},{8,24},{12,28},{16,0},{20,4},{24,8},{28,12},{1,17},{... | collective-permute-start | bytes 1572872 | tf_op jit(solution)/shard_map/ppermute | solution.py:133
  526.0 22.4 %collective-permute-start.42 = (bf16[2,2,2,16,3200]{4,3,2,1,0:T(8,128)(2,1)S(1)}, bf16[2,2,2,16,3200]{4,3,2,1,0:T(8,128)(2,1)S(1)}, u32[]{:S(2)}, u32[]{:S(2)}) collective-permute-start(bf16[2,2,2,16,3200]{4,3,2,1,0:T(8,128)(2,1)S(1)} %maximum_select_fusion.18), channel_id=1, source_target_pairs={{0,4},{4,0},{8,12},{12,8},{16,20},{20,16},{24,28},{28,24},{1,5},{5... | collective-permute-start | bytes 2457608 | tf_op jit(solution)/shard_map/ppermute | solution.py:118
  (105 other events, 1080.0 us)

commit v5 on v2

--- a/solution.py
+++ b/solution.py
@@ -144,14 +144,13 @@
     rows, cols = shard.shape
     pieces = shard.reshape(n_dp, 2, rows // (2 * n_dp), cols)
     own = lax.dynamic_index_in_dim(pieces, d, 0, keepdims=False)
-    down = [(i, (i - 1) % n_fsdp) for i in range(n_fsdp)]
     ring, vring = [], []
     buf = [own] + ([vec] if vec is not None else [])
-    for _ in range(1, n_fsdp):
-        buf = lax.ppermute(buf, "fsdp", down)
-        ring.append(buf[0])
+    for step in range(1, n_fsdp):
+        got = lax.ppermute(buf, "fsdp", [(i, (i - step) % n_fsdp) for i in range(n_fsdp)])
+        ring.append(got[0])
         if vec is not None:
-            vring.append(buf[1])
+            vring.append(got[1])
     vecs = None
     if vec is not None:
         vecs = jnp.roll(jnp.stack([vec] + vring, axis=0), f, axis=0)
@@ -196,18 +195,12 @@
             part, hb = split_bit(part, hb, bit, d, n_dp, 1)
         finals.append(part)
     acc = [jnp.stack([finals[0][i], finals[1][i]], axis=1) for i in range(len(grads))]
-    down = [(i, (i - 1) % n_fsdp) for i in range(n_fsdp)]
-    if n_fsdp == 1:
-        send = [a[0].astype(jnp.bfloat16) for a in acc]
-    else:
-        send = [lax.dynamic_index_in_dim(a, (f + 1) % n_fsdp, 0, keepdims=False).astype(jnp.bfloat16) for a in acc]
+    total = [lax.dynamic_index_in_dim(a, f, 0, keepdims=False) for a in acc]
     for step in range(1, n_fsdp):
-        got = lax.ppermute(send, "fsdp", down)
-        chunk = (f + 1 + step) % n_fsdp
-        send = [
-            (g.astype(jnp.float32) + lax.dynamic_index_in_dim(a, chunk, 0, keepdims=False)).astype(jnp.bfloat16)
-            for g, a in zip(got, acc)
-        ]
+        out = [lax.dynamic_index_in_dim(a, (f + step) % n_fsdp, 0, keepdims=False).astype(jnp.bfloat16) for a in acc]
+        got = lax.ppermute(out, "fsdp", [(i, (i + step) % n_fsdp) for i in range(n_fsdp)])
+        total = [t + g.astype(jnp.float32) for t, g in zip(total, got)]
+    send = [t.astype(jnp.bfloat16) for t in total]
     part, hb = send, []
     for bit in chip_bits(n_dp):
         part, hb = exchange(part, hb, bit, d, n_dp)

time: 587 us -> 613 us (1.044)
  starting transfers between devices: 111 us -> 136 us
    ppermute x27, starting transfers between devices: 73.2 us -> 86.9 us  [the longest x12 48.1 us: reduce_chain(): lax.ppermute(out, 'fsdp', [(i, (i + step) % n_fsdp) for i in range(n_fsdp)])]
    ppermute x20, waiting for transfers between devices: 63.5 us -> 55.8 us  [split_bit(): lax.ppermute([v.astype(jnp.bfloat16) for v in send], 'dp', xor_pairs(n_dp...]
  transfers between devices with their start and end apart: 79 -> 79, of which waited for: 40 -> 38; matrix products, arithmetic and copies ran while one was open for 28% -> 21% of each run, Pallas kernels for 0% -> 0%
where the time goes in v5:
time: 613 us; the launch traced here: 601 us
  waiting for transfers between devices  173 us (28%)
  starting transfers between devices  136 us (22%)
  matrix products  112 us (18%)
  local copies, waits for them, and re-layouts  88.8 us (14%)
  other arithmetic  86 us (14%)
  between operations  6.16 us (1%)
    ppermute x32, waiting for transfers between devices, exchange(): got = lax.ppermute(leaves, 'dp', xor_pairs(n_dp, 1 << bit))  83.7 us
    ppermute x20, waiting for transfers between devices, split_bit(): lax.ppermute([v.astype(jnp.bfloat16) for v in send], 'dp', xor_pairs(n_dp...  55.8 us
    ppermute x12, starting transfers between devices, reduce_chain(): lax.ppermute(out, 'fsdp', [(i, (i + step) % n_fsdp) for i in range(n_fsdp)])  48.1 us
    ppermute x15, starting transfers between devices, gather_chain(): lax.ppermute(buf, 'fsdp', [(i, (i - step) % n_fsdp) for i in range(n_fsdp)])  38.8 us
    ppermute x32, starting transfers between devices, exchange(): got = lax.ppermute(leaves, 'dp', xor_pairs(n_dp, 1 << bit))  28.8 us
    ppermute x20, starting transfers between devices, split_bit(): lax.ppermute([v.astype(jnp.bfloat16) for v in send], 'dp', xor_pairs(n_dp...  19.9 us
    add x12, other arithmetic, split_bit(): k.astype(jnp.float32) + g.astype(jnp.float32)  19.5 us
    ppermute x15, waiting for transfers between devices, gather_chain(): lax.ppermute(buf, 'fsdp', [(i, (i - step) % n_fsdp) for i in range(n_fsdp)])  18.2 us
  transfers between devices with their start and end apart: 79, of which 38 were waited for; matrix products, arithmetic and copies ran while one was open for 21% of the time, Pallas kernels for 0%

profile of v5, /device:TPU:0, one launch (start us, length us, event | category | flops | bytes accessed | tf_op | source)
XLA Modules:
  0.0 600.9 jit_solution(10708286542255842579)
XLA Ops:
  62.9 7.1 %collective-permute-start.28 = (bf16[2,64,1024]{2,1,0:T(8,128)(2,1)S(1)}, bf16[2,64,1024]{2,1,0:T(8,128)(2,1)S(1)}, u32[]{:S(2)}, u32[]{:S(2)}) collective-permute-start(bf16[2,64,1024]{2,1,0:T(8,128)(2,1)S(1)} %dynamic-slice_bitcast_fusion.3), channel_id=1, source_target_pairs={{0,2},{1,3},{2,0},{3,1},{4,6},{5,7},{6,4},{7,5},{8,10},{9,11},{10,... | collective-permute-start | bytes 786440 | tf_op jit(solution)/shard_map/ppermute | solution.py:150
  74.2 9.4 %collective-permute-done.20 = bf16[2,16,4096]{2,1,0:T(8,128)(2,1)S(1)} collective-permute-done((bf16[2,16,4096]{2,1,0:T(8,128)(2,1)S(1)}, bf16[2,16,4096]{2,1,0:T(8,128)(2,1)S(1)}, u32[]{:S(2)}, u32[]{:S(2)}) %collective-permute-start.20) | collective-permute-done | bytes 262176 | tf_op jit(solution)/shard_map/ppermute | solution.py:150
  87.5 7.3 %collective-permute-done.28 = bf16[2,64,1024]{2,1,0:T(8,128)(2,1)S(1)} collective-permute-done((bf16[2,64,1024]{2,1,0:T(8,128)(2,1)S(1)}, bf16[2,64,1024]{2,1,0:T(8,128)(2,1)S(1)}, u32[]{:S(2)}, u32[]{:S(2)}) %collective-permute-start.28) | collective-permute-done | bytes 262176 | tf_op jit(solution)/shard_map/ppermute | solution.py:150
  105.1 9.0 %collective-permute-done.30 = bf16[3,64,1024]{2,1,0:T(8,128)(2,1)S(1)} collective-permute-done((bf16[3,64,1024]{2,1,0:T(8,128)(2,1)S(1)}, bf16[3,64,1024]{2,1,0:T(8,128)(2,1)S(1)}, u32[]{:S(2)}, u32[]{:S(2)}) %collective-permute-start.30) | collective-permute-done | bytes 393248 | tf_op jit(solution)/shard_map/ppermute | solution.py:118
  123.8 6.5 %collective-permute-done.9 = bf16[3,2,16,3072]{3,2,1,0:T(8,128)(2,1)S(1)} collective-permute-done((bf16[3,2,16,3072]{3,2,1,0:T(8,128)(2,1)S(1)}, bf16[3,2,16,3072]{3,2,1,0:T(8,128)(2,1)S(1)}, u32[]{:S(2)}, u32[]{:S(2)}) %collective-permute-start.9) | collective-permute-done | bytes 589856 | tf_op jit(solution)/shard_map/ppermute | solution.py:118
  139.6 7.5 %collective-permute-done.25 = bf16[3,2,16,4096]{3,2,1,0:T(8,128)(2,1)S(1)} collective-permute-done((bf16[3,2,16,4096]{3,2,1,0:T(8,128)(2,1)S(1)}, bf16[3,2,16,4096]{3,2,1,0:T(8,128)(2,1)S(1)}, u32[]{:S(2)}, u32[]{:S(2)}) %collective-permute-start.25) | collective-permute-done | bytes 786464 | tf_op jit(solution)/shard_map/ppermute | solution.py:118
  153.1 5.8 collective-permute-done.33
  222.6 6.3 %maximum_select_fusion.1 = bf16[3,2,2,2,2,64,1024]{6,5,4,3,2,1,0:T(8,128)(2,1)S(1)} fusion(bf16[3,2,2,1,2,64,1024]{6,5,4,3,2,1,0:T(8,128)(2,1)} %bitcast.95, bf16[3,2,2,1,2,64,1024]{6,5,4,3,2,1,0:T(8,128)(2,1)S(1)} %copy-done.3, pred[]{:T(512)S(6)} %eq.39), kind=kLoop, calls=%fused_computation.39 | loop fusion | flops 9437184 | bytes 12582913 | tf_op jit(solution)/shard_map/jit(_where)/select_n | solution.py:122
  234.3 11.0 %multiply_convert_fusion = (bf16[600,4096]{1,0:T(8,128)(2,1)}, f32[600,4096]{1,0:T(8,128)}) fusion(f32[4096]{0:T(1024)S(1)} %bitcast.622, bf16[1024,4096]{1,0:T(8,128)(2,1)S(1)} %bitcast.518, f32[600,1024]{1,0:T(8,128)S(1)} %get-tuple-element.106, f32[1024]{0:T(1024)S(1)} %bitcast.629, f32[1024]{0:T(1024)S(1)} %bitcast.614, f32[600]{0:T(1024)S(1)} %add_rsqrt_fusion, ...), kind=kOutput, calls=%fused_computation.19 | convolution fusion | flops 5050982400 | bytes 25621184 | tf_op jit(solution)/shard_map/dot_general | solution.py:302
  245.3 12.9 %fusion.199 = (bf16[4096]{0:T(1024)(128)(2,1)S(1)}, bf16[600,4096]{1,0:T(8,128)(2,1)S(1)}) fusion(f32[600,4096]{1,0:T(8,128)} %get-tuple-element.108, f32[4096]{0:T(1024)S(1)} %bitcast.623, bf16[4096,1024]{1,0:T(8,128)(2,1)S(1)} %bitcast.514, bf16[600,1024]{1,0:T(8,128)(2,1)S(1)} %copy-done.37, f32[]{:T(128)} %bitcast.98), kind=kOutput, calls=%fused_computation.435 | convolution fusion | flops 5064495104 | bytes 24387588 | tf_op jit(solution)/shard_map/dot_general | solution.py:312
  258.3 10.6 %multiply_reduce_fusion.1 = (bf16[1024]{0:T(1024)(128)(2,1)S(1)}, f32[600]{0:T(1024)S(1)}, f32[600]{0:T(1024)S(1)}, bf16[1024]{0:T(1024)(128)(2,1)S(1)}, f32[600,1024]{1,0:T(8,128)S(1)}) fusion(f32[600,1024]{1,0:T(8,128)S(1)} %get-tuple-element.106, f32[600]{0:T(1024)S(1)} %add_rsqrt_fusion, f32[600]{0:T(1024)S(1)} %broadcast_multiply_fusion.4, ...), kind=kOutput, calls=%fused_computation.127 | convolution fusion | flops 5038691328 | bytes 18236800 | tf_op jit(solution)/shard_map/dot_general | solution.py:317
  275.6 9.9 %convolution_convert_fusion = bf16[1024,4096]{1,0:T(8,128)(2,1)} fusion(bf16[600,4096]{1,0:T(8,128)(2,1)S(1)} %bitcast.642, f32[600,1024]{1,0:T(8,128)S(1)} %get-tuple-element.106, f32[1024]{0:T(1024)S(1)} %bitcast.630, f32[1024]{0:T(1024)S(1)} %bitcast.617, f32[600]{0:T(1024)S(1)} %add_rsqrt_fusion, f32[600]{0:T(1024)S(1)} %broadcast_multiply_fusion.4), kind=kOutput, calls=%fused_computation.31 | convolution fusion | flops 5040431104 | bytes 15774400 | tf_op jit(solution)/shard_map/dot_general | solution.py:315
  288.2 6.6 %fusion.198 = (bf16[16,64]{1,0:T(8,128)(2,1)S(1)}, bf16[12,50,16,64]{3,1,2,0:T(8,128)(2,1)}) fusion(f32[12,16,50,50]{2,3,1,0:T(8,128)} %copy-done, f32[12,16,50]{2,1,0:T(8,128)S(1)} %log_add_fusion, bf16[12,50,16,64]{3,2,1,0:T(8,128)(2,1)} %reshape.2527), kind=kOutput, calls=%fused_computation.434 | convolution fusion | flops 63627776 | bytes 4418048 | tf_op jit(solution)/shard_map/chqk,cqhd->ckhd/dot_general | solution.py:88
  327.2 9.8 %fusion.52 = (bf16[1024]{0:T(1024)(128)(2,1)S(1)}, f32[600]{0:T(1024)S(1)}, f32[600]{0:T(1024)S(1)}, bf16[1024]{0:T(1024)(128)(2,1)S(1)}, f32[600,1024]{1,0:T(8,128)}) fusion(bf16[600,1024]{1,0:T(8,128)(2,1)S(1)} %copy-done.6, f32[600]{0:T(1024)S(1)} %add_rsqrt_fusion.1, f32[600]{0:T(1024)S(1)} %broadcast_multiply_fusion.5, f32[1024]{0:T(1024)S(1)} %bitcast.619, ...), kind=kOutput, calls=%fused_computation.125 | convolution fusion | flops 3781014528 | bytes 13682048 | tf_op jit(solution)/shard_map/dot_general | solution.py:331
  337.1 7.5 %convolution_convert_fusion.2 = bf16[1024,3072]{1,0:T(8,128)(2,1)} fusion(bf16[600,3072]{1,0:T(8,128)(2,1)S(1)} %copy-done.39, bf16[600,1024]{1,0:T(8,128)(2,1)S(1)} %copy-done.6, f32[1024]{0:T(1024)S(1)} %bitcast.628, f32[1024]{0:T(1024)S(1)} %bitcast.620, f32[600]{0:T(1024)S(1)} %add_rsqrt_fusion.1, f32[600]{0:T(1024)S(1)} %broadcast_multiply_fusion.5), kind=kOutput, calls=%fused_computation.42 | convolution fusion | flops 3781705728 | bytes 11219648 | tf_op jit(solution)/shard_map/dot_general | solution.py:328
  344.7 9.3 %convolution_convert_fusion.1 = bf16[4096,1024]{1,0:T(8,128)(2,1)} fusion(bf16[600,4096]{1,0:T(8,128)(2,1)S(1)} %bitcast.644, bf16[600,1024]{1,0:T(8,128)(2,1)S(1)} %copy-done.38, f32[]{:T(128)} %bitcast.98), kind=kOutput, calls=%fused_computation.32 | convolution fusion | flops 5039202304 | bytes 14532612 | tf_op jit(solution)/shard_map/dot_general | solution.py:310
  354.0 6.4 %add_convert_fusion.1 = bf16[600,1024]{1,0:T(8,128)(2,1)} fusion(f32[600,1024]{1,0:T(8,128)S(1)} %copy-done.14, bf16[600,4096]{1,0:T(8,128)(2,1)S(1)} %bitcast.644, bf16[4096,1024]{1,0:T(8,128)(2,1)S(1)} %bitcast.517, f32[1024]{0:T(1024)S(1)} %bitcast.626), kind=kOutput, calls=%fused_computation.132 | convolution fusion | flops 5035008000 | bytes 16994304 | tf_op jit(solution)/shard_map/dot_general | solution.py:306
  418.4 14.8 %collective-permute-done.36 = bf16[4,2,16,3200]{3,2,0,1:T(8,128)(2,1)S(1)} collective-permute-done((bf16[4,2,16,3200]{3,2,0,1:T(8,128)(2,1)S(1)}, bf16[4,2,16,3200]{3,2,0,1:T(8,128)(2,1)S(1)}, u32[]{:S(2)}, u32[]{:S(2)}) %collective-permute-start.36) | collective-permute-done | bytes 819232 | tf_op jit(solution)/shard_map/ppermute | solution.py:133
  489.2 15.4 %collective-permute-done.69 = bf16[4,2,64,1024]{3,2,0,1:T(8,128)(2,1)S(1)} collective-permute-done((bf16[4,2,64,1024]{3,2,0,1:T(8,128)(2,1)S(1)}, bf16[4,2,64,1024]{3,2,0,1:T(8,128)(2,1)S(1)}, u32[]{:S(2)}, u32[]{:S(2)}) %collective-permute-start.69) | collective-permute-done | bytes 1048608 | tf_op jit(solution)/shard_map/ppermute | solution.py:133
  517.2 7.4 %collective-permute-done.61 = bf16[4,16,4096]{2,1,0:T(8,128)(2,1)S(1)} collective-permute-done((bf16[4,16,4096]{2,1,0:T(8,128)(2,1)S(1)}, bf16[4,16,4096]{2,1,0:T(8,128)(2,1)S(1)}, u32[]{:S(2)}, u32[]{:S(2)}) %collective-permute-start.61) | collective-permute-done | bytes 524320 | tf_op jit(solution)/shard_map/ppermute | solution.py:133
  538.5 12.0 %collective-permute-start.74 = (bf16[2,64,1024]{2,1,0:T(8,128)(2,1)S(1)}, bf16[2,64,1024]{2,1,0:T(8,128)(2,1)S(1)}, u32[]{:S(2)}, u32[]{:S(2)}) collective-permute-start(bf16[2,64,1024]{2,1,0:T(8,128)(2,1)S(1)} %get-tuple-element.41), channel_id=1, source_target_pairs={{0,2},{1,3},{2,0},{3,1},{4,6},{5,7},{6,4},{7,5},{8,10},{9,11},{10,... | collective-permute-start | bytes 786440 | tf_op jit(solution)/shard_map/ppermute | solution.py:201
  550.5 13.1 %collective-permute-start.75 = (bf16[2,64,1024]{2,1,0:T(8,128)(2,1)S(1)}, bf16[2,64,1024]{2,1,0:T(8,128)(2,1)S(1)}, u32[]{:S(2)}, u32[]{:S(2)}) collective-permute-start(bf16[2,64,1024]{2,1,0:T(8,128)(2,1)S(1)} %get-tuple-element.42), channel_id=1, source_target_pairs={{0,3},{1,0},{2,1},{3,2},{4,7},{5,4},{6,5},{7,6},{8,11},{9,8},{10,9... | collective-permute-start | bytes 786440 | tf_op jit(solution)/shard_map/ppermute | solution.py:201
  576.7 11.6 %collective-permute-done.66 = bf16[2,2,16,4096]{3,2,1,0:T(8,128)(2,1)S(1)} collective-permute-done((bf16[2,2,16,4096]{3,2,1,0:T(8,128)(2,1)S(1)}, bf16[2,2,16,4096]{3,2,1,0:T(8,128)(2,1)S(1)}, u32[]{:S(2)}, u32[]{:S(2)}) %collective-permute-start.66) | collective-permute-done | bytes 524320 | tf_op jit(solution)/shard_map/ppermute | solution.py:118
  588.6 5.9 collective-permute-done.77
  (492 shorter events, 371.7 us)
Async XLA Ops:
  40.2 30.1 %collective-permute-start.21 = (bf16[2,16,4096]{2,1,0:T(8,128)(2,1)S(1)}, bf16[2,16,4096]{2,1,0:T(8,128)(2,1)S(1)}, u32[]{:S(2)}, u32[]{:S(2)}) collective-permute-start(bf16[2,16,4096]{2,1,0:T(8,128)(2,1)S(1)} %dynamic-slice_bitcast_fusion.4), channel_id=1, source_target_pairs={{0,1},{1,2},{2,3},{3,0},{4,5},{5,6},{6,7},{7,4},{8,9},{9,10},{10,1... | collective-permute-start | bytes 786440 | tf_op jit(solution)/shard_map/ppermute | solution.py:150
  50.2 33.4 %collective-permute-start.20 = (bf16[2,16,4096]{2,1,0:T(8,128)(2,1)S(1)}, bf16[2,16,4096]{2,1,0:T(8,128)(2,1)S(1)}, u32[]{:S(2)}, u32[]{:S(2)}) collective-permute-start(bf16[2,16,4096]{2,1,0:T(8,128)(2,1)S(1)} %dynamic-slice_bitcast_fusion.4), channel_id=1, source_target_pairs={{0,2},{1,3},{2,0},{3,1},{4,6},{5,7},{6,4},{7,5},{8,10},{9,11},{10,... | collective-permute-start | bytes 786440 | tf_op jit(solution)/shard_map/ppermute | solution.py:150
  54.9 30.2 %collective-permute-start.19 = (bf16[2,16,4096]{2,1,0:T(8,128)(2,1)S(1)}, bf16[2,16,4096]{2,1,0:T(8,128)(2,1)S(1)}, u32[]{:S(2)}, u32[]{:S(2)}) collective-permute-start(bf16[2,16,4096]{2,1,0:T(8,128)(2,1)S(1)} %dynamic-slice_bitcast_fusion.4), channel_id=1, source_target_pairs={{0,3},{1,0},{2,1},{3,2},{4,7},{5,4},{6,5},{7,6},{8,11},{9,8},{10,9... | collective-permute-start | bytes 786440 | tf_op jit(solution)/shard_map/ppermute | solution.py:150
  62.9 32.0 %collective-permute-start.28 = (bf16[2,64,1024]{2,1,0:T(8,128)(2,1)S(1)}, bf16[2,64,1024]{2,1,0:T(8,128)(2,1)S(1)}, u32[]{:S(2)}, u32[]{:S(2)}) collective-permute-start(bf16[2,64,1024]{2,1,0:T(8,128)(2,1)S(1)} %dynamic-slice_bitcast_fusion.3), channel_id=1, source_target_pairs={{0,2},{1,3},{2,0},{3,1},{4,6},{5,7},{6,4},{7,5},{8,10},{9,11},{10,... | collective-permute-start | bytes 786440 | tf_op jit(solution)/shard_map/ppermute | solution.py:150
  104.7 30.6 %collective-permute-start.18 = (bf16[3,2,2,2,16,1024]{5,4,3,2,1,0:T(8,128)(2,1)S(1)}, bf16[3,2,2,2,16,1024]{5,4,3,2,1,0:T(8,128)(2,1)S(1)}, u32[]{:S(2)}, u32[]{:S(2)}) collective-permute-start(bf16[3,2,2,2,16,1024]{5,4,3,2,1,0:T(8,128)(2,1)S(1)} %get-tuple-element.67), channel_id=1, source_target_pairs={{0,4},{4,0},{8,12},{12,8},{16,20},{20,16},{24,28},{28,24},{1,5},{5... | collective-permute-start | bytes 2359304 | tf_op jit(solution)/shard_map/ppermute | solution.py:118
  116.3 30.8 %collective-permute-start.25 = (bf16[3,2,16,4096]{3,2,1,0:T(8,128)(2,1)S(1)}, bf16[3,2,16,4096]{3,2,1,0:T(8,128)(2,1)S(1)}, u32[]{:S(2)}, u32[]{:S(2)}) collective-permute-start(bf16[3,2,16,4096]{3,2,1,0:T(8,128)(2,1)S(1)} %maximum_select_fusion.22), channel_id=1, source_target_pairs={{0,8},{4,12},{8,0},{12,4},{16,24},{20,28},{24,16},{28,20},{1,9},{5... | collective-permute-start | bytes 2359304 | tf_op jit(solution)/shard_map/ppermute | solution.py:118
  121.6 29.5 %collective-permute-start.23 = (bf16[3,2,16,4096]{3,2,1,0:T(8,128)(2,1)S(1)}, bf16[3,2,16,4096]{3,2,1,0:T(8,128)(2,1)S(1)}, u32[]{:S(2)}, u32[]{:S(2)}) collective-permute-start(bf16[3,2,16,4096]{3,2,1,0:T(8,128)(2,1)S(1)} %maximum_select_fusion.20), channel_id=1, source_target_pairs={{0,16},{4,20},{8,24},{12,28},{16,0},{20,4},{24,8},{28,12},{1,17},{... | collective-permute-start | bytes 2359304 | tf_op jit(solution)/shard_map/ppermute | solution.py:118
  130.3 28.6 %collective-permute-start.33 = (bf16[3,2,64,1024]{3,2,1,0:T(8,128)(2,1)S(1)}, bf16[3,2,64,1024]{3,2,1,0:T(8,128)(2,1)S(1)}, u32[]{:S(2)}, u32[]{:S(2)}) collective-permute-start(bf16[3,2,64,1024]{3,2,1,0:T(8,128)(2,1)S(1)} %maximum_select_fusion.26), channel_id=1, source_target_pairs={{0,8},{4,12},{8,0},{12,4},{16,24},{20,28},{24,16},{28,20},{1,9},{5... | collective-permute-start | bytes 2359304 | tf_op jit(solution)/shard_map/ppermute | solution.py:118
  135.0 32.1 %collective-permute-start.10 = (bf16[3,2,2,2,16,3072]{5,4,3,2,1,0:T(8,128)(2,1)S(1)}, bf16[3,2,2,2,16,3072]{5,4,3,2,1,0:T(8,128)(2,1)S(1)}, u32[]{:S(2)}, u32[]{:S(2)}) collective-permute-start(bf16[3,2,2,2,16,3072]{5,4,3,2,1,0:T(8,128)(2,1)S(1)} %get-tuple-element.39), channel_id=1, source_target_pairs={{0,4},{4,0},{8,12},{12,8},{16,20},{20,16},{24,28},{28,24},{1,5},{5... | collective-permute-start | bytes 7077896 | tf_op jit(solution)/shard_map/ppermute | solution.py:118
  135.3 28.7 %collective-permute-start.31 = (bf16[3,2,64,1024]{3,2,1,0:T(8,128)(2,1)S(1)}, bf16[3,2,64,1024]{3,2,1,0:T(8,128)(2,1)S(1)}, u32[]{:S(2)}, u32[]{:S(2)}) collective-permute-start(bf16[3,2,64,1024]{3,2,1,0:T(8,128)(2,1)S(1)} %maximum_select_fusion.24), channel_id=1, source_target_pairs={{0,16},{4,20},{8,24},{12,28},{16,0},{20,4},{24,8},{28,12},{1,17},{... | collective-permute-start | bytes 2359304 | tf_op jit(solution)/shard_map/ppermute | solution.py:118
  153.1 59.8 %collective-permute-start.26 = (bf16[3,2,2,2,16,4096]{5,4,3,2,1,0:T(8,128)(2,1)}, bf16[3,2,2,2,16,4096]{5,4,3,2,1,0:T(8,128)(2,1)}, u32[]{:S(2)}, u32[]{:S(2)}) collective-permute-start(bf16[3,2,2,2,16,4096]{5,4,3,2,1,0:T(8,128)(2,1)} %get-tuple-element.37), channel_id=1, source_target_pairs={{0,4},{4,0},{8,12},{12,8},{16,20},{20,16},{24,28},{28,24},{1,5},{5... | collective-permute-start | bytes 9437192 | tf_op jit(solution)/shard_map/ppermute | solution.py:118
  167.1 55.5 %collective-permute-start.34 = (bf16[3,2,2,2,64,1024]{5,4,3,2,1,0:T(8,128)(2,1)}, bf16[3,2,2,2,64,1024]{5,4,3,2,1,0:T(8,128)(2,1)}, u32[]{:S(2)}, u32[]{:S(2)}) collective-permute-start(bf16[3,2,2,2,64,1024]{5,4,3,2,1,0:T(8,128)(2,1)} %get-tuple-element.35), channel_id=1, source_target_pairs={{0,4},{4,0},{8,12},{12,8},{16,20},{20,16},{24,28},{28,24},{1,5},{5... | collective-permute-start | bytes 9437192 | tf_op jit(solution)/shard_map/ppermute | solution.py:118
  366.8 41.9 %collective-permute-start.35 = (bf16[4,2,2,2,16,3200]{5,4,3,2,1,0:T(8,128)(2,1)S(1)}, bf16[4,2,2,2,16,3200]{5,4,3,2,1,0:T(8,128)(2,1)}, u32[]{:S(2)}, u32[]{:S(2)}) collective-permute-start(bf16[4,2,2,2,16,3200]{5,4,3,2,1,0:T(8,128)(2,1)S(1)} %fusion.18), channel_id=1, source_target_pairs={{0,4},{4,0},{8,12},{12,8},{16,20},{20,16},{24,28},{28,24},{1,5},{5... | collective-permute-start | bytes 9830408 | tf_op jit(solution)/shard_map/ppermute | solution.py:133
  402.6 37.3 %collective-permute-start.57 = (bf16[4,2,2,2,16,4096]{5,4,3,2,1,0:T(8,128)(2,1)S(1)}, bf16[4,2,2,2,16,4096]{5,4,3,2,1,0:T(8,128)(2,1)}, u32[]{:S(2)}, u32[]{:S(2)}) collective-permute-start(bf16[4,2,2,2,16,4096]{5,4,3,2,1,0:T(8,128)(2,1)S(1)} %dynamic-slice_bitcast_fusion.1), channel_id=1, source_target_pairs={{0,4},{4,0},{8,12},{12,8},{16,20},{20,16},{24,28},{28,24},{1,5},{5... | collective-permute-start | bytes 12582920 | tf_op jit(solution)/shard_map/ppermute | solution.py:133
  402.6 48.0 %collective-permute-start.68 = (bf16[4,2,2,2,64,1024]{5,4,3,2,1,0:T(8,128)(2,1)}, bf16[4,2,2,2,64,1024]{5,4,3,2,1,0:T(8,128)(2,1)}, u32[]{:S(2)}, u32[]{:S(2)}) collective-permute-start(bf16[4,2,2,2,64,1024]{5,4,3,2,1,0:T(8,128)(2,1)} %dynamic-slice_bitcast_fusion), channel_id=1, source_target_pairs={{0,4},{4,0},{8,12},{12,8},{16,20},{20,16},{24,28},{28,24},{1,5},{5... | collective-permute-start | bytes 12582920 | tf_op jit(solution)/shard_map/ppermute | solution.py:133
  447.1 37.1 %collective-permute-start.58 = (bf16[4,2,16,4096]{3,2,0,1:T(8,128)(2,1)}, bf16[4,2,16,4096]{3,2,0,1:T(8,128)(2,1)}, u32[]{:S(2)}, u32[]{:S(2)}) collective-permute-start(bf16[4,2,16,4096]{3,2,0,1:T(8,128)(2,1)} %fusion.80), channel_id=1, source_target_pairs={{0,16},{4,20},{8,24},{12,28},{16,0},{20,4},{24,8},{28,12},{1,17},{... | collective-permute-start | bytes 3145736 | tf_op jit(solution)/shard_map/ppermute | solution.py:133
  449.2 36.9 %collective-permute-start.60 = (bf16[4,2,16,4096]{3,2,1,0:T(8,128)(2,1)}, bf16[4,2,16,4096]{3,2,1,0:T(8,128)(2,1)}, u32[]{:S(2)}, u32[]{:S(2)}) collective-permute-start(bf16[4,2,16,4096]{3,2,1,0:T(8,128)(2,1)} %fusion.78), channel_id=1, source_target_pairs={{0,8},{4,12},{8,0},{12,4},{16,24},{20,28},{24,16},{28,20},{1,9},{5... | collective-permute-start | bytes 3145736 | tf_op jit(solution)/shard_map/ppermute | solution.py:133
  483.5 29.9 %collective-permute-start.44 = (bf16[2,2,16,3200]{3,2,1,0:T(8,128)(2,1)S(1)}, bf16[2,2,16,3200]{3,2,1,0:T(8,128)(2,1)S(1)}, u32[]{:S(2)}, u32[]{:S(2)}) collective-permute-start(bf16[2,2,16,3200]{3,2,1,0:T(8,128)(2,1)S(1)} %maximum_select_fusion.37), channel_id=1, source_target_pairs={{0,16},{4,20},{8,24},{12,28},{16,0},{20,4},{24,8},{28,12},{1,17},{... | collective-permute-start | bytes 1228808 | tf_op jit(solution)/shard_map/ppermute | solution.py:118
  485.7 31.4 %collective-permute-start.59 = (bf16[4,16,4096]{2,1,0:T(8,128)(2,1)S(1)}, bf16[4,16,4096]{2,1,0:T(8,128)(2,1)S(1)}, u32[]{:S(2)}, u32[]{:S(2)}) collective-permute-start(bf16[4,16,4096]{2,1,0:T(8,128)(2,1)S(1)} %fusion.96), channel_id=1, source_target_pairs={{0,8},{4,12},{8,0},{12,4},{16,24},{20,28},{24,16},{28,20},{1,9},{5... | collective-permute-start | bytes 1572872 | tf_op jit(solution)/shard_map/ppermute | solution.py:133
  488.0 36.7 %collective-permute-start.61 = (bf16[4,16,4096]{2,1,0:T(8,128)(2,1)S(1)}, bf16[4,16,4096]{2,1,0:T(8,128)(2,1)S(1)}, u32[]{:S(2)}, u32[]{:S(2)}) collective-permute-start(bf16[4,16,4096]{2,1,0:T(8,128)(2,1)S(1)} %fusion.97), channel_id=1, source_target_pairs={{0,16},{4,20},{8,24},{12,28},{16,0},{20,4},{24,8},{28,12},{1,17},{... | collective-permute-start | bytes 1572872 | tf_op jit(solution)/shard_map/ppermute | solution.py:133
  513.5 55.9 %collective-permute-start.45 = (bf16[2,2,2,16,3200]{4,3,2,1,0:T(8,128)(2,1)S(1)}, bf16[2,2,2,16,3200]{4,3,2,1,0:T(8,128)(2,1)S(1)}, u32[]{:S(2)}, u32[]{:S(2)}) collective-permute-start(bf16[2,2,2,16,3200]{4,3,2,1,0:T(8,128)(2,1)S(1)} %maximum_select_fusion.18), channel_id=1, source_target_pairs={{0,4},{4,0},{8,12},{12,8},{16,20},{20,16},{24,28},{28,24},{1,5},{5... | collective-permute-start | bytes 2457608 | tf_op jit(solution)/shard_map/ppermute | solution.py:118
  530.2 33.4 %collective-permute-start.64 = (bf16[2,16,4096]{2,1,0:T(8,128)(2,1)S(1)}, bf16[2,16,4096]{2,1,0:T(8,128)(2,1)S(1)}, u32[]{:S(2)}, u32[]{:S(2)}) collective-permute-start(bf16[2,16,4096]{2,1,0:T(8,128)(2,1)S(1)} %get-tuple-element.45), channel_id=1, source_target_pairs={{0,3},{1,0},{2,1},{3,2},{4,7},{5,4},{6,5},{7,6},{8,11},{9,8},{10,9... | collective-permute-start | bytes 786440 | tf_op jit(solution)/shard_map/ppermute | solution.py:201
  533.4 31.8 %collective-permute-start.73 = (bf16[2,64,1024]{2,1,0:T(8,128)(2,1)S(1)}, bf16[2,64,1024]{2,1,0:T(8,128)(2,1)S(1)}, u32[]{:S(2)}, u32[]{:S(2)}) collective-permute-start(bf16[2,64,1024]{2,1,0:T(8,128)(2,1)S(1)} %get-tuple-element.40), channel_id=1, source_target_pairs={{0,1},{1,2},{2,3},{3,0},{4,5},{5,6},{6,7},{7,4},{8,9},{9,10},{10,1... | collective-permute-start | bytes 786440 | tf_op jit(solution)/shard_map/ppermute | solution.py:201
  538.5 27.6 %collective-permute-start.74 = (bf16[2,64,1024]{2,1,0:T(8,128)(2,1)S(1)}, bf16[2,64,1024]{2,1,0:T(8,128)(2,1)S(1)}, u32[]{:S(2)}, u32[]{:S(2)}) collective-permute-start(bf16[2,64,1024]{2,1,0:T(8,128)(2,1)S(1)} %get-tuple-element.41), channel_id=1, source_target_pairs={{0,2},{1,3},{2,0},{3,1},{4,6},{5,7},{6,4},{7,5},{8,10},{9,11},{10,... | collective-permute-start | bytes 786440 | tf_op jit(solution)/shard_map/ppermute | solution.py:201
  (110 other events, 1284.7 us)

commit v6 on v5

--- a/solution.py
+++ b/solution.py
@@ -138,16 +138,20 @@
     return list(range(1, n_dp.bit_length() - 1))
 
 
-def gather_chain(shard, vec, n_dp, n_fsdp):
+def gather_chain(shard, vec, n_dp, n_fsdp, direct=False):
     d = lax.axis_index("dp")
     f = lax.axis_index("fsdp")
     rows, cols = shard.shape
     pieces = shard.reshape(n_dp, 2, rows // (2 * n_dp), cols)
     own = lax.dynamic_index_in_dim(pieces, d, 0, keepdims=False)
+    down = [(i, (i - 1) % n_fsdp) for i in range(n_fsdp)]
     ring, vring = [], []
     buf = [own] + ([vec] if vec is not None else [])
     for step in range(1, n_fsdp):
-        got = lax.ppermute(buf, "fsdp", [(i, (i - step) % n_fsdp) for i in range(n_fsdp)])
+        if direct:
+            got = lax.ppermute(buf, "fsdp", [(i, (i - step) % n_fsdp) for i in range(n_fsdp)])
+        else:
+            got = buf = lax.ppermute(buf, "fsdp", down)
         ring.append(got[0])
         if vec is not None:
             vring.append(got[1])
@@ -174,7 +178,7 @@
     return jnp.roll(rel, f, axis=0).reshape(n_fsdp * rows, cols), vecs
 
 
-def reduce_chain(grads, n_dp, n_fsdp):
+def reduce_chain(grads, n_dp, n_fsdp, direct=False):
     d = lax.axis_index("dp")
     f = lax.axis_index("fsdp")
     bits = n_dp.bit_length() - 1
@@ -195,12 +199,26 @@
             part, hb = split_bit(part, hb, bit, d, n_dp, 1)
         finals.append(part)
     acc = [jnp.stack([finals[0][i], finals[1][i]], axis=1) for i in range(len(grads))]
-    total = [lax.dynamic_index_in_dim(a, f, 0, keepdims=False) for a in acc]
-    for step in range(1, n_fsdp):
-        out = [lax.dynamic_index_in_dim(a, (f + step) % n_fsdp, 0, keepdims=False).astype(jnp.bfloat16) for a in acc]
-        got = lax.ppermute(out, "fsdp", [(i, (i + step) % n_fsdp) for i in range(n_fsdp)])
-        total = [t + g.astype(jnp.float32) for t, g in zip(total, got)]
-    send = [t.astype(jnp.bfloat16) for t in total]
+    if direct:
+        total = [lax.dynamic_index_in_dim(a, f, 0, keepdims=False) for a in acc]
+        for step in range(1, n_fsdp):
+            out = [lax.dynamic_index_in_dim(a, (f + step) % n_fsdp, 0, keepdims=False).astype(jnp.bfloat16) for a in acc]
+            got = lax.ppermute(out, "fsdp", [(i, (i + step) % n_fsdp) for i in range(n_fsdp)])
+            total = [t + g.astype(jnp.float32) for t, g in zip(total, got)]
+        send = [t.astype(jnp.bfloat16) for t in total]
+    else:
+        down = [(i, (i - 1) % n_fsdp) for i in range(n_fsdp)]
+        if n_fsdp == 1:
+            send = [a[0].astype(jnp.bfloat16) for a in acc]
+        else:
+            send = [lax.dynamic_index_in_dim(a, (f + 1) % n_fsdp, 0, keepdims=False).astype(jnp.bfloat16) for a in acc]
+        for step in range(1, n_fsdp):
+            got = lax.ppermute(send, "fsdp", down)
+            chunk = (f + 1 + step) % n_fsdp
+            send = [
+                (g.astype(jnp.float32) + lax.dynamic_index_in_dim(a, chunk, 0, keepdims=False)).astype(jnp.bfloat16)
+                for g, a in zip(got, acc)
+            ]
     part, hb = send, []
     for bit in chip_bits(n_dp):
         part, hb = exchange(part, hb, bit, d, n_dp)
@@ -263,7 +281,7 @@
     vec_local = jnp.concatenate([v.astype(jnp.bfloat16) for v in vectors])
     low = [w.astype(jnp.bfloat16) for w in (qkv_weight, out_weight, up_weight, down_weight)]
     if small:
-        qkv_low, vec_rows = gather_chain(low[0], vec_local, n_dp, n_fsdp)
+        qkv_low, vec_rows = gather_chain(low[0], vec_local, n_dp, n_fsdp, True)
         out_low, _ = gather_chain(low[1], None, n_dp, n_fsdp)
         up_low, _ = gather_chain(low[2], None, n_dp, n_fsdp)
         down_low, _ = gather_chain(low[3], None, n_dp, n_fsdp)
@@ -360,7 +378,7 @@
             pad = -(slot // rows) % 128
             vec_view = jnp.pad(vec_view, ((0, 0),) * 4 + ((0, pad),))
             joined = jnp.concatenate([qkv_view, vec_view], axis=-1)
-            (both_shard,) = reduce_chain([joined.reshape(grad_qkv_weight.shape[0], -1)], n_dp, n_fsdp)
+            (both_shard,) = reduce_chain([joined.reshape(grad_qkv_weight.shape[0], -1)], n_dp, n_fsdp, True)
             cols = grad_qkv_weight.shape[1]
             grad_qkv_shard = both_shard[:, :cols]
             vec_flat = both_shard[:, cols : cols + slot // rows].reshape(-1)

time: 613 us -> 585 us (0.954)
  starting transfers between devices: 136 us -> 106 us
    ppermute x12 -> x3, starting transfers between devices: 48.1 us -> 5.14 us  [reduce_chain(): lax.ppermute(out, 'fsdp', [(i, (i + step) % n_fsdp) for i in range(n_fsdp)])]
    ppermute x0 -> x18, starting transfers between devices: none -> 40.6 us  [the longest x9 21.4 us: reduce_chain(): got = lax.ppermute(send, 'fsdp', down)]
    ppermute x0 -> x18, waiting for transfers between devices: none -> 34.6 us  [the longest x9 19.4 us: reduce_chain(): got = lax.ppermute(send, 'fsdp', down)]
    ppermute x15 -> x6, starting transfers between devices: 38.8 us -> 10.9 us  [gather_chain(): lax.ppermute(buf, 'fsdp', [(i, (i - step) % n_fsdp) for i in range(n_fsdp)])]
    ppermute x15 -> x6, waiting for transfers between devices: 18.2 us -> 0.02 us  [gather_chain(): lax.ppermute(buf, 'fsdp', [(i, (i - step) % n_fsdp) for i in range(n_fsdp)])]
    ppermute x32, waiting for transfers between devices: 83.7 us -> 76 us  [exchange(): got = lax.ppermute(leaves, 'dp', xor_pairs(n_dp, 1 << bit))]
    ppermute x12 -> x3, waiting for transfers between devices: 15.2 us -> 7.93 us  [reduce_chain(): lax.ppermute(out, 'fsdp', [(i, (i + step) % n_fsdp) for i in range(n_fsdp)])]
    unnamed x137 -> x151, local copies, waits for them, and re-layouts: 16.1 us -> 16.5 us
  transfers between devices with their start and end apart: 79 -> 79, of which waited for: 38 -> 43; matrix products, arithmetic and copies ran while one was open for 21% -> 29% of each run, Pallas kernels for 0% -> 0%
where the time goes in v6:
time: 585 us; the launch traced here: 577 us
  waiting for transfers between devices  176 us (30%)
  matrix products  115 us (20%)
  starting transfers between devices  106 us (18%)
  local copies, waits for them, and re-layouts  90 us (15%)
  other arithmetic  84.2 us (14%)
  between operations  6.29 us (1%)
    ppermute x32, waiting for transfers between devices, exchange(): got = lax.ppermute(leaves, 'dp', xor_pairs(n_dp, 1 << bit))  76 us
    ppermute x20, waiting for transfers between devices, split_bit(): lax.ppermute([v.astype(jnp.bfloat16) for v in send], 'dp', xor_pairs(n_dp...  57.9 us
    ppermute x32, starting transfers between devices, exchange(): got = lax.ppermute(leaves, 'dp', xor_pairs(n_dp, 1 << bit))  28.1 us
    ppermute x9, starting transfers between devices, reduce_chain(): got = lax.ppermute(send, 'fsdp', down)  21.4 us
    ppermute x20, starting transfers between devices, split_bit(): lax.ppermute([v.astype(jnp.bfloat16) for v in send], 'dp', xor_pairs(n_dp...  21 us
    ppermute x9, waiting for transfers between devices, reduce_chain(): got = lax.ppermute(send, 'fsdp', down)  19.4 us
    add x12, other arithmetic, split_bit(): k.astype(jnp.float32) + g.astype(jnp.float32)  19.3 us
    ppermute x9, starting transfers between devices, gather_chain(): got = buf = lax.ppermute(buf, 'fsdp', down)  19.1 us
  transfers between devices with their start and end apart: 79, of which 43 were waited for; matrix products, arithmetic and copies ran while one was open for 29% of the time, Pallas kernels for 0%

profile of v6, /device:TPU:0, one launch (start us, length us, event | category | flops | bytes accessed | tf_op | source)
XLA Modules:
  0.0 577.4 jit_solution(5973636070694844075)
XLA Ops:
  91.3 7.3 %collective-permute-done.24 = bf16[3,16,4096]{2,1,0:T(8,128)(2,1)S(1)} collective-permute-done((bf16[3,16,4096]{2,1,0:T(8,128)(2,1)S(1)}, bf16[3,16,4096]{2,1,0:T(8,128)(2,1)S(1)}, u32[]{:S(2)}, u32[]{:S(2)}) %collective-permute-start.24) | collective-permute-done | bytes 393248 | tf_op jit(solution)/shard_map/ppermute | solution.py:118
  112.4 7.7 %collective-permute-done.25 = bf16[3,2,16,4096]{3,2,1,0:T(8,128)(2,1)S(1)} collective-permute-done((bf16[3,2,16,4096]{3,2,1,0:T(8,128)(2,1)S(1)}, bf16[3,2,16,4096]{3,2,1,0:T(8,128)(2,1)S(1)}, u32[]{:S(2)}, u32[]{:S(2)}) %collective-permute-start.25) | collective-permute-done | bytes 786464 | tf_op jit(solution)/shard_map/ppermute | solution.py:118
  127.2 9.1 %collective-permute-done.33 = bf16[3,2,64,1024]{3,2,1,0:T(8,128)(2,1)S(1)} collective-permute-done((bf16[3,2,64,1024]{3,2,1,0:T(8,128)(2,1)S(1)}, bf16[3,2,64,1024]{3,2,1,0:T(8,128)(2,1)S(1)}, u32[]{:S(2)}, u32[]{:S(2)}) %collective-permute-start.33) | collective-permute-done | bytes 786464 | tf_op jit(solution)/shard_map/ppermute | solution.py:118
  192.1 5.2 fusion.11
  197.3 6.3 %maximum_select_fusion.1 = bf16[3,2,2,2,2,64,1024]{6,5,4,3,2,1,0:T(8,128)(2,1)S(1)} fusion(bf16[3,2,2,1,2,64,1024]{6,5,4,3,2,1,0:T(8,128)(2,1)} %bitcast.95, bf16[3,2,2,1,2,64,1024]{6,5,4,3,2,1,0:T(8,128)(2,1)S(1)} %copy-done.7, pred[]{:T(512)S(6)} %eq.42), kind=kLoop, calls=%fused_computation.39 | loop fusion | flops 9437184 | bytes 12582913 | tf_op jit(solution)/shard_map/jit(_where)/select_n | solution.py:122
  209.0 10.9 %multiply_convert_fusion = (bf16[600,4096]{1,0:T(8,128)(2,1)}, f32[600,4096]{1,0:T(8,128)}) fusion(f32[4096]{0:T(1024)S(1)} %bitcast.598, bf16[1024,4096]{1,0:T(8,128)(2,1)S(1)} %bitcast.494, f32[600,1024]{1,0:T(8,128)S(1)} %get-tuple-element.97, f32[1024]{0:T(1024)S(1)} %bitcast.605, f32[1024]{0:T(1024)S(1)} %bitcast.590, f32[600]{0:T(1024)S(1)} %add_rsqrt_fusion, ...), kind=kOutput, calls=%fused_computation.19 | convolution fusion | flops 5050982400 | bytes 25621184 | tf_op jit(solution)/shard_map/dot_general | solution.py:320
  219.9 13.0 %fusion.193 = (bf16[4096]{0:T(1024)(128)(2,1)S(1)}, bf16[600,4096]{1,0:T(8,128)(2,1)S(1)}) fusion(f32[600,4096]{1,0:T(8,128)} %get-tuple-element.99, f32[4096]{0:T(1024)S(1)} %bitcast.599, bf16[4096,1024]{1,0:T(8,128)(2,1)S(1)} %bitcast.490, bf16[600,1024]{1,0:T(8,128)(2,1)S(1)} %copy-done.43, f32[]{:T(128)} %bitcast.98), kind=kOutput, calls=%fused_computation.429 | convolution fusion | flops 5064495104 | bytes 24387588 | tf_op jit(solution)/shard_map/dot_general | solution.py:330
  232.9 10.3 %multiply_reduce_fusion.1 = (bf16[1024]{0:T(1024)(128)(2,1)S(1)}, f32[600]{0:T(1024)S(1)}, f32[600]{0:T(1024)S(1)}, bf16[1024]{0:T(1024)(128)(2,1)S(1)}, f32[600,1024]{1,0:T(8,128)S(1)}) fusion(f32[600,1024]{1,0:T(8,128)S(1)} %get-tuple-element.97, f32[600]{0:T(1024)S(1)} %add_rsqrt_fusion, f32[600]{0:T(1024)S(1)} %broadcast_multiply_fusion.4, ...), kind=kOutput, calls=%fused_computation.127 | convolution fusion | flops 5038691328 | bytes 18236800 | tf_op jit(solution)/shard_map/dot_general | solution.py:335
  249.9 9.8 %convolution_convert_fusion = bf16[1024,4096]{1,0:T(8,128)(2,1)} fusion(bf16[600,4096]{1,0:T(8,128)(2,1)S(1)} %bitcast.618, f32[600,1024]{1,0:T(8,128)S(1)} %get-tuple-element.97, f32[1024]{0:T(1024)S(1)} %bitcast.606, f32[1024]{0:T(1024)S(1)} %bitcast.593, f32[600]{0:T(1024)S(1)} %add_rsqrt_fusion, f32[600]{0:T(1024)S(1)} %broadcast_multiply_fusion.4), kind=kOutput, calls=%fused_computation.31 | convolution fusion | flops 5040431104 | bytes 15774400 | tf_op jit(solution)/shard_map/dot_general | solution.py:333
  262.5 6.6 %fusion.192 = (bf16[16,64]{1,0:T(8,128)(2,1)S(1)}, bf16[12,50,16,64]{3,1,2,0:T(8,128)(2,1)}) fusion(f32[12,16,50,50]{2,3,1,0:T(8,128)} %copy-done, f32[12,16,50]{2,1,0:T(8,128)S(1)} %log_add_fusion, bf16[12,50,16,64]{3,2,1,0:T(8,128)(2,1)} %reshape.2521), kind=kOutput, calls=%fused_computation.428 | convolution fusion | flops 63627776 | bytes 4418048 | tf_op jit(solution)/shard_map/chqk,cqhd->ckhd/dot_general | solution.py:88
  278.6 12.7 %convolution_convert_fusion.1 = bf16[4096,1024]{1,0:T(8,128)(2,1)} fusion(bf16[600,4096]{1,0:T(8,128)(2,1)} %get-tuple-element.98, bf16[600,1024]{1,0:T(8,128)(2,1)S(1)} %copy-done.44, f32[]{:T(128)} %bitcast.98), kind=kOutput, calls=%fused_computation.32 | convolution fusion | flops 5039202304 | bytes 14532612 | tf_op jit(solution)/shard_map/dot_general | solution.py:328
  291.3 6.4 %add_convert_fusion.1 = bf16[600,1024]{1,0:T(8,128)(2,1)} fusion(f32[600,1024]{1,0:T(8,128)S(1)} %copy-done.18, bf16[600,4096]{1,0:T(8,128)(2,1)S(1)} %bitcast.620, bf16[4096,1024]{1,0:T(8,128)(2,1)S(1)} %bitcast.493, f32[1024]{0:T(1024)S(1)} %bitcast.604), kind=kOutput, calls=%fused_computation.132 | convolution fusion | flops 5035008000 | bytes 16994304 | tf_op jit(solution)/shard_map/dot_general | solution.py:324
  324.9 9.7 %fusion.52 = (bf16[1024]{0:T(1024)(128)(2,1)S(1)}, f32[600]{0:T(1024)S(1)}, f32[600]{0:T(1024)S(1)}, bf16[1024]{0:T(1024)(128)(2,1)S(1)}, f32[600,1024]{1,0:T(8,128)}) fusion(bf16[600,1024]{1,0:T(8,128)(2,1)S(1)} %copy-done.10, f32[600]{0:T(1024)S(1)} %add_rsqrt_fusion.1, f32[600]{0:T(1024)S(1)} %broadcast_multiply_fusion.5, f32[1024]{0:T(1024)S(1)} %bitcast.595, ...), kind=kOutput, calls=%fused_computation.125 | convolution fusion | flops 3781014528 | bytes 13682048 | tf_op jit(solution)/shard_map/dot_general | solution.py:349
  335.4 7.9 %convolution_convert_fusion.2 = bf16[1024,3072]{1,0:T(8,128)(2,1)S(1)} fusion(bf16[600,3072]{1,0:T(8,128)(2,1)} %constant_dynamic-update-slice_fusion, bf16[600,1024]{1,0:T(8,128)(2,1)S(1)} %copy-done.10, f32[1024]{0:T(1024)S(1)} %bitcast.603, f32[1024]{0:T(1024)S(1)} %bitcast.596, f32[600]{0:T(1024)S(1)} %add_rsqrt_fusion.1, ...), kind=kOutput, calls=%fused_computation.42 | convolution fusion | flops 3781705728 | bytes 11219648 | tf_op jit(solution)/shard_map/dot_general | solution.py:346
  347.9 5.6 collective-permute-done.47
  395.6 14.4 %collective-permute-done.36 = bf16[4,2,16,3200]{3,2,0,1:T(8,128)(2,1)S(1)} collective-permute-done((bf16[4,2,16,3200]{3,2,0,1:T(8,128)(2,1)S(1)}, bf16[4,2,16,3200]{3,2,0,1:T(8,128)(2,1)S(1)}, u32[]{:S(2)}, u32[]{:S(2)}) %collective-permute-start.36) | collective-permute-done | bytes 819232 | tf_op jit(solution)/shard_map/ppermute | solution.py:133
  427.4 5.6 convert_add_fusion
  446.2 6.0 %collective-permute-done.41 = bf16[2,16,3200]{2,1,0:T(8,128)(2,1)} collective-permute-done((bf16[2,16,3200]{2,1,0:T(8,128)(2,1)S(1)}, bf16[2,16,3200]{2,1,0:T(8,128)(2,1)}, u32[]{:S(2)}, u32[]{:S(2)}) %collective-permute-start.41) | collective-permute-done | bytes 204832 | tf_op jit(solution)/shard_map/ppermute | solution.py:206
  468.7 14.3 %collective-permute-done.69 = bf16[4,2,64,1024]{3,2,0,1:T(8,128)(2,1)S(1)} collective-permute-done((bf16[4,2,64,1024]{3,2,0,1:T(8,128)(2,1)S(1)}, bf16[4,2,64,1024]{3,2,0,1:T(8,128)(2,1)S(1)}, u32[]{:S(2)}, u32[]{:S(2)}) %collective-permute-start.69) | collective-permute-done | bytes 1048608 | tf_op jit(solution)/shard_map/ppermute | solution.py:133
  485.8 6.0 %collective-permute-done.44 = bf16[2,2,16,3200]{3,2,1,0:T(8,128)(2,1)S(1)} collective-permute-done((bf16[2,2,16,3200]{3,2,1,0:T(8,128)(2,1)S(1)}, bf16[2,2,16,3200]{3,2,1,0:T(8,128)(2,1)S(1)}, u32[]{:S(2)}, u32[]{:S(2)}) %collective-permute-start.44) | collective-permute-done | bytes 409632 | tf_op jit(solution)/shard_map/ppermute | solution.py:118
  495.3 7.8 %collective-permute-done.61 = bf16[4,16,4096]{2,1,0:T(8,128)(2,1)S(1)} collective-permute-done((bf16[4,16,4096]{2,1,0:T(8,128)(2,1)S(1)}, bf16[4,16,4096]{2,1,0:T(8,128)(2,1)S(1)}, u32[]{:S(2)}, u32[]{:S(2)}) %collective-permute-start.61) | collective-permute-done | bytes 524320 | tf_op jit(solution)/shard_map/ppermute | solution.py:133
  518.8 6.6 %collective-permute-done.73 = bf16[2,64,1024]{2,1,0:T(8,128)(2,1)S(1)} collective-permute-done((bf16[2,64,1024]{2,1,0:T(8,128)(2,1)S(1)}, bf16[2,64,1024]{2,1,0:T(8,128)(2,1)S(1)}, u32[]{:S(2)}, u32[]{:S(2)}) %collective-permute-start.73) | collective-permute-done | bytes 262176 | tf_op jit(solution)/shard_map/ppermute | solution.py:216
  555.4 8.4 %collective-permute-done.66 = bf16[2,2,16,4096]{3,2,1,0:T(8,128)(2,1)S(1)} collective-permute-done((bf16[2,2,16,4096]{3,2,1,0:T(8,128)(2,1)S(1)}, bf16[2,2,16,4096]{3,2,1,0:T(8,128)(2,1)S(1)}, u32[]{:S(2)}, u32[]{:S(2)}) %collective-permute-start.66) | collective-permute-done | bytes 524320 | tf_op jit(solution)/shard_map/ppermute | solution.py:118
  564.2 6.7 %collective-permute-done.77 = bf16[2,2,64,1024]{3,2,1,0:T(8,128)(2,1)S(1)} collective-permute-done((bf16[2,2,64,1024]{3,2,1,0:T(8,128)(2,1)S(1)}, bf16[2,2,64,1024]{3,2,1,0:T(8,128)(2,1)S(1)}, u32[]{:S(2)}, u32[]{:S(2)}) %collective-permute-start.77) | collective-permute-done | bytes 524320 | tf_op jit(solution)/shard_map/ppermute | solution.py:118
  (512 shorter events, 367.0 us)
Async XLA Ops:
  17.9 38.3 %collective-permute-start.5 = (bf16[2,16,3072]{2,1,0:T(8,128)(2,1)S(1)}, bf16[2,16,3072]{2,1,0:T(8,128)(2,1)S(1)}, u32[]{:S(2)}, u32[]{:S(2)}) collective-permute-start(bf16[2,16,3072]{2,1,0:T(8,128)(2,1)S(1)} %dynamic-slice_bitcast_fusion.5), channel_id=1, source_target_pairs={{0,1},{1,2},{2,3},{3,0},{4,5},{5,6},{6,7},{7,4},{8,9},{9,10},{10,1... | collective-permute-start | bytes 589832 | tf_op jit(solution)/shard_map/ppermute | solution.py:152
  18.6 39.1 %collective-permute-start.4 = (bf16[2,16,3072]{2,1,0:T(8,128)(2,1)S(1)}, bf16[2,16,3072]{2,1,0:T(8,128)(2,1)S(1)}, u32[]{:S(2)}, u32[]{:S(2)}) collective-permute-start(bf16[2,16,3072]{2,1,0:T(8,128)(2,1)S(1)} %dynamic-slice_bitcast_fusion.5), channel_id=1, source_target_pairs={{0,2},{1,3},{2,0},{3,1},{4,6},{5,7},{6,4},{7,5},{8,10},{9,11},{10,... | collective-permute-start | bytes 589832 | tf_op jit(solution)/shard_map/ppermute | solution.py:152
  29.8 29.4 %collective-permute-start.3 = (bf16[2,16,3072]{2,1,0:T(8,128)(2,1)S(1)}, bf16[2,16,3072]{2,1,0:T(8,128)(2,1)S(1)}, u32[]{:S(2)}, u32[]{:S(2)}) collective-permute-start(bf16[2,16,3072]{2,1,0:T(8,128)(2,1)S(1)} %dynamic-slice_bitcast_fusion.5), channel_id=1, source_target_pairs={{0,3},{1,0},{2,1},{3,2},{4,7},{5,4},{6,5},{7,6},{8,11},{9,8},{10,9... | collective-permute-start | bytes 589832 | tf_op jit(solution)/shard_map/ppermute | solution.py:152
  34.0 31.6 %collective-permute-start.19 = (bf16[2,16,4096]{2,1,0:T(8,128)(2,1)S(1)}, bf16[2,16,4096]{2,1,0:T(8,128)(2,1)S(1)}, u32[]{:S(2)}, u32[]{:S(2)}) collective-permute-start(bf16[2,16,4096]{2,1,0:T(8,128)(2,1)S(1)} %dynamic-slice_bitcast_fusion.4), channel_id=1, source_target_pairs={{0,3},{1,0},{2,1},{3,2},{4,7},{5,4},{6,5},{7,6},{8,11},{9,8},{10,9... | collective-permute-start | bytes 786440 | tf_op jit(solution)/shard_map/ppermute | solution.py:154
  69.8 38.0 %collective-permute-start.18 = (bf16[3,2,2,2,16,1024]{5,4,3,2,1,0:T(8,128)(2,1)S(1)}, bf16[3,2,2,2,16,1024]{5,4,3,2,1,0:T(8,128)(2,1)S(1)}, u32[]{:S(2)}, u32[]{:S(2)}) collective-permute-start(bf16[3,2,2,2,16,1024]{5,4,3,2,1,0:T(8,128)(2,1)S(1)} %get-tuple-element.61), channel_id=1, source_target_pairs={{0,4},{4,0},{8,12},{12,8},{16,20},{20,16},{24,28},{28,24},{1,5},{5... | collective-permute-start | bytes 2359304 | tf_op jit(solution)/shard_map/ppermute | solution.py:118
  98.6 43.4 %collective-permute-start.10 = (bf16[3,2,2,2,16,3072]{5,4,3,2,1,0:T(8,128)(2,1)S(1)}, bf16[3,2,2,2,16,3072]{5,4,3,2,1,0:T(8,128)(2,1)S(1)}, u32[]{:S(2)}, u32[]{:S(2)}) collective-permute-start(bf16[3,2,2,2,16,3072]{5,4,3,2,1,0:T(8,128)(2,1)S(1)} %get-tuple-element.39), channel_id=1, source_target_pairs={{0,4},{4,0},{8,12},{12,8},{16,20},{20,16},{24,28},{28,24},{1,5},{5... | collective-permute-start | bytes 7077896 | tf_op jit(solution)/shard_map/ppermute | solution.py:118
  105.4 30.9 %collective-permute-start.33 = (bf16[3,2,64,1024]{3,2,1,0:T(8,128)(2,1)S(1)}, bf16[3,2,64,1024]{3,2,1,0:T(8,128)(2,1)S(1)}, u32[]{:S(2)}, u32[]{:S(2)}) collective-permute-start(bf16[3,2,64,1024]{3,2,1,0:T(8,128)(2,1)S(1)} %maximum_select_fusion.26), channel_id=1, source_target_pairs={{0,8},{4,12},{8,0},{12,4},{16,24},{20,28},{24,16},{28,20},{1,9},{5... | collective-permute-start | bytes 2359304 | tf_op jit(solution)/shard_map/ppermute | solution.py:118
  107.9 31.0 %collective-permute-start.31 = (bf16[3,2,64,1024]{3,2,1,0:T(8,128)(2,1)S(1)}, bf16[3,2,64,1024]{3,2,1,0:T(8,128)(2,1)S(1)}, u32[]{:S(2)}, u32[]{:S(2)}) collective-permute-start(bf16[3,2,64,1024]{3,2,1,0:T(8,128)(2,1)S(1)} %maximum_select_fusion.24), channel_id=1, source_target_pairs={{0,16},{4,20},{8,24},{12,28},{16,0},{20,4},{24,8},{28,12},{1,17},{... | collective-permute-start | bytes 2359304 | tf_op jit(solution)/shard_map/ppermute | solution.py:118
  127.2 60.5 %collective-permute-start.26 = (bf16[3,2,2,2,16,4096]{5,4,3,2,1,0:T(8,128)(2,1)}, bf16[3,2,2,2,16,4096]{5,4,3,2,1,0:T(8,128)(2,1)}, u32[]{:S(2)}, u32[]{:S(2)}) collective-permute-start(bf16[3,2,2,2,16,4096]{5,4,3,2,1,0:T(8,128)(2,1)} %get-tuple-element.37), channel_id=1, source_target_pairs={{0,4},{4,0},{8,12},{12,8},{16,20},{20,16},{24,28},{28,24},{1,5},{5... | collective-permute-start | bytes 9437192 | tf_op jit(solution)/shard_map/ppermute | solution.py:118
  142.0 55.3 %collective-permute-start.34 = (bf16[3,2,2,2,64,1024]{5,4,3,2,1,0:T(8,128)(2,1)}, bf16[3,2,2,2,64,1024]{5,4,3,2,1,0:T(8,128)(2,1)}, u32[]{:S(2)}, u32[]{:S(2)}) collective-permute-start(bf16[3,2,2,2,64,1024]{5,4,3,2,1,0:T(8,128)(2,1)} %get-tuple-element.35), channel_id=1, source_target_pairs={{0,4},{4,0},{8,12},{12,8},{16,20},{20,16},{24,28},{28,24},{1,5},{5... | collective-permute-start | bytes 9437192 | tf_op jit(solution)/shard_map/ppermute | solution.py:118
  300.0 43.3 %collective-permute-start.46 = (bf16[4,2,2,2,16,1024]{5,4,3,2,1,0:T(8,128)(2,1)}, bf16[4,2,2,2,16,1024]{5,4,3,2,1,0:T(8,128)(2,1)}, u32[]{:S(2)}, u32[]{:S(2)}) collective-permute-start(bf16[4,2,2,2,16,1024]{5,4,3,2,1,0:T(8,128)(2,1)} %dynamic-slice_bitcast_fusion.2), channel_id=1, source_target_pairs={{0,4},{4,0},{8,12},{12,8},{16,20},{20,16},{24,28},{28,24},{1,5},{5... | collective-permute-start | bytes 3145736 | tf_op jit(solution)/shard_map/ppermute | solution.py:133
  345.8 39.7 %collective-permute-start.35 = (bf16[4,2,2,2,16,3200]{5,4,3,2,1,0:T(8,128)(2,1)S(1)}, bf16[4,2,2,2,16,3200]{5,4,3,2,1,0:T(8,128)(2,1)}, u32[]{:S(2)}, u32[]{:S(2)}) collective-permute-start(bf16[4,2,2,2,16,3200]{5,4,3,2,1,0:T(8,128)(2,1)S(1)} %fusion.18), channel_id=1, source_target_pairs={{0,4},{4,0},{8,12},{12,8},{16,20},{20,16},{24,28},{28,24},{1,5},{5... | collective-permute-start | bytes 9830408 | tf_op jit(solution)/shard_map/ppermute | solution.py:133
  379.4 38.2 %collective-permute-start.57 = (bf16[4,2,2,2,16,4096]{5,4,3,2,1,0:T(8,128)(2,1)}, bf16[4,2,2,2,16,4096]{5,4,3,2,1,0:T(8,128)(2,1)}, u32[]{:S(2)}, u32[]{:S(2)}) collective-permute-start(bf16[4,2,2,2,16,4096]{5,4,3,2,1,0:T(8,128)(2,1)} %dynamic-slice_bitcast_fusion.1), channel_id=1, source_target_pairs={{0,4},{4,0},{8,12},{12,8},{16,20},{20,16},{24,28},{28,24},{1,5},{5... | collective-permute-start | bytes 12582920 | tf_op jit(solution)/shard_map/ppermute | solution.py:133
  379.4 48.0 %collective-permute-start.68 = (bf16[4,2,2,2,64,1024]{5,4,3,2,1,0:T(8,128)(2,1)}, bf16[4,2,2,2,64,1024]{5,4,3,2,1,0:T(8,128)(2,1)}, u32[]{:S(2)}, u32[]{:S(2)}) collective-permute-start(bf16[4,2,2,2,64,1024]{5,4,3,2,1,0:T(8,128)(2,1)} %dynamic-slice_bitcast_fusion), channel_id=1, source_target_pairs={{0,4},{4,0},{8,12},{12,8},{16,20},{20,16},{24,28},{28,24},{1,5},{5... | collective-permute-start | bytes 12582920 | tf_op jit(solution)/shard_map/ppermute | solution.py:133
  424.9 37.3 %collective-permute-start.58 = (bf16[4,2,16,4096]{3,2,0,1:T(8,128)(2,1)}, bf16[4,2,16,4096]{3,2,0,1:T(8,128)(2,1)}, u32[]{:S(2)}, u32[]{:S(2)}) collective-permute-start(bf16[4,2,16,4096]{3,2,0,1:T(8,128)(2,1)} %fusion.80), channel_id=1, source_target_pairs={{0,16},{4,20},{8,24},{12,28},{16,0},{20,4},{24,8},{28,12},{1,17},{... | collective-permute-start | bytes 3145736 | tf_op jit(solution)/shard_map/ppermute | solution.py:133
  427.1 38.7 %collective-permute-start.60 = (bf16[4,2,16,4096]{3,2,1,0:T(8,128)(2,1)}, bf16[4,2,16,4096]{3,2,1,0:T(8,128)(2,1)}, u32[]{:S(2)}, u32[]{:S(2)}) collective-permute-start(bf16[4,2,16,4096]{3,2,1,0:T(8,128)(2,1)} %fusion.78), channel_id=1, source_target_pairs={{0,8},{4,12},{8,0},{12,4},{16,24},{20,28},{24,16},{28,20},{1,9},{5... | collective-permute-start | bytes 3145736 | tf_op jit(solution)/shard_map/ppermute | solution.py:133
  457.0 26.1 %collective-permute-start.69 = (bf16[4,2,64,1024]{3,2,0,1:T(8,128)(2,1)S(1)}, bf16[4,2,64,1024]{3,2,0,1:T(8,128)(2,1)S(1)}, u32[]{:S(2)}, u32[]{:S(2)}) collective-permute-start(bf16[4,2,64,1024]{3,2,0,1:T(8,128)(2,1)S(1)} %fusion.81), channel_id=1, source_target_pairs={{0,16},{4,20},{8,24},{12,28},{16,0},{20,4},{24,8},{28,12},{1,17},{... | collective-permute-start | bytes 3145736 | tf_op jit(solution)/shard_map/ppermute | solution.py:133
  457.9 26.2 %collective-permute-start.71 = (bf16[4,2,64,1024]{3,2,1,0:T(8,128)(2,1)S(1)}, bf16[4,2,64,1024]{3,2,1,0:T(8,128)(2,1)S(1)}, u32[]{:S(2)}, u32[]{:S(2)}) collective-permute-start(bf16[4,2,64,1024]{3,2,1,0:T(8,128)(2,1)S(1)} %fusion.79), channel_id=1, source_target_pairs={{0,8},{4,12},{8,0},{12,4},{16,24},{20,28},{24,16},{28,20},{1,9},{5... | collective-permute-start | bytes 3145736 | tf_op jit(solution)/shard_map/ppermute | solution.py:133
  461.2 30.6 %collective-permute-start.44 = (bf16[2,2,16,3200]{3,2,1,0:T(8,128)(2,1)S(1)}, bf16[2,2,16,3200]{3,2,1,0:T(8,128)(2,1)S(1)}, u32[]{:S(2)}, u32[]{:S(2)}) collective-permute-start(bf16[2,2,16,3200]{3,2,1,0:T(8,128)(2,1)S(1)} %maximum_select_fusion.37), channel_id=1, source_target_pairs={{0,16},{4,20},{8,24},{12,28},{16,0},{20,4},{24,8},{28,12},{1,17},{... | collective-permute-start | bytes 1228808 | tf_op jit(solution)/shard_map/ppermute | solution.py:118
  463.7 31.5 %collective-permute-start.59 = (bf16[4,16,4096]{2,1,0:T(8,128)(2,1)S(1)}, bf16[4,16,4096]{2,1,0:T(8,128)(2,1)S(1)}, u32[]{:S(2)}, u32[]{:S(2)}) collective-permute-start(bf16[4,16,4096]{2,1,0:T(8,128)(2,1)S(1)} %fusion.96), channel_id=1, source_target_pairs={{0,8},{4,12},{8,0},{12,4},{16,24},{20,28},{24,16},{28,20},{1,9},{5... | collective-permute-start | bytes 1572872 | tf_op jit(solution)/shard_map/ppermute | solution.py:133
  467.3 35.7 %collective-permute-start.61 = (bf16[4,16,4096]{2,1,0:T(8,128)(2,1)S(1)}, bf16[4,16,4096]{2,1,0:T(8,128)(2,1)S(1)}, u32[]{:S(2)}, u32[]{:S(2)}) collective-permute-start(bf16[4,16,4096]{2,1,0:T(8,128)(2,1)S(1)} %fusion.97), channel_id=1, source_target_pairs={{0,16},{4,20},{8,24},{12,28},{16,0},{20,4},{24,8},{28,12},{1,17},{... | collective-permute-start | bytes 1572872 | tf_op jit(solution)/shard_map/ppermute | solution.py:133
  483.6 24.2 %collective-permute-start.70 = (bf16[4,64,1024]{2,1,0:T(8,128)(2,1)S(1)}, bf16[4,64,1024]{2,1,0:T(8,128)(2,1)S(1)}, u32[]{:S(2)}, u32[]{:S(2)}) collective-permute-start(bf16[4,64,1024]{2,1,0:T(8,128)(2,1)S(1)} %fusion.98), channel_id=1, source_target_pairs={{0,8},{4,12},{8,0},{12,4},{16,24},{20,28},{24,16},{28,20},{1,9},{5... | collective-permute-start | bytes 1572872 | tf_op jit(solution)/shard_map/ppermute | solution.py:133
  484.5 28.5 %collective-permute-start.72 = (bf16[4,64,1024]{2,1,0:T(8,128)(2,1)S(1)}, bf16[4,64,1024]{2,1,0:T(8,128)(2,1)S(1)}, u32[]{:S(2)}, u32[]{:S(2)}) collective-permute-start(bf16[4,64,1024]{2,1,0:T(8,128)(2,1)S(1)} %fusion.99), channel_id=1, source_target_pairs={{0,16},{4,20},{8,24},{12,28},{16,0},{20,4},{24,8},{28,12},{1,17},{... | collective-permute-start | bytes 1572872 | tf_op jit(solution)/shard_map/ppermute | solution.py:133
  492.0 40.9 %collective-permute-start.45 = (bf16[2,2,2,16,3200]{4,3,2,1,0:T(8,128)(2,1)S(1)}, bf16[2,2,2,16,3200]{4,3,2,1,0:T(8,128)(2,1)S(1)}, u32[]{:S(2)}, u32[]{:S(2)}) collective-permute-start(bf16[2,2,2,16,3200]{4,3,2,1,0:T(8,128)(2,1)S(1)} %maximum_select_fusion.18), channel_id=1, source_target_pairs={{0,4},{4,0},{8,12},{12,8},{16,20},{20,16},{24,28},{28,24},{1,5},{5... | collective-permute-start | bytes 2457608 | tf_op jit(solution)/shard_map/ppermute | solution.py:118
  (117 other events, 1231.5 us)

commit v7 on v6

--- a/solution.py
+++ b/solution.py
@@ -219,10 +219,26 @@
                 (g.astype(jnp.float32) + lax.dynamic_index_in_dim(a, chunk, 0, keepdims=False)).astype(jnp.bfloat16)
                 for g, a in zip(got, acc)
             ]
-    part, hb = send, []
-    for bit in chip_bits(n_dp):
-        part, hb = exchange(part, hb, bit, d, n_dp)
-    both = part
+    bits_chip = chip_bits(n_dp)
+    if direct and len(bits_chip) == 2:
+        masks = [2, 4, 6]
+        got = []
+        for mask in masks:
+            got.append(lax.ppermute(send, "dp", xor_pairs(n_dp, mask)))
+        both = []
+        for i, own in enumerate(send):
+            cand = jnp.stack([own] + [g[i] for g in got]).reshape((2, 2) + own.shape)
+            high = ((d >> 2) & 1) == 1
+            low_bit = ((d >> 1) & 1) == 1
+            cand = jnp.where(high, cand[::-1], cand)
+            cand = jnp.where(low_bit, cand[:, ::-1], cand)
+            both.append(cand)
+        hb = [2, 1]
+    else:
+        part, hb = send, []
+        for bit in bits_chip:
+            part, hb = exchange(part, hb, bit, d, n_dp)
+        both = part
     if n_dp > 1:
         both, hb = exchange(both, hb, 0, d, n_dp)
     return [b.reshape(g.shape[0] // n_fsdp, g.shape[1]).astype(jnp.float32) for b, g in zip(both, grads)]

time: 585 us -> 585 us (level)
    ppermute x32 -> x30, waiting for transfers between devices: 76 us -> 66.4 us  [exchange(): got = lax.ppermute(leaves, 'dp', xor_pairs(n_dp, 1 << bit))]
    ppermute x0 -> x3, waiting for transfers between devices: none -> 7.48 us  [reduce_chain(): got.append(lax.ppermute(send, 'dp', xor_pairs(n_dp, mask)))]
    ppermute x32 -> x30, starting transfers between devices: 28.1 us -> 26.2 us  [exchange(): got = lax.ppermute(leaves, 'dp', xor_pairs(n_dp, 1 << bit))]
    select_n x32 -> x29, other arithmetic: 14.2 us -> 14.1 us  [exchange(): jnp.where(mine, jnp.stack([a, g], axis=pos), jnp.stack([g, a], axis=pos))]
  transfers between devices with their start and end apart: 79 -> 80, of which waited for: 43 -> 43; matrix products, arithmetic and copies ran while one was open for 29% -> 28% of each run, Pallas kernels for 0% -> 0%
where the time goes in v7:
time: 585 us; the launch traced here: 578 us
  waiting for transfers between devices  181 us (31%)
  matrix products  115 us (20%)
  starting transfers between devices  102 us (17%)
  local copies, waits for them, and re-layouts  88.3 us (15%)
  other arithmetic  84.8 us (14%)
  between operations  6.31 us (1%)
    ppermute x30, waiting for transfers between devices, exchange(): got = lax.ppermute(leaves, 'dp', xor_pairs(n_dp, 1 << bit))  66.4 us
    ppermute x20, waiting for transfers between devices, split_bit(): lax.ppermute([v.astype(jnp.bfloat16) for v in send], 'dp', xor_pairs(n_dp...  60.5 us
    ppermute x30, starting transfers between devices, exchange(): got = lax.ppermute(leaves, 'dp', xor_pairs(n_dp, 1 << bit))  26.2 us
    ppermute x9, waiting for transfers between devices, reduce_chain(): got = lax.ppermute(send, 'fsdp', down)  23.9 us
    ppermute x20, starting transfers between devices, split_bit(): lax.ppermute([v.astype(jnp.bfloat16) for v in send], 'dp', xor_pairs(n_dp...  21.1 us
    add x12, other arithmetic, split_bit(): k.astype(jnp.float32) + g.astype(jnp.float32)  19.2 us
    ppermute x9, starting transfers between devices, gather_chain(): got = buf = lax.ppermute(buf, 'fsdp', down)  19.2 us
    concatenate x4, other arithmetic, gather_chain(): return (jnp.roll(rel, f, axis=0).reshape(n_fsdp * rows, cols), vecs)  17 us
  transfers between devices with their start and end apart: 80, of which 43 were waited for; matrix products, arithmetic and copies ran while one was open for 28% of the time, Pallas kernels for 0%

profile of v7, /device:TPU:0, one launch (start us, length us, event | category | flops | bytes accessed | tf_op | source)
XLA Modules:
  0.0 577.9 jit_solution(13040953609625384198)
XLA Ops:
  91.4 7.2 %collective-permute-done.24 = bf16[3,16,4096]{2,1,0:T(8,128)(2,1)S(1)} collective-permute-done((bf16[3,16,4096]{2,1,0:T(8,128)(2,1)S(1)}, bf16[3,16,4096]{2,1,0:T(8,128)(2,1)S(1)}, u32[]{:S(2)}, u32[]{:S(2)}) %collective-permute-start.24) | collective-permute-done | bytes 393248 | tf_op jit(solution)/shard_map/ppermute | solution.py:118
  112.4 7.8 %collective-permute-done.25 = bf16[3,2,16,4096]{3,2,1,0:T(8,128)(2,1)S(1)} collective-permute-done((bf16[3,2,16,4096]{3,2,1,0:T(8,128)(2,1)S(1)}, bf16[3,2,16,4096]{3,2,1,0:T(8,128)(2,1)S(1)}, u32[]{:S(2)}, u32[]{:S(2)}) %collective-permute-start.25) | collective-permute-done | bytes 786464 | tf_op jit(solution)/shard_map/ppermute | solution.py:118
  127.2 9.2 %collective-permute-done.33 = bf16[3,2,64,1024]{3,2,1,0:T(8,128)(2,1)S(1)} collective-permute-done((bf16[3,2,64,1024]{3,2,1,0:T(8,128)(2,1)S(1)}, bf16[3,2,64,1024]{3,2,1,0:T(8,128)(2,1)S(1)}, u32[]{:S(2)}, u32[]{:S(2)}) %collective-permute-start.33) | collective-permute-done | bytes 786464 | tf_op jit(solution)/shard_map/ppermute | solution.py:118
  192.4 5.2 fusion.11
  197.6 6.3 %maximum_select_fusion.1 = bf16[3,2,2,2,2,64,1024]{6,5,4,3,2,1,0:T(8,128)(2,1)S(1)} fusion(bf16[3,2,2,1,2,64,1024]{6,5,4,3,2,1,0:T(8,128)(2,1)} %bitcast.95, bf16[3,2,2,1,2,64,1024]{6,5,4,3,2,1,0:T(8,128)(2,1)S(1)} %copy-done.7, pred[]{:T(512)S(6)} %eq.46), kind=kLoop, calls=%fused_computation.39 | loop fusion | flops 9437184 | bytes 12582913 | tf_op jit(solution)/shard_map/jit(_where)/select_n | solution.py:122
  209.3 10.9 %multiply_convert_fusion = (bf16[600,4096]{1,0:T(8,128)(2,1)}, f32[600,4096]{1,0:T(8,128)}) fusion(f32[4096]{0:T(1024)S(1)} %bitcast.594, bf16[1024,4096]{1,0:T(8,128)(2,1)S(1)} %bitcast.493, f32[600,1024]{1,0:T(8,128)S(1)} %get-tuple-element.97, f32[1024]{0:T(1024)S(1)} %bitcast.601, f32[1024]{0:T(1024)S(1)} %bitcast.586, f32[600]{0:T(1024)S(1)} %add_rsqrt_fusion, ...), kind=kOutput, calls=%fused_computation.19 | convolution fusion | flops 5050982400 | bytes 25621184 | tf_op jit(solution)/shard_map/dot_general | solution.py:336
  220.2 13.0 %fusion.192 = (bf16[4096]{0:T(1024)(128)(2,1)S(1)}, bf16[600,4096]{1,0:T(8,128)(2,1)S(1)}) fusion(f32[600,4096]{1,0:T(8,128)} %get-tuple-element.99, f32[4096]{0:T(1024)S(1)} %bitcast.595, bf16[4096,1024]{1,0:T(8,128)(2,1)S(1)} %bitcast.489, bf16[600,1024]{1,0:T(8,128)(2,1)S(1)} %copy-done.43, f32[]{:T(128)} %bitcast.98), kind=kOutput, calls=%fused_computation.428 | convolution fusion | flops 5064495104 | bytes 24387588 | tf_op jit(solution)/shard_map/dot_general | solution.py:346
  233.2 10.3 %multiply_reduce_fusion.1 = (bf16[1024]{0:T(1024)(128)(2,1)S(1)}, f32[600]{0:T(1024)S(1)}, f32[600]{0:T(1024)S(1)}, bf16[1024]{0:T(1024)(128)(2,1)S(1)}, f32[600,1024]{1,0:T(8,128)S(1)}) fusion(f32[600,1024]{1,0:T(8,128)S(1)} %get-tuple-element.97, f32[600]{0:T(1024)S(1)} %add_rsqrt_fusion, f32[600]{0:T(1024)S(1)} %broadcast_multiply_fusion.4, ...), kind=kOutput, calls=%fused_computation.127 | convolution fusion | flops 5038691328 | bytes 18236800 | tf_op jit(solution)/shard_map/dot_general | solution.py:351
  250.2 9.8 %convolution_convert_fusion = bf16[1024,4096]{1,0:T(8,128)(2,1)} fusion(bf16[600,4096]{1,0:T(8,128)(2,1)S(1)} %bitcast.614, f32[600,1024]{1,0:T(8,128)S(1)} %get-tuple-element.97, f32[1024]{0:T(1024)S(1)} %bitcast.602, f32[1024]{0:T(1024)S(1)} %bitcast.589, f32[600]{0:T(1024)S(1)} %add_rsqrt_fusion, f32[600]{0:T(1024)S(1)} %broadcast_multiply_fusion.4), kind=kOutput, calls=%fused_computation.31 | convolution fusion | flops 5040431104 | bytes 15774400 | tf_op jit(solution)/shard_map/dot_general | solution.py:349
  262.8 6.6 %fusion.191 = (bf16[16,64]{1,0:T(8,128)(2,1)S(1)}, bf16[12,50,16,64]{3,1,2,0:T(8,128)(2,1)}) fusion(f32[12,16,50,50]{2,3,1,0:T(8,128)} %copy-done, f32[12,16,50]{2,1,0:T(8,128)S(1)} %log_add_fusion, bf16[12,50,16,64]{3,2,1,0:T(8,128)(2,1)} %reshape.2348), kind=kOutput, calls=%fused_computation.427 | convolution fusion | flops 63627776 | bytes 4418048 | tf_op jit(solution)/shard_map/chqk,cqhd->ckhd/dot_general | solution.py:88
  278.9 12.7 %convolution_convert_fusion.1 = bf16[4096,1024]{1,0:T(8,128)(2,1)} fusion(bf16[600,4096]{1,0:T(8,128)(2,1)} %get-tuple-element.98, bf16[600,1024]{1,0:T(8,128)(2,1)S(1)} %copy-done.44, f32[]{:T(128)} %bitcast.98), kind=kOutput, calls=%fused_computation.32 | convolution fusion | flops 5039202304 | bytes 14532612 | tf_op jit(solution)/shard_map/dot_general | solution.py:344
  291.6 6.4 %add_convert_fusion.1 = bf16[600,1024]{1,0:T(8,128)(2,1)} fusion(f32[600,1024]{1,0:T(8,128)S(1)} %copy-done.18, bf16[600,4096]{1,0:T(8,128)(2,1)S(1)} %bitcast.616, bf16[4096,1024]{1,0:T(8,128)(2,1)S(1)} %bitcast.492, f32[1024]{0:T(1024)S(1)} %bitcast.600), kind=kOutput, calls=%fused_computation.132 | convolution fusion | flops 5035008000 | bytes 16994304 | tf_op jit(solution)/shard_map/dot_general | solution.py:340
  325.2 9.7 %fusion.52 = (bf16[1024]{0:T(1024)(128)(2,1)S(1)}, f32[600]{0:T(1024)S(1)}, f32[600]{0:T(1024)S(1)}, bf16[1024]{0:T(1024)(128)(2,1)S(1)}, f32[600,1024]{1,0:T(8,128)}) fusion(bf16[600,1024]{1,0:T(8,128)(2,1)S(1)} %copy-done.10, f32[600]{0:T(1024)S(1)} %add_rsqrt_fusion.1, f32[600]{0:T(1024)S(1)} %broadcast_multiply_fusion.5, f32[1024]{0:T(1024)S(1)} %bitcast.591, ...), kind=kOutput, calls=%fused_computation.125 | convolution fusion | flops 3781014528 | bytes 13682048 | tf_op jit(solution)/shard_map/dot_general | solution.py:365
  335.7 7.9 %convolution_convert_fusion.2 = bf16[1024,3072]{1,0:T(8,128)(2,1)S(1)} fusion(bf16[600,3072]{1,0:T(8,128)(2,1)} %constant_dynamic-update-slice_fusion, bf16[600,1024]{1,0:T(8,128)(2,1)S(1)} %copy-done.10, f32[1024]{0:T(1024)S(1)} %bitcast.599, f32[1024]{0:T(1024)S(1)} %bitcast.592, f32[600]{0:T(1024)S(1)} %add_rsqrt_fusion.1, ...), kind=kOutput, calls=%fused_computation.42 | convolution fusion | flops 3781705728 | bytes 11219648 | tf_op jit(solution)/shard_map/dot_general | solution.py:362
  348.2 5.5 collective-permute-done.48
  395.9 14.4 %collective-permute-done.36 = bf16[4,2,16,3200]{3,2,0,1:T(8,128)(2,1)S(1)} collective-permute-done((bf16[4,2,16,3200]{3,2,0,1:T(8,128)(2,1)S(1)}, bf16[4,2,16,3200]{3,2,0,1:T(8,128)(2,1)S(1)}, u32[]{:S(2)}, u32[]{:S(2)}) %collective-permute-start.36) | collective-permute-done | bytes 819232 | tf_op jit(solution)/shard_map/ppermute | solution.py:133
  427.7 5.7 convert_add_fusion
  446.5 6.1 %collective-permute-done.41 = bf16[2,16,3200]{2,1,0:T(8,128)(2,1)} collective-permute-done((bf16[2,16,3200]{2,1,0:T(8,128)(2,1)S(1)}, bf16[2,16,3200]{2,1,0:T(8,128)(2,1)}, u32[]{:S(2)}, u32[]{:S(2)}) %collective-permute-start.41) | collective-permute-done | bytes 204832 | tf_op jit(solution)/shard_map/ppermute | solution.py:206
  473.2 15.7 %collective-permute-done.70 = bf16[4,2,64,1024]{3,2,0,1:T(8,128)(2,1)S(1)} collective-permute-done((bf16[4,2,64,1024]{3,2,0,1:T(8,128)(2,1)S(1)}, bf16[4,2,64,1024]{3,2,0,1:T(8,128)(2,1)S(1)}, u32[]{:S(2)}, u32[]{:S(2)}) %collective-permute-start.70) | collective-permute-done | bytes 1048608 | tf_op jit(solution)/shard_map/ppermute | solution.py:133
  493.8 9.7 %collective-permute-done.60 = bf16[4,16,4096]{2,1,0:T(8,128)(2,1)S(1)} collective-permute-done((bf16[4,16,4096]{2,1,0:T(8,128)(2,1)S(1)}, bf16[4,16,4096]{2,1,0:T(8,128)(2,1)S(1)}, u32[]{:S(2)}, u32[]{:S(2)}) %collective-permute-start.60) | collective-permute-done | bytes 524320 | tf_op jit(solution)/shard_map/ppermute | solution.py:133
  507.6 6.1 %collective-permute-done.71 = bf16[4,64,1024]{2,1,0:T(8,128)(2,1)S(1)} collective-permute-done((bf16[4,64,1024]{2,1,0:T(8,128)(2,1)S(1)}, bf16[4,64,1024]{2,1,0:T(8,128)(2,1)S(1)}, u32[]{:S(2)}, u32[]{:S(2)}) %collective-permute-start.71) | collective-permute-done | bytes 524320 | tf_op jit(solution)/shard_map/ppermute | solution.py:133
  519.8 6.4 %collective-permute-done.74 = bf16[2,64,1024]{2,1,0:T(8,128)(2,1)S(1)} collective-permute-done((bf16[2,64,1024]{2,1,0:T(8,128)(2,1)S(1)}, bf16[2,64,1024]{2,1,0:T(8,128)(2,1)S(1)}, u32[]{:S(2)}, u32[]{:S(2)}) %collective-permute-start.74) | collective-permute-done | bytes 262176 | tf_op jit(solution)/shard_map/ppermute | solution.py:216
  556.6 7.3 %collective-permute-done.67 = bf16[2,2,16,4096]{3,2,1,0:T(8,128)(2,1)S(1)} collective-permute-done((bf16[2,2,16,4096]{3,2,1,0:T(8,128)(2,1)S(1)}, bf16[2,2,16,4096]{3,2,1,0:T(8,128)(2,1)S(1)}, u32[]{:S(2)}, u32[]{:S(2)}) %collective-permute-start.67) | collective-permute-done | bytes 524320 | tf_op jit(solution)/shard_map/ppermute | solution.py:118
  564.2 7.2 %collective-permute-done.78 = bf16[2,2,64,1024]{3,2,1,0:T(8,128)(2,1)S(1)} collective-permute-done((bf16[2,2,64,1024]{3,2,1,0:T(8,128)(2,1)S(1)}, bf16[2,2,64,1024]{3,2,1,0:T(8,128)(2,1)S(1)}, u32[]{:S(2)}, u32[]{:S(2)}) %collective-permute-start.78) | collective-permute-done | bytes 524320 | tf_op jit(solution)/shard_map/ppermute | solution.py:118
  (513 shorter events, 364.8 us)
Async XLA Ops:
  17.9 38.3 %collective-permute-start.5 = (bf16[2,16,3072]{2,1,0:T(8,128)(2,1)S(1)}, bf16[2,16,3072]{2,1,0:T(8,128)(2,1)S(1)}, u32[]{:S(2)}, u32[]{:S(2)}) collective-permute-start(bf16[2,16,3072]{2,1,0:T(8,128)(2,1)S(1)} %dynamic-slice_bitcast_fusion.5), channel_id=1, source_target_pairs={{0,1},{1,2},{2,3},{3,0},{4,5},{5,6},{6,7},{7,4},{8,9},{9,10},{10,1... | collective-permute-start | bytes 589832 | tf_op jit(solution)/shard_map/ppermute | solution.py:152
  18.6 39.1 %collective-permute-start.4 = (bf16[2,16,3072]{2,1,0:T(8,128)(2,1)S(1)}, bf16[2,16,3072]{2,1,0:T(8,128)(2,1)S(1)}, u32[]{:S(2)}, u32[]{:S(2)}) collective-permute-start(bf16[2,16,3072]{2,1,0:T(8,128)(2,1)S(1)} %dynamic-slice_bitcast_fusion.5), channel_id=1, source_target_pairs={{0,2},{1,3},{2,0},{3,1},{4,6},{5,7},{6,4},{7,5},{8,10},{9,11},{10,... | collective-permute-start | bytes 589832 | tf_op jit(solution)/shard_map/ppermute | solution.py:152
  29.8 29.4 %collective-permute-start.3 = (bf16[2,16,3072]{2,1,0:T(8,128)(2,1)S(1)}, bf16[2,16,3072]{2,1,0:T(8,128)(2,1)S(1)}, u32[]{:S(2)}, u32[]{:S(2)}) collective-permute-start(bf16[2,16,3072]{2,1,0:T(8,128)(2,1)S(1)} %dynamic-slice_bitcast_fusion.5), channel_id=1, source_target_pairs={{0,3},{1,0},{2,1},{3,2},{4,7},{5,4},{6,5},{7,6},{8,11},{9,8},{10,9... | collective-permute-start | bytes 589832 | tf_op jit(solution)/shard_map/ppermute | solution.py:152
  34.0 31.6 %collective-permute-start.19 = (bf16[2,16,4096]{2,1,0:T(8,128)(2,1)S(1)}, bf16[2,16,4096]{2,1,0:T(8,128)(2,1)S(1)}, u32[]{:S(2)}, u32[]{:S(2)}) collective-permute-start(bf16[2,16,4096]{2,1,0:T(8,128)(2,1)S(1)} %dynamic-slice_bitcast_fusion.4), channel_id=1, source_target_pairs={{0,3},{1,0},{2,1},{3,2},{4,7},{5,4},{6,5},{7,6},{8,11},{9,8},{10,9... | collective-permute-start | bytes 786440 | tf_op jit(solution)/shard_map/ppermute | solution.py:154
  69.9 38.0 %collective-permute-start.18 = (bf16[3,2,2,2,16,1024]{5,4,3,2,1,0:T(8,128)(2,1)S(1)}, bf16[3,2,2,2,16,1024]{5,4,3,2,1,0:T(8,128)(2,1)S(1)}, u32[]{:S(2)}, u32[]{:S(2)}) collective-permute-start(bf16[3,2,2,2,16,1024]{5,4,3,2,1,0:T(8,128)(2,1)S(1)} %get-tuple-element.61), channel_id=1, source_target_pairs={{0,4},{4,0},{8,12},{12,8},{16,20},{20,16},{24,28},{28,24},{1,5},{5... | collective-permute-start | bytes 2359304 | tf_op jit(solution)/shard_map/ppermute | solution.py:118
  98.6 43.4 %collective-permute-start.10 = (bf16[3,2,2,2,16,3072]{5,4,3,2,1,0:T(8,128)(2,1)S(1)}, bf16[3,2,2,2,16,3072]{5,4,3,2,1,0:T(8,128)(2,1)S(1)}, u32[]{:S(2)}, u32[]{:S(2)}) collective-permute-start(bf16[3,2,2,2,16,3072]{5,4,3,2,1,0:T(8,128)(2,1)S(1)} %get-tuple-element.39), channel_id=1, source_target_pairs={{0,4},{4,0},{8,12},{12,8},{16,20},{20,16},{24,28},{28,24},{1,5},{5... | collective-permute-start | bytes 7077896 | tf_op jit(solution)/shard_map/ppermute | solution.py:118
  98.7 21.4 %collective-permute-start.25 = (bf16[3,2,16,4096]{3,2,1,0:T(8,128)(2,1)S(1)}, bf16[3,2,16,4096]{3,2,1,0:T(8,128)(2,1)S(1)}, u32[]{:S(2)}, u32[]{:S(2)}) collective-permute-start(bf16[3,2,16,4096]{3,2,1,0:T(8,128)(2,1)S(1)} %maximum_select_fusion.20), channel_id=1, source_target_pairs={{0,8},{4,12},{8,0},{12,4},{16,24},{20,28},{24,16},{28,20},{1,9},{5... | collective-permute-start | bytes 2359304 | tf_op jit(solution)/shard_map/ppermute | solution.py:118
  105.5 30.9 %collective-permute-start.33 = (bf16[3,2,64,1024]{3,2,1,0:T(8,128)(2,1)S(1)}, bf16[3,2,64,1024]{3,2,1,0:T(8,128)(2,1)S(1)}, u32[]{:S(2)}, u32[]{:S(2)}) collective-permute-start(bf16[3,2,64,1024]{3,2,1,0:T(8,128)(2,1)S(1)} %maximum_select_fusion.24), channel_id=1, source_target_pairs={{0,8},{4,12},{8,0},{12,4},{16,24},{20,28},{24,16},{28,20},{1,9},{5... | collective-permute-start | bytes 2359304 | tf_op jit(solution)/shard_map/ppermute | solution.py:118
  107.9 31.0 %collective-permute-start.31 = (bf16[3,2,64,1024]{3,2,1,0:T(8,128)(2,1)S(1)}, bf16[3,2,64,1024]{3,2,1,0:T(8,128)(2,1)S(1)}, u32[]{:S(2)}, u32[]{:S(2)}) collective-permute-start(bf16[3,2,64,1024]{3,2,1,0:T(8,128)(2,1)S(1)} %maximum_select_fusion.22), channel_id=1, source_target_pairs={{0,16},{4,20},{8,24},{12,28},{16,0},{20,4},{24,8},{28,12},{1,17},{... | collective-permute-start | bytes 2359304 | tf_op jit(solution)/shard_map/ppermute | solution.py:118
  127.2 60.7 %collective-permute-start.26 = (bf16[3,2,2,2,16,4096]{5,4,3,2,1,0:T(8,128)(2,1)}, bf16[3,2,2,2,16,4096]{5,4,3,2,1,0:T(8,128)(2,1)}, u32[]{:S(2)}, u32[]{:S(2)}) collective-permute-start(bf16[3,2,2,2,16,4096]{5,4,3,2,1,0:T(8,128)(2,1)} %get-tuple-element.37), channel_id=1, source_target_pairs={{0,4},{4,0},{8,12},{12,8},{16,20},{20,16},{24,28},{28,24},{1,5},{5... | collective-permute-start | bytes 9437192 | tf_op jit(solution)/shard_map/ppermute | solution.py:118
  142.0 55.6 %collective-permute-start.34 = (bf16[3,2,2,2,64,1024]{5,4,3,2,1,0:T(8,128)(2,1)}, bf16[3,2,2,2,64,1024]{5,4,3,2,1,0:T(8,128)(2,1)}, u32[]{:S(2)}, u32[]{:S(2)}) collective-permute-start(bf16[3,2,2,2,64,1024]{5,4,3,2,1,0:T(8,128)(2,1)} %get-tuple-element.35), channel_id=1, source_target_pairs={{0,4},{4,0},{8,12},{12,8},{16,20},{20,16},{24,28},{28,24},{1,5},{5... | collective-permute-start | bytes 9437192 | tf_op jit(solution)/shard_map/ppermute | solution.py:118
  300.3 43.3 %collective-permute-start.47 = (bf16[4,2,2,2,16,1024]{5,4,3,2,1,0:T(8,128)(2,1)}, bf16[4,2,2,2,16,1024]{5,4,3,2,1,0:T(8,128)(2,1)}, u32[]{:S(2)}, u32[]{:S(2)}) collective-permute-start(bf16[4,2,2,2,16,1024]{5,4,3,2,1,0:T(8,128)(2,1)} %dynamic-slice_bitcast_fusion.2), channel_id=1, source_target_pairs={{0,4},{4,0},{8,12},{12,8},{16,20},{20,16},{24,28},{28,24},{1,5},{5... | collective-permute-start | bytes 3145736 | tf_op jit(solution)/shard_map/ppermute | solution.py:133
  346.1 39.8 %collective-permute-start.35 = (bf16[4,2,2,2,16,3200]{5,4,3,2,1,0:T(8,128)(2,1)S(1)}, bf16[4,2,2,2,16,3200]{5,4,3,2,1,0:T(8,128)(2,1)}, u32[]{:S(2)}, u32[]{:S(2)}) collective-permute-start(bf16[4,2,2,2,16,3200]{5,4,3,2,1,0:T(8,128)(2,1)S(1)} %fusion.18), channel_id=1, source_target_pairs={{0,4},{4,0},{8,12},{12,8},{16,20},{20,16},{24,28},{28,24},{1,5},{5... | collective-permute-start | bytes 9830408 | tf_op jit(solution)/shard_map/ppermute | solution.py:133
  379.7 38.3 %collective-permute-start.58 = (bf16[4,2,2,2,16,4096]{5,4,3,2,1,0:T(8,128)(2,1)}, bf16[4,2,2,2,16,4096]{5,4,3,2,1,0:T(8,128)(2,1)}, u32[]{:S(2)}, u32[]{:S(2)}) collective-permute-start(bf16[4,2,2,2,16,4096]{5,4,3,2,1,0:T(8,128)(2,1)} %dynamic-slice_bitcast_fusion.1), channel_id=1, source_target_pairs={{0,4},{4,0},{8,12},{12,8},{16,20},{20,16},{24,28},{28,24},{1,5},{5... | collective-permute-start | bytes 12582920 | tf_op jit(solution)/shard_map/ppermute | solution.py:133
  379.7 48.1 %collective-permute-start.69 = (bf16[4,2,2,2,64,1024]{5,4,3,2,1,0:T(8,128)(2,1)}, bf16[4,2,2,2,64,1024]{5,4,3,2,1,0:T(8,128)(2,1)}, u32[]{:S(2)}, u32[]{:S(2)}) collective-permute-start(bf16[4,2,2,2,64,1024]{5,4,3,2,1,0:T(8,128)(2,1)} %dynamic-slice_bitcast_fusion), channel_id=1, source_target_pairs={{0,4},{4,0},{8,12},{12,8},{16,20},{20,16},{24,28},{28,24},{1,5},{5... | collective-permute-start | bytes 12582920 | tf_op jit(solution)/shard_map/ppermute | solution.py:133
  410.5 22.9 %collective-permute-start.37 = (bf16[4,16,3200]{2,1,0:T(8,128)(2,1)S(1)}, bf16[4,16,3200]{2,1,0:T(8,128)(2,1)}, u32[]{:S(2)}, u32[]{:S(2)}) collective-permute-start(bf16[4,16,3200]{2,1,0:T(8,128)(2,1)S(1)} %fusion.129), channel_id=1, source_target_pairs={{0,8},{4,12},{8,0},{12,4},{16,24},{20,28},{24,16},{28,20},{1,9},{5... | collective-permute-start | bytes 1228808 | tf_op jit(solution)/shard_map/ppermute | solution.py:133
  425.1 43.3 %collective-permute-start.59 = (bf16[4,2,16,4096]{3,2,0,1:T(8,128)(2,1)}, bf16[4,2,16,4096]{3,2,0,1:T(8,128)(2,1)}, u32[]{:S(2)}, u32[]{:S(2)}) collective-permute-start(bf16[4,2,16,4096]{3,2,0,1:T(8,128)(2,1)} %fusion.79), channel_id=1, source_target_pairs={{0,16},{4,20},{8,24},{12,28},{16,0},{20,4},{24,8},{28,12},{1,17},{... | collective-permute-start | bytes 3145736 | tf_op jit(solution)/shard_map/ppermute | solution.py:133
  427.3 43.2 %collective-permute-start.61 = (bf16[4,2,16,4096]{3,2,1,0:T(8,128)(2,1)}, bf16[4,2,16,4096]{3,2,1,0:T(8,128)(2,1)}, u32[]{:S(2)}, u32[]{:S(2)}) collective-permute-start(bf16[4,2,16,4096]{3,2,1,0:T(8,128)(2,1)} %fusion.77), channel_id=1, source_target_pairs={{0,8},{4,12},{8,0},{12,4},{16,24},{20,28},{24,16},{28,20},{1,9},{5... | collective-permute-start | bytes 3145736 | tf_op jit(solution)/shard_map/ppermute | solution.py:133
  462.8 26.0 %collective-permute-start.70 = (bf16[4,2,64,1024]{3,2,0,1:T(8,128)(2,1)S(1)}, bf16[4,2,64,1024]{3,2,0,1:T(8,128)(2,1)S(1)}, u32[]{:S(2)}, u32[]{:S(2)}) collective-permute-start(bf16[4,2,64,1024]{3,2,0,1:T(8,128)(2,1)S(1)} %fusion.80), channel_id=1, source_target_pairs={{0,16},{4,20},{8,24},{12,28},{16,0},{20,4},{24,8},{28,12},{1,17},{... | collective-permute-start | bytes 3145736 | tf_op jit(solution)/shard_map/ppermute | solution.py:133
  466.2 26.0 %collective-permute-start.72 = (bf16[4,2,64,1024]{3,2,1,0:T(8,128)(2,1)S(1)}, bf16[4,2,64,1024]{3,2,1,0:T(8,128)(2,1)S(1)}, u32[]{:S(2)}, u32[]{:S(2)}) collective-permute-start(bf16[4,2,64,1024]{3,2,1,0:T(8,128)(2,1)S(1)} %fusion.78), channel_id=1, source_target_pairs={{0,8},{4,12},{8,0},{12,4},{16,24},{20,28},{24,16},{28,20},{1,9},{5... | collective-permute-start | bytes 3145736 | tf_op jit(solution)/shard_map/ppermute | solution.py:133
  468.2 51.3 %collective-permute-start.46 = (bf16[2,2,2,16,3200]{4,3,2,1,0:T(8,128)(2,1)S(1)}, bf16[2,2,2,16,3200]{4,3,2,1,0:T(8,128)(2,1)S(1)}, u32[]{:S(2)}, u32[]{:S(2)}) collective-permute-start(bf16[2,2,2,16,3200]{4,3,2,1,0:T(8,128)(2,1)S(1)} %reverse_select_fusion), channel_id=1, source_target_pairs={{0,4},{4,0},{8,12},{12,8},{16,20},{20,16},{24,28},{28,24},{1,5},{5... | collective-permute-start | bytes 2457608 | tf_op jit(solution)/shard_map/ppermute | solution.py:118
  470.0 33.5 %collective-permute-start.60 = (bf16[4,16,4096]{2,1,0:T(8,128)(2,1)S(1)}, bf16[4,16,4096]{2,1,0:T(8,128)(2,1)S(1)}, u32[]{:S(2)}, u32[]{:S(2)}) collective-permute-start(bf16[4,16,4096]{2,1,0:T(8,128)(2,1)S(1)} %fusion.95), channel_id=1, source_target_pairs={{0,8},{4,12},{8,0},{12,4},{16,24},{20,28},{24,16},{28,20},{1,9},{5... | collective-permute-start | bytes 1572872 | tf_op jit(solution)/shard_map/ppermute | solution.py:133
  472.1 31.5 %collective-permute-start.62 = (bf16[4,16,4096]{2,1,0:T(8,128)(2,1)S(1)}, bf16[4,16,4096]{2,1,0:T(8,128)(2,1)S(1)}, u32[]{:S(2)}, u32[]{:S(2)}) collective-permute-start(bf16[4,16,4096]{2,1,0:T(8,128)(2,1)S(1)} %fusion.96), channel_id=1, source_target_pairs={{0,16},{4,20},{8,24},{12,28},{16,0},{20,4},{24,8},{28,12},{1,17},{... | collective-permute-start | bytes 1572872 | tf_op jit(solution)/shard_map/ppermute | solution.py:133
  489.3 24.4 %collective-permute-start.71 = (bf16[4,64,1024]{2,1,0:T(8,128)(2,1)S(1)}, bf16[4,64,1024]{2,1,0:T(8,128)(2,1)S(1)}, u32[]{:S(2)}, u32[]{:S(2)}) collective-permute-start(bf16[4,64,1024]{2,1,0:T(8,128)(2,1)S(1)} %fusion.97), channel_id=1, source_target_pairs={{0,8},{4,12},{8,0},{12,4},{16,24},{20,28},{24,16},{28,20},{1,9},{5... | collective-permute-start | bytes 1572872 | tf_op jit(solution)/shard_map/ppermute | solution.py:133
  (118 other events, 1228.6 us)

commit v8 on v7

--- a/solution.py
+++ b/solution.py
@@ -178,7 +178,7 @@
     return jnp.roll(rel, f, axis=0).reshape(n_fsdp * rows, cols), vecs
 
 
-def reduce_chain(grads, n_dp, n_fsdp, direct=False):
+def reduce_chain(grads, n_dp, n_fsdp, direct=False, direct_gather=None):
     d = lax.axis_index("dp")
     f = lax.axis_index("fsdp")
     bits = n_dp.bit_length() - 1
@@ -220,7 +220,9 @@
                 for g, a in zip(got, acc)
             ]
     bits_chip = chip_bits(n_dp)
-    if direct and len(bits_chip) == 2:
+    if direct_gather is None:
+        direct_gather = direct
+    if direct_gather and len(bits_chip) == 2:
         masks = [2, 4, 6]
         got = []
         for mask in masks:
@@ -384,7 +386,7 @@
     )
     if small:
         (grad_down_shard,) = reduce_chain([grad_down_weight], n_dp, n_fsdp)
-        (grad_up_shard,) = reduce_chain([grad_up_weight], n_dp, n_fsdp)
+        (grad_up_shard,) = reduce_chain([grad_up_weight], n_dp, n_fsdp, direct_gather=True)
         (grad_out_shard,) = reduce_chain([grad_out_weight], n_dp, n_fsdp)
         rows = grad_qkv_weight.shape[0] // (n_fsdp * 2 * n_dp)
         slot = vec_grads.shape[1] // (2 * n_dp)

time: 585 us -> 586 us (level)
    ppermute x30 -> x28, waiting for transfers between devices: 66.4 us -> 59.4 us  [exchange(): got = lax.ppermute(leaves, 'dp', xor_pairs(n_dp, 1 << bit))]
    ppermute x3 -> x6, waiting for transfers between devices: 7.48 us -> 13.6 us  [reduce_chain(): got.append(lax.ppermute(send, 'dp', xor_pairs(n_dp, mask)))]
    ppermute x30 -> x28, starting transfers between devices: 26.2 us -> 24.1 us  [exchange(): got = lax.ppermute(leaves, 'dp', xor_pairs(n_dp, 1 << bit))]
    select_n x29 -> x26, other arithmetic: 14.1 us -> 13.9 us  [exchange(): jnp.where(mine, jnp.stack([a, g], axis=pos), jnp.stack([g, a], axis=pos))]
  transfers between devices with their start and end apart: 80 -> 81, of which waited for: 43 -> 44; matrix products, arithmetic and copies ran while one was open for 28% -> 28% of each run, Pallas kernels for 0% -> 0%
where the time goes in v8:
time: 586 us; the launch traced here: 579 us
  waiting for transfers between devices  180 us (31%)
  matrix products  115 us (20%)
  starting transfers between devices  104 us (18%)
  other arithmetic  87.4 us (15%)
  local copies, waits for them, and re-layouts  85.9 us (15%)
  between operations  6.32 us (1%)
    ppermute x20, waiting for transfers between devices, split_bit(): lax.ppermute([v.astype(jnp.bfloat16) for v in send], 'dp', xor_pairs(n_dp...  60.4 us
    ppermute x28, waiting for transfers between devices, exchange(): got = lax.ppermute(leaves, 'dp', xor_pairs(n_dp, 1 << bit))  59.4 us
    ppermute x28, starting transfers between devices, exchange(): got = lax.ppermute(leaves, 'dp', xor_pairs(n_dp, 1 << bit))  24.1 us
    ppermute x9, waiting for transfers between devices, reduce_chain(): got = lax.ppermute(send, 'fsdp', down)  23.9 us
    ppermute x20, starting transfers between devices, split_bit(): lax.ppermute([v.astype(jnp.bfloat16) for v in send], 'dp', xor_pairs(n_dp...  21.1 us
    add x12, other arithmetic, split_bit(): k.astype(jnp.float32) + g.astype(jnp.float32)  19.3 us
    ppermute x9, starting transfers between devices, gather_chain(): got = buf = lax.ppermute(buf, 'fsdp', down)  19.2 us
    concatenate x4, other arithmetic, gather_chain(): return (jnp.roll(rel, f, axis=0).reshape(n_fsdp * rows, cols), vecs)  17 us
  transfers between devices with their start and end apart: 81, of which 44 were waited for; matrix products, arithmetic and copies ran while one was open for 28% of the time, Pallas kernels for 0%

profile of v8, /device:TPU:0, one launch (start us, length us, event | category | flops | bytes accessed | tf_op | source)
XLA Modules:
  0.0 578.7 jit_solution(4546366595744956190)
XLA Ops:
  91.4 7.2 %collective-permute-done.24 = bf16[3,16,4096]{2,1,0:T(8,128)(2,1)S(1)} collective-permute-done((bf16[3,16,4096]{2,1,0:T(8,128)(2,1)S(1)}, bf16[3,16,4096]{2,1,0:T(8,128)(2,1)S(1)}, u32[]{:S(2)}, u32[]{:S(2)}) %collective-permute-start.24) | collective-permute-done | bytes 393248 | tf_op jit(solution)/shard_map/ppermute | solution.py:118
  112.4 7.8 %collective-permute-done.25 = bf16[3,2,16,4096]{3,2,1,0:T(8,128)(2,1)S(1)} collective-permute-done((bf16[3,2,16,4096]{3,2,1,0:T(8,128)(2,1)S(1)}, bf16[3,2,16,4096]{3,2,1,0:T(8,128)(2,1)S(1)}, u32[]{:S(2)}, u32[]{:S(2)}) %collective-permute-start.25) | collective-permute-done | bytes 786464 | tf_op jit(solution)/shard_map/ppermute | solution.py:118
  127.2 9.2 %collective-permute-done.33 = bf16[3,2,64,1024]{3,2,1,0:T(8,128)(2,1)S(1)} collective-permute-done((bf16[3,2,64,1024]{3,2,1,0:T(8,128)(2,1)S(1)}, bf16[3,2,64,1024]{3,2,1,0:T(8,128)(2,1)S(1)}, u32[]{:S(2)}, u32[]{:S(2)}) %collective-permute-start.33) | collective-permute-done | bytes 786464 | tf_op jit(solution)/shard_map/ppermute | solution.py:118
  192.3 5.2 fusion.11
  197.5 6.3 %maximum_select_fusion.1 = bf16[3,2,2,2,2,64,1024]{6,5,4,3,2,1,0:T(8,128)(2,1)S(1)} fusion(bf16[3,2,2,1,2,64,1024]{6,5,4,3,2,1,0:T(8,128)(2,1)} %bitcast.95, bf16[3,2,2,1,2,64,1024]{6,5,4,3,2,1,0:T(8,128)(2,1)S(1)} %copy-done.7, pred[]{:T(512)S(6)} %eq.46), kind=kLoop, calls=%fused_computation.39 | loop fusion | flops 9437184 | bytes 12582913 | tf_op jit(solution)/shard_map/jit(_where)/select_n | solution.py:122
  204.0 5.1 fusion.8
  209.2 10.9 %multiply_convert_fusion = (bf16[600,4096]{1,0:T(8,128)(2,1)}, f32[600,4096]{1,0:T(8,128)}) fusion(f32[4096]{0:T(1024)S(1)} %bitcast.591, bf16[1024,4096]{1,0:T(8,128)(2,1)S(1)} %bitcast.494, f32[600,1024]{1,0:T(8,128)S(1)} %get-tuple-element.97, f32[1024]{0:T(1024)S(1)} %bitcast.598, f32[1024]{0:T(1024)S(1)} %bitcast.583, f32[600]{0:T(1024)S(1)} %add_rsqrt_fusion, ...), kind=kOutput, calls=%fused_computation.19 | convolution fusion | flops 5050982400 | bytes 25621184 | tf_op jit(solution)/shard_map/dot_general | solution.py:338
  220.1 13.0 %fusion.191 = (bf16[4096]{0:T(1024)(128)(2,1)S(1)}, bf16[600,4096]{1,0:T(8,128)(2,1)S(1)}) fusion(f32[600,4096]{1,0:T(8,128)} %get-tuple-element.99, f32[4096]{0:T(1024)S(1)} %bitcast.592, bf16[4096,1024]{1,0:T(8,128)(2,1)S(1)} %bitcast.490, bf16[600,1024]{1,0:T(8,128)(2,1)S(1)} %copy-done.43, f32[]{:T(128)} %bitcast.98), kind=kOutput, calls=%fused_computation.427 | convolution fusion | flops 5064495104 | bytes 24387588 | tf_op jit(solution)/shard_map/dot_general | solution.py:348
  233.1 10.3 %multiply_reduce_fusion.1 = (bf16[1024]{0:T(1024)(128)(2,1)S(1)}, f32[600]{0:T(1024)S(1)}, f32[600]{0:T(1024)S(1)}, bf16[1024]{0:T(1024)(128)(2,1)S(1)}, f32[600,1024]{1,0:T(8,128)S(1)}) fusion(f32[600,1024]{1,0:T(8,128)S(1)} %get-tuple-element.97, f32[600]{0:T(1024)S(1)} %add_rsqrt_fusion, f32[600]{0:T(1024)S(1)} %broadcast_multiply_fusion.4, ...), kind=kOutput, calls=%fused_computation.127 | convolution fusion | flops 5038691328 | bytes 18236800 | tf_op jit(solution)/shard_map/dot_general | solution.py:353
  250.0 9.8 %convolution_convert_fusion = bf16[1024,4096]{1,0:T(8,128)(2,1)} fusion(bf16[600,4096]{1,0:T(8,128)(2,1)S(1)} %bitcast.611, f32[600,1024]{1,0:T(8,128)S(1)} %get-tuple-element.97, f32[1024]{0:T(1024)S(1)} %bitcast.599, f32[1024]{0:T(1024)S(1)} %bitcast.586, f32[600]{0:T(1024)S(1)} %add_rsqrt_fusion, f32[600]{0:T(1024)S(1)} %broadcast_multiply_fusion.4), kind=kOutput, calls=%fused_computation.31 | convolution fusion | flops 5040431104 | bytes 15774400 | tf_op jit(solution)/shard_map/dot_general | solution.py:351
  262.6 6.6 %fusion.190 = (bf16[16,64]{1,0:T(8,128)(2,1)S(1)}, bf16[12,50,16,64]{3,1,2,0:T(8,128)(2,1)}) fusion(f32[12,16,50,50]{2,3,1,0:T(8,128)} %copy-done, f32[12,16,50]{2,1,0:T(8,128)S(1)} %log_add_fusion, bf16[12,50,16,64]{3,2,1,0:T(8,128)(2,1)} %reshape.2175), kind=kOutput, calls=%fused_computation.426 | convolution fusion | flops 63627776 | bytes 4418048 | tf_op jit(solution)/shard_map/chqk,cqhd->ckhd/dot_general | solution.py:88
  278.7 12.7 %convolution_convert_fusion.1 = bf16[4096,1024]{1,0:T(8,128)(2,1)} fusion(bf16[600,4096]{1,0:T(8,128)(2,1)} %get-tuple-element.98, bf16[600,1024]{1,0:T(8,128)(2,1)S(1)} %copy-done.44, f32[]{:T(128)} %bitcast.98), kind=kOutput, calls=%fused_computation.32 | convolution fusion | flops 5039202304 | bytes 14532612 | tf_op jit(solution)/shard_map/dot_general | solution.py:346
  291.5 6.4 %add_convert_fusion.1 = bf16[600,1024]{1,0:T(8,128)(2,1)} fusion(f32[600,1024]{1,0:T(8,128)S(1)} %copy-done.18, bf16[600,4096]{1,0:T(8,128)(2,1)S(1)} %bitcast.613, bf16[4096,1024]{1,0:T(8,128)(2,1)S(1)} %bitcast.493, f32[1024]{0:T(1024)S(1)} %bitcast.597), kind=kOutput, calls=%fused_computation.132 | convolution fusion | flops 5035008000 | bytes 16994304 | tf_op jit(solution)/shard_map/dot_general | solution.py:342
  325.0 9.7 %fusion.52 = (bf16[1024]{0:T(1024)(128)(2,1)S(1)}, f32[600]{0:T(1024)S(1)}, f32[600]{0:T(1024)S(1)}, bf16[1024]{0:T(1024)(128)(2,1)S(1)}, f32[600,1024]{1,0:T(8,128)}) fusion(bf16[600,1024]{1,0:T(8,128)(2,1)S(1)} %copy-done.10, f32[600]{0:T(1024)S(1)} %add_rsqrt_fusion.1, f32[600]{0:T(1024)S(1)} %broadcast_multiply_fusion.5, f32[1024]{0:T(1024)S(1)} %bitcast.588, ...), kind=kOutput, calls=%fused_computation.125 | convolution fusion | flops 3781014528 | bytes 13682048 | tf_op jit(solution)/shard_map/dot_general | solution.py:367
  335.5 7.9 %convolution_convert_fusion.2 = bf16[1024,3072]{1,0:T(8,128)(2,1)S(1)} fusion(bf16[600,3072]{1,0:T(8,128)(2,1)} %constant_dynamic-update-slice_fusion, bf16[600,1024]{1,0:T(8,128)(2,1)S(1)} %copy-done.10, f32[1024]{0:T(1024)S(1)} %bitcast.596, f32[1024]{0:T(1024)S(1)} %bitcast.589, f32[600]{0:T(1024)S(1)} %add_rsqrt_fusion.1, ...), kind=kOutput, calls=%fused_computation.42 | convolution fusion | flops 3781705728 | bytes 11219648 | tf_op jit(solution)/shard_map/dot_general | solution.py:364
  348.0 5.6 collective-permute-done.48
  395.8 14.3 %collective-permute-done.36 = bf16[4,2,16,3200]{3,2,0,1:T(8,128)(2,1)S(1)} collective-permute-done((bf16[4,2,16,3200]{3,2,0,1:T(8,128)(2,1)S(1)}, bf16[4,2,16,3200]{3,2,0,1:T(8,128)(2,1)S(1)}, u32[]{:S(2)}, u32[]{:S(2)}) %collective-permute-start.36) | collective-permute-done | bytes 819232 | tf_op jit(solution)/shard_map/ppermute | solution.py:133
  427.6 5.6 convert_add_fusion
  446.4 6.1 %collective-permute-done.41 = bf16[2,16,3200]{2,1,0:T(8,128)(2,1)} collective-permute-done((bf16[2,16,3200]{2,1,0:T(8,128)(2,1)S(1)}, bf16[2,16,3200]{2,1,0:T(8,128)(2,1)}, u32[]{:S(2)}, u32[]{:S(2)}) %collective-permute-start.41) | collective-permute-done | bytes 204832 | tf_op jit(solution)/shard_map/ppermute | solution.py:206
  473.0 15.7 %collective-permute-done.71 = bf16[4,2,64,1024]{3,2,0,1:T(8,128)(2,1)S(1)} collective-permute-done((bf16[4,2,64,1024]{3,2,0,1:T(8,128)(2,1)S(1)}, bf16[4,2,64,1024]{3,2,0,1:T(8,128)(2,1)S(1)}, u32[]{:S(2)}, u32[]{:S(2)}) %collective-permute-start.71) | collective-permute-done | bytes 1048608 | tf_op jit(solution)/shard_map/ppermute | solution.py:133
  493.7 9.6 %collective-permute-done.60 = bf16[4,16,4096]{2,1,0:T(8,128)(2,1)S(1)} collective-permute-done((bf16[4,16,4096]{2,1,0:T(8,128)(2,1)S(1)}, bf16[4,16,4096]{2,1,0:T(8,128)(2,1)S(1)}, u32[]{:S(2)}, u32[]{:S(2)}) %collective-permute-start.60) | collective-permute-done | bytes 524320 | tf_op jit(solution)/shard_map/ppermute | solution.py:133
  507.5 6.1 %collective-permute-done.72 = bf16[4,64,1024]{2,1,0:T(8,128)(2,1)S(1)} collective-permute-done((bf16[4,64,1024]{2,1,0:T(8,128)(2,1)S(1)}, bf16[4,64,1024]{2,1,0:T(8,128)(2,1)S(1)}, u32[]{:S(2)}, u32[]{:S(2)}) %collective-permute-start.72) | collective-permute-done | bytes 524320 | tf_op jit(solution)/shard_map/ppermute | solution.py:133
  519.7 6.4 %collective-permute-done.75 = bf16[2,64,1024]{2,1,0:T(8,128)(2,1)S(1)} collective-permute-done((bf16[2,64,1024]{2,1,0:T(8,128)(2,1)S(1)}, bf16[2,64,1024]{2,1,0:T(8,128)(2,1)S(1)}, u32[]{:S(2)}, u32[]{:S(2)}) %collective-permute-start.75) | collective-permute-done | bytes 262176 | tf_op jit(solution)/shard_map/ppermute | solution.py:216
  561.5 10.7 %collective-permute-done.79 = bf16[2,2,64,1024]{3,2,1,0:T(8,128)(2,1)S(1)} collective-permute-done((bf16[2,2,64,1024]{3,2,1,0:T(8,128)(2,1)S(1)}, bf16[2,2,64,1024]{3,2,1,0:T(8,128)(2,1)S(1)}, u32[]{:S(2)}, u32[]{:S(2)}) %collective-permute-start.79) | collective-permute-done | bytes 524320 | tf_op jit(solution)/shard_map/ppermute | solution.py:118
  (514 shorter events, 364.5 us)
Async XLA Ops:
  17.9 38.3 %collective-permute-start.5 = (bf16[2,16,3072]{2,1,0:T(8,128)(2,1)S(1)}, bf16[2,16,3072]{2,1,0:T(8,128)(2,1)S(1)}, u32[]{:S(2)}, u32[]{:S(2)}) collective-permute-start(bf16[2,16,3072]{2,1,0:T(8,128)(2,1)S(1)} %dynamic-slice_bitcast_fusion.5), channel_id=1, source_target_pairs={{0,1},{1,2},{2,3},{3,0},{4,5},{5,6},{6,7},{7,4},{8,9},{9,10},{10,1... | collective-permute-start | bytes 589832 | tf_op jit(solution)/shard_map/ppermute | solution.py:152
  18.6 39.1 %collective-permute-start.4 = (bf16[2,16,3072]{2,1,0:T(8,128)(2,1)S(1)}, bf16[2,16,3072]{2,1,0:T(8,128)(2,1)S(1)}, u32[]{:S(2)}, u32[]{:S(2)}) collective-permute-start(bf16[2,16,3072]{2,1,0:T(8,128)(2,1)S(1)} %dynamic-slice_bitcast_fusion.5), channel_id=1, source_target_pairs={{0,2},{1,3},{2,0},{3,1},{4,6},{5,7},{6,4},{7,5},{8,10},{9,11},{10,... | collective-permute-start | bytes 589832 | tf_op jit(solution)/shard_map/ppermute | solution.py:152
  29.8 29.4 %collective-permute-start.3 = (bf16[2,16,3072]{2,1,0:T(8,128)(2,1)S(1)}, bf16[2,16,3072]{2,1,0:T(8,128)(2,1)S(1)}, u32[]{:S(2)}, u32[]{:S(2)}) collective-permute-start(bf16[2,16,3072]{2,1,0:T(8,128)(2,1)S(1)} %dynamic-slice_bitcast_fusion.5), channel_id=1, source_target_pairs={{0,3},{1,0},{2,1},{3,2},{4,7},{5,4},{6,5},{7,6},{8,11},{9,8},{10,9... | collective-permute-start | bytes 589832 | tf_op jit(solution)/shard_map/ppermute | solution.py:152
  34.0 31.6 %collective-permute-start.19 = (bf16[2,16,4096]{2,1,0:T(8,128)(2,1)S(1)}, bf16[2,16,4096]{2,1,0:T(8,128)(2,1)S(1)}, u32[]{:S(2)}, u32[]{:S(2)}) collective-permute-start(bf16[2,16,4096]{2,1,0:T(8,128)(2,1)S(1)} %dynamic-slice_bitcast_fusion.4), channel_id=1, source_target_pairs={{0,3},{1,0},{2,1},{3,2},{4,7},{5,4},{6,5},{7,6},{8,11},{9,8},{10,9... | collective-permute-start | bytes 786440 | tf_op jit(solution)/shard_map/ppermute | solution.py:154
  69.9 38.0 %collective-permute-start.18 = (bf16[3,2,2,2,16,1024]{5,4,3,2,1,0:T(8,128)(2,1)S(1)}, bf16[3,2,2,2,16,1024]{5,4,3,2,1,0:T(8,128)(2,1)S(1)}, u32[]{:S(2)}, u32[]{:S(2)}) collective-permute-start(bf16[3,2,2,2,16,1024]{5,4,3,2,1,0:T(8,128)(2,1)S(1)} %get-tuple-element.61), channel_id=1, source_target_pairs={{0,4},{4,0},{8,12},{12,8},{16,20},{20,16},{24,28},{28,24},{1,5},{5... | collective-permute-start | bytes 2359304 | tf_op jit(solution)/shard_map/ppermute | solution.py:118
  98.6 43.4 %collective-permute-start.10 = (bf16[3,2,2,2,16,3072]{5,4,3,2,1,0:T(8,128)(2,1)S(1)}, bf16[3,2,2,2,16,3072]{5,4,3,2,1,0:T(8,128)(2,1)S(1)}, u32[]{:S(2)}, u32[]{:S(2)}) collective-permute-start(bf16[3,2,2,2,16,3072]{5,4,3,2,1,0:T(8,128)(2,1)S(1)} %get-tuple-element.39), channel_id=1, source_target_pairs={{0,4},{4,0},{8,12},{12,8},{16,20},{20,16},{24,28},{28,24},{1,5},{5... | collective-permute-start | bytes 7077896 | tf_op jit(solution)/shard_map/ppermute | solution.py:118
  98.7 21.4 %collective-permute-start.25 = (bf16[3,2,16,4096]{3,2,1,0:T(8,128)(2,1)S(1)}, bf16[3,2,16,4096]{3,2,1,0:T(8,128)(2,1)S(1)}, u32[]{:S(2)}, u32[]{:S(2)}) collective-permute-start(bf16[3,2,16,4096]{3,2,1,0:T(8,128)(2,1)S(1)} %maximum_select_fusion.18), channel_id=1, source_target_pairs={{0,8},{4,12},{8,0},{12,4},{16,24},{20,28},{24,16},{28,20},{1,9},{5... | collective-permute-start | bytes 2359304 | tf_op jit(solution)/shard_map/ppermute | solution.py:118
  105.5 30.9 %collective-permute-start.33 = (bf16[3,2,64,1024]{3,2,1,0:T(8,128)(2,1)S(1)}, bf16[3,2,64,1024]{3,2,1,0:T(8,128)(2,1)S(1)}, u32[]{:S(2)}, u32[]{:S(2)}) collective-permute-start(bf16[3,2,64,1024]{3,2,1,0:T(8,128)(2,1)S(1)} %maximum_select_fusion.22), channel_id=1, source_target_pairs={{0,8},{4,12},{8,0},{12,4},{16,24},{20,28},{24,16},{28,20},{1,9},{5... | collective-permute-start | bytes 2359304 | tf_op jit(solution)/shard_map/ppermute | solution.py:118
  107.9 31.0 %collective-permute-start.31 = (bf16[3,2,64,1024]{3,2,1,0:T(8,128)(2,1)S(1)}, bf16[3,2,64,1024]{3,2,1,0:T(8,128)(2,1)S(1)}, u32[]{:S(2)}, u32[]{:S(2)}) collective-permute-start(bf16[3,2,64,1024]{3,2,1,0:T(8,128)(2,1)S(1)} %maximum_select_fusion.20), channel_id=1, source_target_pairs={{0,16},{4,20},{8,24},{12,28},{16,0},{20,4},{24,8},{28,12},{1,17},{... | collective-permute-start | bytes 2359304 | tf_op jit(solution)/shard_map/ppermute | solution.py:118
  127.2 60.7 %collective-permute-start.26 = (bf16[3,2,2,2,16,4096]{5,4,3,2,1,0:T(8,128)(2,1)}, bf16[3,2,2,2,16,4096]{5,4,3,2,1,0:T(8,128)(2,1)}, u32[]{:S(2)}, u32[]{:S(2)}) collective-permute-start(bf16[3,2,2,2,16,4096]{5,4,3,2,1,0:T(8,128)(2,1)} %get-tuple-element.37), channel_id=1, source_target_pairs={{0,4},{4,0},{8,12},{12,8},{16,20},{20,16},{24,28},{28,24},{1,5},{5... | collective-permute-start | bytes 9437192 | tf_op jit(solution)/shard_map/ppermute | solution.py:118
  142.0 55.5 %collective-permute-start.34 = (bf16[3,2,2,2,64,1024]{5,4,3,2,1,0:T(8,128)(2,1)}, bf16[3,2,2,2,64,1024]{5,4,3,2,1,0:T(8,128)(2,1)}, u32[]{:S(2)}, u32[]{:S(2)}) collective-permute-start(bf16[3,2,2,2,64,1024]{5,4,3,2,1,0:T(8,128)(2,1)} %get-tuple-element.35), channel_id=1, source_target_pairs={{0,4},{4,0},{8,12},{12,8},{16,20},{20,16},{24,28},{28,24},{1,5},{5... | collective-permute-start | bytes 9437192 | tf_op jit(solution)/shard_map/ppermute | solution.py:118
  300.2 43.3 %collective-permute-start.47 = (bf16[4,2,2,2,16,1024]{5,4,3,2,1,0:T(8,128)(2,1)}, bf16[4,2,2,2,16,1024]{5,4,3,2,1,0:T(8,128)(2,1)}, u32[]{:S(2)}, u32[]{:S(2)}) collective-permute-start(bf16[4,2,2,2,16,1024]{5,4,3,2,1,0:T(8,128)(2,1)} %dynamic-slice_bitcast_fusion.2), channel_id=1, source_target_pairs={{0,4},{4,0},{8,12},{12,8},{16,20},{20,16},{24,28},{28,24},{1,5},{5... | collective-permute-start | bytes 3145736 | tf_op jit(solution)/shard_map/ppermute | solution.py:133
  346.0 39.7 %collective-permute-start.35 = (bf16[4,2,2,2,16,3200]{5,4,3,2,1,0:T(8,128)(2,1)S(1)}, bf16[4,2,2,2,16,3200]{5,4,3,2,1,0:T(8,128)(2,1)}, u32[]{:S(2)}, u32[]{:S(2)}) collective-permute-start(bf16[4,2,2,2,16,3200]{5,4,3,2,1,0:T(8,128)(2,1)S(1)} %fusion.18), channel_id=1, source_target_pairs={{0,4},{4,0},{8,12},{12,8},{16,20},{20,16},{24,28},{28,24},{1,5},{5... | collective-permute-start | bytes 9830408 | tf_op jit(solution)/shard_map/ppermute | solution.py:133
  379.5 38.3 %collective-permute-start.58 = (bf16[4,2,2,2,16,4096]{5,4,3,2,1,0:T(8,128)(2,1)}, bf16[4,2,2,2,16,4096]{5,4,3,2,1,0:T(8,128)(2,1)}, u32[]{:S(2)}, u32[]{:S(2)}) collective-permute-start(bf16[4,2,2,2,16,4096]{5,4,3,2,1,0:T(8,128)(2,1)} %dynamic-slice_bitcast_fusion.1), channel_id=1, source_target_pairs={{0,4},{4,0},{8,12},{12,8},{16,20},{20,16},{24,28},{28,24},{1,5},{5... | collective-permute-start | bytes 12582920 | tf_op jit(solution)/shard_map/ppermute | solution.py:133
  379.5 48.1 %collective-permute-start.70 = (bf16[4,2,2,2,64,1024]{5,4,3,2,1,0:T(8,128)(2,1)}, bf16[4,2,2,2,64,1024]{5,4,3,2,1,0:T(8,128)(2,1)}, u32[]{:S(2)}, u32[]{:S(2)}) collective-permute-start(bf16[4,2,2,2,64,1024]{5,4,3,2,1,0:T(8,128)(2,1)} %dynamic-slice_bitcast_fusion), channel_id=1, source_target_pairs={{0,4},{4,0},{8,12},{12,8},{16,20},{20,16},{24,28},{28,24},{1,5},{5... | collective-permute-start | bytes 12582920 | tf_op jit(solution)/shard_map/ppermute | solution.py:133
  410.3 23.0 %collective-permute-start.37 = (bf16[4,16,3200]{2,1,0:T(8,128)(2,1)S(1)}, bf16[4,16,3200]{2,1,0:T(8,128)(2,1)}, u32[]{:S(2)}, u32[]{:S(2)}) collective-permute-start(bf16[4,16,3200]{2,1,0:T(8,128)(2,1)S(1)} %fusion.128), channel_id=1, source_target_pairs={{0,8},{4,12},{8,0},{12,4},{16,24},{20,28},{24,16},{28,20},{1,9},{5... | collective-permute-start | bytes 1228808 | tf_op jit(solution)/shard_map/ppermute | solution.py:133
  425.0 43.3 %collective-permute-start.59 = (bf16[4,2,16,4096]{3,2,0,1:T(8,128)(2,1)}, bf16[4,2,16,4096]{3,2,0,1:T(8,128)(2,1)}, u32[]{:S(2)}, u32[]{:S(2)}) collective-permute-start(bf16[4,2,16,4096]{3,2,0,1:T(8,128)(2,1)} %fusion.78), channel_id=1, source_target_pairs={{0,16},{4,20},{8,24},{12,28},{16,0},{20,4},{24,8},{28,12},{1,17},{... | collective-permute-start | bytes 3145736 | tf_op jit(solution)/shard_map/ppermute | solution.py:133
  427.2 43.2 %collective-permute-start.61 = (bf16[4,2,16,4096]{3,2,1,0:T(8,128)(2,1)}, bf16[4,2,16,4096]{3,2,1,0:T(8,128)(2,1)}, u32[]{:S(2)}, u32[]{:S(2)}) collective-permute-start(bf16[4,2,16,4096]{3,2,1,0:T(8,128)(2,1)} %fusion.76), channel_id=1, source_target_pairs={{0,8},{4,12},{8,0},{12,4},{16,24},{20,28},{24,16},{28,20},{1,9},{5... | collective-permute-start | bytes 3145736 | tf_op jit(solution)/shard_map/ppermute | solution.py:133
  462.7 26.0 %collective-permute-start.71 = (bf16[4,2,64,1024]{3,2,0,1:T(8,128)(2,1)S(1)}, bf16[4,2,64,1024]{3,2,0,1:T(8,128)(2,1)S(1)}, u32[]{:S(2)}, u32[]{:S(2)}) collective-permute-start(bf16[4,2,64,1024]{3,2,0,1:T(8,128)(2,1)S(1)} %fusion.79), channel_id=1, source_target_pairs={{0,16},{4,20},{8,24},{12,28},{16,0},{20,4},{24,8},{28,12},{1,17},{... | collective-permute-start | bytes 3145736 | tf_op jit(solution)/shard_map/ppermute | solution.py:133
  466.1 26.0 %collective-permute-start.73 = (bf16[4,2,64,1024]{3,2,1,0:T(8,128)(2,1)S(1)}, bf16[4,2,64,1024]{3,2,1,0:T(8,128)(2,1)S(1)}, u32[]{:S(2)}, u32[]{:S(2)}) collective-permute-start(bf16[4,2,64,1024]{3,2,1,0:T(8,128)(2,1)S(1)} %fusion.77), channel_id=1, source_target_pairs={{0,8},{4,12},{8,0},{12,4},{16,24},{20,28},{24,16},{28,20},{1,9},{5... | collective-permute-start | bytes 3145736 | tf_op jit(solution)/shard_map/ppermute | solution.py:133
  468.1 51.4 %collective-permute-start.46 = (bf16[2,2,2,16,3200]{4,3,2,1,0:T(8,128)(2,1)S(1)}, bf16[2,2,2,16,3200]{4,3,2,1,0:T(8,128)(2,1)S(1)}, u32[]{:S(2)}, u32[]{:S(2)}) collective-permute-start(bf16[2,2,2,16,3200]{4,3,2,1,0:T(8,128)(2,1)S(1)} %reverse_select_fusion.2), channel_id=1, source_target_pairs={{0,4},{4,0},{8,12},{12,8},{16,20},{20,16},{24,28},{28,24},{1,5},{5... | collective-permute-start | bytes 2457608 | tf_op jit(solution)/shard_map/ppermute | solution.py:118
  469.9 33.5 %collective-permute-start.60 = (bf16[4,16,4096]{2,1,0:T(8,128)(2,1)S(1)}, bf16[4,16,4096]{2,1,0:T(8,128)(2,1)S(1)}, u32[]{:S(2)}, u32[]{:S(2)}) collective-permute-start(bf16[4,16,4096]{2,1,0:T(8,128)(2,1)S(1)} %fusion.94), channel_id=1, source_target_pairs={{0,8},{4,12},{8,0},{12,4},{16,24},{20,28},{24,16},{28,20},{1,9},{5... | collective-permute-start | bytes 1572872 | tf_op jit(solution)/shard_map/ppermute | solution.py:133
  472.0 31.5 %collective-permute-start.62 = (bf16[4,16,4096]{2,1,0:T(8,128)(2,1)S(1)}, bf16[4,16,4096]{2,1,0:T(8,128)(2,1)S(1)}, u32[]{:S(2)}, u32[]{:S(2)}) collective-permute-start(bf16[4,16,4096]{2,1,0:T(8,128)(2,1)S(1)} %fusion.95), channel_id=1, source_target_pairs={{0,16},{4,20},{8,24},{12,28},{16,0},{20,4},{24,8},{28,12},{1,17},{... | collective-permute-start | bytes 1572872 | tf_op jit(solution)/shard_map/ppermute | solution.py:133
  489.1 24.4 %collective-permute-start.72 = (bf16[4,64,1024]{2,1,0:T(8,128)(2,1)S(1)}, bf16[4,64,1024]{2,1,0:T(8,128)(2,1)S(1)}, u32[]{:S(2)}, u32[]{:S(2)}) collective-permute-start(bf16[4,64,1024]{2,1,0:T(8,128)(2,1)S(1)} %fusion.96), channel_id=1, source_target_pairs={{0,8},{4,12},{8,0},{12,4},{16,24},{20,28},{24,16},{28,20},{1,9},{5... | collective-permute-start | bytes 1572872 | tf_op jit(solution)/shard_map/ppermute | solution.py:133
  (119 other events, 1249.8 us)

commit v9 on v8

--- a/solution.py
+++ b/solution.py
@@ -161,6 +161,17 @@
     if n_fsdp == 1:
         return shard, vecs
     zrel = jnp.stack(ring, axis=0)
+    if direct and len(chip_bits(n_dp)) == 2:
+        got = []
+        for mask in [2, 4, 6]:
+            got.append(lax.ppermute(zrel, "dp", xor_pairs(n_dp, mask)))
+        cand = jnp.stack([zrel] + got, axis=1).reshape((n_fsdp - 1, 2, 2) + zrel.shape[1:])
+        cand = jnp.where(((d >> 2) & 1) == 1, cand[:, ::-1], cand)
+        both = jnp.where(((d >> 1) & 1) == 1, cand[:, :, ::-1], cand)
+        (both,), _ = exchange([both], [2, 1], 0, d, n_dp, 1)
+        plane = both.reshape((n_fsdp - 1, n_dp) + both.shape[-3:])
+        rel = jnp.concatenate([pieces[None], plane], axis=0)
+        return jnp.roll(rel, f, axis=0).reshape(n_fsdp * rows, cols), vecs
     halves = []
     for h in range(2):
         order = chip_bits(n_dp)
@@ -387,7 +398,7 @@
     if small:
         (grad_down_shard,) = reduce_chain([grad_down_weight], n_dp, n_fsdp)
         (grad_up_shard,) = reduce_chain([grad_up_weight], n_dp, n_fsdp, direct_gather=True)
-        (grad_out_shard,) = reduce_chain([grad_out_weight], n_dp, n_fsdp)
+        (grad_out_shard,) = reduce_chain([grad_out_weight], n_dp, n_fsdp, direct_gather=True)
         rows = grad_qkv_weight.shape[0] // (n_fsdp * 2 * n_dp)
         slot = vec_grads.shape[1] // (2 * n_dp)
         if slot % rows == 0:

time: 586 us -> 587 us (level)
  local copies, waits for them, and re-layouts: 85.9 us -> 77.7 us
  waiting for transfers between devices: 180 us -> 186 us
    ppermute x0 -> x3, waiting for transfers between devices: none -> 11.2 us  [gather_chain(): got.append(lax.ppermute(zrel, 'dp', xor_pairs(n_dp, mask)))]
    ppermute x28 -> x22, waiting for transfers between devices: 59.4 us -> 48.6 us  [exchange(): got = lax.ppermute(leaves, 'dp', xor_pairs(n_dp, 1 << bit))]
    ppermute x28 -> x22, starting transfers between devices: 24.1 us -> 17.1 us  [exchange(): got = lax.ppermute(leaves, 'dp', xor_pairs(n_dp, 1 << bit))]
    ppermute x6 -> x9, waiting for transfers between devices: 13.6 us -> 16.4 us  [reduce_chain(): got.append(lax.ppermute(send, 'dp', xor_pairs(n_dp, mask)))]
    unnamed x151 -> x143, local copies, waits for them, and re-layouts: 16.4 us -> 17 us
    select_n x26 -> x20, other arithmetic: 13.9 us -> 13.5 us  [exchange(): jnp.where(mine, jnp.stack([a, g], axis=pos), jnp.stack([g, a], axis=pos))]
  transfers between devices with their start and end apart: 81 -> 81, of which waited for: 44 -> 44; matrix products, arithmetic and copies ran while one was open for 28% -> 24% of each run, Pallas kernels for 0% -> 0%
where the time goes in v9:
time: 587 us; the launch traced here: 580 us
  waiting for transfers between devices  186 us (32%)
  matrix products  115 us (20%)
  starting transfers between devices  104 us (18%)
  other arithmetic  90.7 us (15%)
  local copies, waits for them, and re-layouts  77.7 us (13%)
  between operations  6.28 us (1%)
    ppermute x20, waiting for transfers between devices, split_bit(): lax.ppermute([v.astype(jnp.bfloat16) for v in send], 'dp', xor_pairs(n_dp...  63.2 us
    ppermute x22, waiting for transfers between devices, exchange(): got = lax.ppermute(leaves, 'dp', xor_pairs(n_dp, 1 << bit))  48.6 us
    ppermute x9, starting transfers between devices, gather_chain(): got = buf = lax.ppermute(buf, 'fsdp', down)  24.1 us
    ppermute x9, waiting for transfers between devices, reduce_chain(): got = lax.ppermute(send, 'fsdp', down)  23.2 us
    add x12, other arithmetic, split_bit(): k.astype(jnp.float32) + g.astype(jnp.float32)  18 us
    ppermute x22, starting transfers between devices, exchange(): got = lax.ppermute(leaves, 'dp', xor_pairs(n_dp, 1 << bit))  17.1 us
    unnamed x143, local copies, waits for them, and re-layouts  17 us
    concatenate x4, other arithmetic, gather_chain(): return (jnp.roll(rel, f, axis=0).reshape(n_fsdp * rows, cols), vecs)  16.8 us
  transfers between devices with their start and end apart: 81, of which 44 were waited for; matrix products, arithmetic and copies ran while one was open for 24% of the time, Pallas kernels for 0%

profile of v9, /device:TPU:0, one launch (start us, length us, event | category | flops | bytes accessed | tf_op | source)
XLA Modules:
  0.0 580.1 jit_solution(14659796485135720178)
XLA Ops:
  80.1 5.9 %collective-permute-done.28 = bf16[2,64,1024]{2,1,0:T(8,128)(2,1)S(1)} collective-permute-done((bf16[2,64,1024]{2,1,0:T(8,128)(2,1)S(1)}, bf16[2,64,1024]{2,1,0:T(8,128)(2,1)S(1)}, u32[]{:S(2)}, u32[]{:S(2)}) %collective-permute-start.28) | collective-permute-done | bytes 262176 | tf_op jit(solution)/shard_map/ppermute | solution.py:154
  89.0 11.2 %collective-permute-done.8 = bf16[3,2,16,3072]{3,2,1,0:T(8,128)(2,1)S(1)} collective-permute-done((bf16[3,2,16,3072]{3,2,1,0:T(8,128)(2,1)S(1)}, bf16[3,2,16,3072]{3,2,1,0:T(8,128)(2,1)S(1)}, u32[]{:S(2)}, u32[]{:S(2)}) %collective-permute-start.8) | collective-permute-done | bytes 589856 | tf_op jit(solution)/shard_map/ppermute | solution.py:167
  120.6 8.8 %collective-permute-done.24 = bf16[3,2,16,4096]{3,2,1,0:T(8,128)(2,1)S(1)} collective-permute-done((bf16[3,2,16,4096]{3,2,1,0:T(8,128)(2,1)S(1)}, bf16[3,2,16,4096]{3,2,1,0:T(8,128)(2,1)S(1)}, u32[]{:S(2)}, u32[]{:S(2)}) %collective-permute-start.24) | collective-permute-done | bytes 786464 | tf_op jit(solution)/shard_map/ppermute | solution.py:118
  134.6 9.0 %collective-permute-done.32 = bf16[3,2,64,1024]{3,2,1,0:T(8,128)(2,1)S(1)} collective-permute-done((bf16[3,2,64,1024]{3,2,1,0:T(8,128)(2,1)S(1)}, bf16[3,2,64,1024]{3,2,1,0:T(8,128)(2,1)S(1)}, u32[]{:S(2)}, u32[]{:S(2)}) %collective-permute-start.32) | collective-permute-done | bytes 786464 | tf_op jit(solution)/shard_map/ppermute | solution.py:118
  200.5 5.2 fusion.11
  205.7 6.3 %maximum_select_fusion.1 = bf16[3,2,2,2,2,64,1024]{6,5,4,3,2,1,0:T(8,128)(2,1)S(1)} fusion(bf16[3,2,2,1,2,64,1024]{6,5,4,3,2,1,0:T(8,128)(2,1)} %bitcast.89, bf16[3,2,2,1,2,64,1024]{6,5,4,3,2,1,0:T(8,128)(2,1)S(1)} %copy-done.7, pred[]{:T(512)S(6)} %eq.46), kind=kLoop, calls=%fused_computation.39 | loop fusion | flops 9437184 | bytes 12582913 | tf_op jit(solution)/shard_map/jit(_where)/select_n | solution.py:122
  217.4 10.6 %multiply_convert_fusion = (bf16[600,4096]{1,0:T(8,128)(2,1)}, f32[600,4096]{1,0:T(8,128)}) fusion(f32[4096]{0:T(1024)S(1)} %bitcast.573, bf16[1024,4096]{1,0:T(8,128)(2,1)S(1)} %bitcast.484, f32[600,1024]{1,0:T(8,128)S(1)} %get-tuple-element.90, f32[1024]{0:T(1024)S(1)} %bitcast.580, f32[1024]{0:T(1024)S(1)} %bitcast.565, f32[600]{0:T(1024)S(1)} %add_rsqrt_fusion, ...), kind=kOutput, calls=%fused_computation.19 | convolution fusion | flops 5050982400 | bytes 25621184 | tf_op jit(solution)/shard_map/dot_general | solution.py:349
  227.9 13.0 %fusion.189 = (bf16[4096]{0:T(1024)(128)(2,1)S(1)}, bf16[600,4096]{1,0:T(8,128)(2,1)S(1)}) fusion(f32[600,4096]{1,0:T(8,128)} %get-tuple-element.92, f32[4096]{0:T(1024)S(1)} %bitcast.574, bf16[4096,1024]{1,0:T(8,128)(2,1)S(1)} %bitcast.482, bf16[600,1024]{1,0:T(8,128)(2,1)S(1)} %copy-done.44, f32[]{:T(128)} %bitcast.92), kind=kOutput, calls=%fused_computation.414 | convolution fusion | flops 5064495104 | bytes 24387588 | tf_op jit(solution)/shard_map/dot_general | solution.py:359
  240.9 10.3 %multiply_reduce_fusion.1 = (bf16[1024]{0:T(1024)(128)(2,1)S(1)}, f32[600]{0:T(1024)S(1)}, f32[600]{0:T(1024)S(1)}, bf16[1024]{0:T(1024)(128)(2,1)S(1)}, f32[600,1024]{1,0:T(8,128)S(1)}) fusion(f32[600,1024]{1,0:T(8,128)S(1)} %get-tuple-element.90, f32[600]{0:T(1024)S(1)} %add_rsqrt_fusion, f32[600]{0:T(1024)S(1)} %broadcast_multiply_fusion.4, ...), kind=kOutput, calls=%fused_computation.129 | convolution fusion | flops 5038691328 | bytes 18236800 | tf_op jit(solution)/shard_map/dot_general | solution.py:364
  258.1 9.6 %convolution_convert_fusion = bf16[1024,4096]{1,0:T(8,128)(2,1)} fusion(bf16[600,4096]{1,0:T(8,128)(2,1)S(1)} %bitcast.593, f32[600,1024]{1,0:T(8,128)S(1)} %get-tuple-element.90, f32[1024]{0:T(1024)S(1)} %bitcast.581, f32[1024]{0:T(1024)S(1)} %bitcast.568, f32[600]{0:T(1024)S(1)} %add_rsqrt_fusion, f32[600]{0:T(1024)S(1)} %broadcast_multiply_fusion.4), kind=kOutput, calls=%fused_computation.31 | convolution fusion | flops 5040431104 | bytes 15774400 | tf_op jit(solution)/shard_map/dot_general | solution.py:362
  270.5 6.6 %fusion.188 = (bf16[16,64]{1,0:T(8,128)(2,1)S(1)}, bf16[12,50,16,64]{3,1,2,0:T(8,128)(2,1)}) fusion(f32[12,16,50,50]{2,3,1,0:T(8,128)} %copy-done, f32[12,16,50]{2,1,0:T(8,128)S(1)} %log_add_fusion, bf16[12,50,16,64]{3,2,1,0:T(8,128)(2,1)} %reshape.1658), kind=kOutput, calls=%fused_computation.413 | convolution fusion | flops 63627776 | bytes 4418048 | tf_op jit(solution)/shard_map/chqk,cqhd->ckhd/dot_general | solution.py:88
  309.7 9.8 %fusion.52 = (bf16[1024]{0:T(1024)(128)(2,1)S(1)}, f32[600]{0:T(1024)S(1)}, f32[600]{0:T(1024)S(1)}, bf16[1024]{0:T(1024)(128)(2,1)S(1)}, f32[600,1024]{1,0:T(8,128)}) fusion(bf16[600,1024]{1,0:T(8,128)(2,1)S(1)} %copy-done.10, f32[600]{0:T(1024)S(1)} %add_rsqrt_fusion.1, f32[600]{0:T(1024)S(1)} %broadcast_multiply_fusion.5, f32[1024]{0:T(1024)S(1)} %bitcast.570, ...), kind=kOutput, calls=%fused_computation.127 | convolution fusion | flops 3781014528 | bytes 13682048 | tf_op jit(solution)/shard_map/dot_general | solution.py:378
  319.5 7.6 %convolution_convert_fusion.2 = bf16[1024,3072]{1,0:T(8,128)(2,1)} fusion(bf16[600,3072]{1,0:T(8,128)(2,1)S(1)} %copy-done.46, bf16[600,1024]{1,0:T(8,128)(2,1)S(1)} %copy-done.10, f32[1024]{0:T(1024)S(1)} %bitcast.579, f32[1024]{0:T(1024)S(1)} %bitcast.571, f32[600]{0:T(1024)S(1)} %add_rsqrt_fusion.1, f32[600]{0:T(1024)S(1)} %broadcast_multiply_fusion.5), kind=kOutput, calls=%fused_computation.42 | convolution fusion | flops 3781705728 | bytes 11219648 | tf_op jit(solution)/shard_map/dot_general | solution.py:375
  332.4 10.1 %add_convert_fusion.1 = bf16[600,1024]{1,0:T(8,128)(2,1)} fusion(f32[600,1024]{1,0:T(8,128)S(1)} %copy-done.18, bf16[600,4096]{1,0:T(8,128)(2,1)} %get-tuple-element.91, bf16[4096,1024]{1,0:T(8,128)(2,1)} %bitcast.483, f32[1024]{0:T(1024)S(1)} %bitcast.577), kind=kOutput, calls=%fused_computation.134 | convolution fusion | flops 5035008000 | bytes 16994304 | tf_op jit(solution)/shard_map/dot_general | solution.py:353
  342.5 9.8 %convolution_convert_fusion.1 = bf16[4096,1024]{1,0:T(8,128)(2,1)S(1)} fusion(bf16[600,4096]{1,0:T(8,128)(2,1)} %get-tuple-element.91, bf16[600,1024]{1,0:T(8,128)(2,1)S(1)} %copy-done.45, f32[]{:T(128)} %bitcast.92), kind=kOutput, calls=%fused_computation.32 | convolution fusion | flops 5039202304 | bytes 14532612 | tf_op jit(solution)/shard_map/dot_general | solution.py:357
  354.8 6.8 %collective-permute-done.47 = bf16[4,2,16,1024]{3,2,0,1:T(8,128)(2,1)S(1)} collective-permute-done((bf16[4,2,16,1024]{3,2,0,1:T(8,128)(2,1)S(1)}, bf16[4,2,16,1024]{3,2,0,1:T(8,128)(2,1)S(1)}, u32[]{:S(2)}, u32[]{:S(2)}) %collective-permute-start.47) | collective-permute-done | bytes 262176 | tf_op jit(solution)/shard_map/ppermute | solution.py:133
  397.3 16.4 %collective-permute-done.35 = bf16[4,2,16,3200]{3,2,0,1:T(8,128)(2,1)S(1)} collective-permute-done((bf16[4,2,16,3200]{3,2,0,1:T(8,128)(2,1)S(1)}, bf16[4,2,16,3200]{3,2,0,1:T(8,128)(2,1)S(1)}, u32[]{:S(2)}, u32[]{:S(2)}) %collective-permute-start.35) | collective-permute-done | bytes 819232 | tf_op jit(solution)/shard_map/ppermute | solution.py:133
  428.6 5.6 convert_add_fusion
  447.2 6.5 %collective-permute-done.40 = bf16[2,16,3200]{2,1,0:T(8,128)(2,1)} collective-permute-done((bf16[2,16,3200]{2,1,0:T(8,128)(2,1)S(1)}, bf16[2,16,3200]{2,1,0:T(8,128)(2,1)}, u32[]{:S(2)}, u32[]{:S(2)}) %collective-permute-start.40) | collective-permute-done | bytes 204832 | tf_op jit(solution)/shard_map/ppermute | solution.py:217
  474.4 15.7 %collective-permute-done.71 = bf16[4,2,64,1024]{3,2,0,1:T(8,128)(2,1)S(1)} collective-permute-done((bf16[4,2,64,1024]{3,2,0,1:T(8,128)(2,1)S(1)}, bf16[4,2,64,1024]{3,2,0,1:T(8,128)(2,1)S(1)}, u32[]{:S(2)}, u32[]{:S(2)}) %collective-permute-start.71) | collective-permute-done | bytes 1048608 | tf_op jit(solution)/shard_map/ppermute | solution.py:133
  495.1 9.6 %collective-permute-done.60 = bf16[4,16,4096]{2,1,0:T(8,128)(2,1)S(1)} collective-permute-done((bf16[4,16,4096]{2,1,0:T(8,128)(2,1)S(1)}, bf16[4,16,4096]{2,1,0:T(8,128)(2,1)S(1)}, u32[]{:S(2)}, u32[]{:S(2)}) %collective-permute-start.60) | collective-permute-done | bytes 524320 | tf_op jit(solution)/shard_map/ppermute | solution.py:133
  508.1 6.7 %collective-permute-done.72 = bf16[4,64,1024]{2,1,0:T(8,128)(2,1)S(1)} collective-permute-done((bf16[4,64,1024]{2,1,0:T(8,128)(2,1)S(1)}, bf16[4,64,1024]{2,1,0:T(8,128)(2,1)S(1)}, u32[]{:S(2)}, u32[]{:S(2)}) %collective-permute-start.72) | collective-permute-done | bytes 524320 | tf_op jit(solution)/shard_map/ppermute | solution.py:133
  521.0 6.4 %collective-permute-done.75 = bf16[2,64,1024]{2,1,0:T(8,128)(2,1)S(1)} collective-permute-done((bf16[2,64,1024]{2,1,0:T(8,128)(2,1)S(1)}, bf16[2,64,1024]{2,1,0:T(8,128)(2,1)S(1)}, u32[]{:S(2)}, u32[]{:S(2)}) %collective-permute-start.75) | collective-permute-done | bytes 262176 | tf_op jit(solution)/shard_map/ppermute | solution.py:227
  562.7 10.8 %collective-permute-done.79 = bf16[2,2,64,1024]{3,2,1,0:T(8,128)(2,1)S(1)} collective-permute-done((bf16[2,2,64,1024]{3,2,1,0:T(8,128)(2,1)S(1)}, bf16[2,2,64,1024]{3,2,1,0:T(8,128)(2,1)S(1)}, u32[]{:S(2)}, u32[]{:S(2)}) %collective-permute-start.79) | collective-permute-done | bytes 524320 | tf_op jit(solution)/shard_map/ppermute | solution.py:118
  (500 shorter events, 355.8 us)
Async XLA Ops:
  17.9 38.3 %collective-permute-start.5 = (bf16[2,16,3072]{2,1,0:T(8,128)(2,1)S(1)}, bf16[2,16,3072]{2,1,0:T(8,128)(2,1)S(1)}, u32[]{:S(2)}, u32[]{:S(2)}) collective-permute-start(bf16[2,16,3072]{2,1,0:T(8,128)(2,1)S(1)} %dynamic-slice_bitcast_fusion.5), channel_id=1, source_target_pairs={{0,1},{1,2},{2,3},{3,0},{4,5},{5,6},{6,7},{7,4},{8,9},{9,10},{10,1... | collective-permute-start | bytes 589832 | tf_op jit(solution)/shard_map/ppermute | solution.py:152
  18.6 39.2 %collective-permute-start.4 = (bf16[2,16,3072]{2,1,0:T(8,128)(2,1)S(1)}, bf16[2,16,3072]{2,1,0:T(8,128)(2,1)S(1)}, u32[]{:S(2)}, u32[]{:S(2)}) collective-permute-start(bf16[2,16,3072]{2,1,0:T(8,128)(2,1)S(1)} %dynamic-slice_bitcast_fusion.5), channel_id=1, source_target_pairs={{0,2},{1,3},{2,0},{3,1},{4,6},{5,7},{6,4},{7,5},{8,10},{9,11},{10,... | collective-permute-start | bytes 589832 | tf_op jit(solution)/shard_map/ppermute | solution.py:152
  29.9 29.4 %collective-permute-start.3 = (bf16[2,16,3072]{2,1,0:T(8,128)(2,1)S(1)}, bf16[2,16,3072]{2,1,0:T(8,128)(2,1)S(1)}, u32[]{:S(2)}, u32[]{:S(2)}) collective-permute-start(bf16[2,16,3072]{2,1,0:T(8,128)(2,1)S(1)} %dynamic-slice_bitcast_fusion.5), channel_id=1, source_target_pairs={{0,3},{1,0},{2,1},{3,2},{4,7},{5,4},{6,5},{7,6},{8,11},{9,8},{10,9... | collective-permute-start | bytes 589832 | tf_op jit(solution)/shard_map/ppermute | solution.py:152
  34.1 25.8 %collective-permute-start.18 = (bf16[2,16,4096]{2,1,0:T(8,128)(2,1)S(1)}, bf16[2,16,4096]{2,1,0:T(8,128)(2,1)S(1)}, u32[]{:S(2)}, u32[]{:S(2)}) collective-permute-start(bf16[2,16,4096]{2,1,0:T(8,128)(2,1)S(1)} %dynamic-slice_bitcast_fusion.4), channel_id=1, source_target_pairs={{0,3},{1,0},{2,1},{3,2},{4,7},{5,4},{6,5},{7,6},{8,11},{9,8},{10,9... | collective-permute-start | bytes 786440 | tf_op jit(solution)/shard_map/ppermute | solution.py:154
  59.4 28.4 %collective-permute-start.7 = (bf16[3,2,16,3072]{3,2,1,0:T(8,128)(2,1)S(1)}, bf16[3,2,16,3072]{3,2,1,0:T(8,128)(2,1)S(1)}, u32[]{:S(2)}, u32[]{:S(2)}) collective-permute-start(bf16[3,2,16,3072]{3,2,1,0:T(8,128)(2,1)S(1)} %get-tuple-element.61), channel_id=1, source_target_pairs={{0,16},{4,20},{8,24},{12,28},{16,0},{20,4},{24,8},{28,12},{1,17},{... | collective-permute-start | bytes 1769480 | tf_op jit(solution)/shard_map/ppermute | solution.py:167
  75.1 25.0 %collective-permute-start.8 = (bf16[3,2,16,3072]{3,2,1,0:T(8,128)(2,1)S(1)}, bf16[3,2,16,3072]{3,2,1,0:T(8,128)(2,1)S(1)}, u32[]{:S(2)}, u32[]{:S(2)}) collective-permute-start(bf16[3,2,16,3072]{3,2,1,0:T(8,128)(2,1)S(1)} %get-tuple-element.61), channel_id=1, source_target_pairs={{0,24},{4,28},{8,16},{12,20},{16,8},{20,12},{24,0},{28,4},{1,25},{... | collective-permute-start | bytes 1769480 | tf_op jit(solution)/shard_map/ppermute | solution.py:167
  76.9 38.3 %collective-permute-start.17 = (bf16[3,2,2,2,16,1024]{5,4,3,2,1,0:T(8,128)(2,1)S(1)}, bf16[3,2,2,2,16,1024]{5,4,3,2,1,0:T(8,128)(2,1)S(1)}, u32[]{:S(2)}, u32[]{:S(2)}) collective-permute-start(bf16[3,2,2,2,16,1024]{5,4,3,2,1,0:T(8,128)(2,1)S(1)} %get-tuple-element.59), channel_id=1, source_target_pairs={{0,4},{4,0},{8,12},{12,8},{16,20},{20,16},{24,28},{28,24},{1,5},{5... | collective-permute-start | bytes 2359304 | tf_op jit(solution)/shard_map/ppermute | solution.py:118
  88.4 24.1 %collective-permute-start.29 = (bf16[3,64,1024]{2,1,0:T(8,128)(2,1)S(1)}, bf16[3,64,1024]{2,1,0:T(8,128)(2,1)S(1)}, u32[]{:S(2)}, u32[]{:S(2)}) collective-permute-start(bf16[3,64,1024]{2,1,0:T(8,128)(2,1)S(1)} %get-tuple-element.45), channel_id=1, source_target_pairs={{0,8},{4,12},{8,0},{12,4},{16,24},{20,28},{24,16},{28,20},{1,9},{5... | collective-permute-start | bytes 1179656 | tf_op jit(solution)/shard_map/ppermute | solution.py:118
  104.2 46.3 %collective-permute-start.9 = (bf16[3,2,2,2,16,3072]{5,4,3,2,1,0:T(8,128)(2,1)S(1)}, bf16[3,2,2,2,16,3072]{5,4,3,2,1,0:T(8,128)(2,1)S(1)}, u32[]{:S(2)}, u32[]{:S(2)}) collective-permute-start(bf16[3,2,2,2,16,3072]{5,4,3,2,1,0:T(8,128)(2,1)S(1)} %reverse_select_fusion), channel_id=1, source_target_pairs={{0,4},{4,0},{8,12},{12,8},{16,20},{20,16},{24,28},{28,24},{1,5},{5... | collective-permute-start | bytes 7077896 | tf_op jit(solution)/shard_map/ppermute | solution.py:118
  112.5 31.2 %collective-permute-start.32 = (bf16[3,2,64,1024]{3,2,1,0:T(8,128)(2,1)S(1)}, bf16[3,2,64,1024]{3,2,1,0:T(8,128)(2,1)S(1)}, u32[]{:S(2)}, u32[]{:S(2)}) collective-permute-start(bf16[3,2,64,1024]{3,2,1,0:T(8,128)(2,1)S(1)} %maximum_select_fusion.20), channel_id=1, source_target_pairs={{0,8},{4,12},{8,0},{12,4},{16,24},{20,28},{24,16},{28,20},{1,9},{5... | collective-permute-start | bytes 2359304 | tf_op jit(solution)/shard_map/ppermute | solution.py:118
  115.2 32.1 %collective-permute-start.30 = (bf16[3,2,64,1024]{3,2,1,0:T(8,128)(2,1)S(1)}, bf16[3,2,64,1024]{3,2,1,0:T(8,128)(2,1)S(1)}, u32[]{:S(2)}, u32[]{:S(2)}) collective-permute-start(bf16[3,2,64,1024]{3,2,1,0:T(8,128)(2,1)S(1)} %maximum_select_fusion.18), channel_id=1, source_target_pairs={{0,16},{4,20},{8,24},{12,28},{16,0},{20,4},{24,8},{28,12},{1,17},{... | collective-permute-start | bytes 2359304 | tf_op jit(solution)/shard_map/ppermute | solution.py:118
  134.6 61.4 %collective-permute-start.25 = (bf16[3,2,2,2,16,4096]{5,4,3,2,1,0:T(8,128)(2,1)}, bf16[3,2,2,2,16,4096]{5,4,3,2,1,0:T(8,128)(2,1)}, u32[]{:S(2)}, u32[]{:S(2)}) collective-permute-start(bf16[3,2,2,2,16,4096]{5,4,3,2,1,0:T(8,128)(2,1)} %get-tuple-element.37), channel_id=1, source_target_pairs={{0,4},{4,0},{8,12},{12,8},{16,20},{20,16},{24,28},{28,24},{1,5},{5... | collective-permute-start | bytes 9437192 | tf_op jit(solution)/shard_map/ppermute | solution.py:118
  150.5 55.2 %collective-permute-start.33 = (bf16[3,2,2,2,64,1024]{5,4,3,2,1,0:T(8,128)(2,1)}, bf16[3,2,2,2,64,1024]{5,4,3,2,1,0:T(8,128)(2,1)}, u32[]{:S(2)}, u32[]{:S(2)}) collective-permute-start(bf16[3,2,2,2,64,1024]{5,4,3,2,1,0:T(8,128)(2,1)} %get-tuple-element.35), channel_id=1, source_target_pairs={{0,4},{4,0},{8,12},{12,8},{16,20},{20,16},{24,28},{28,24},{1,5},{5... | collective-permute-start | bytes 9437192 | tf_op jit(solution)/shard_map/ppermute | solution.py:118
  332.1 57.2 %collective-permute-start.34 = (bf16[4,2,2,2,16,3200]{5,4,3,2,1,0:T(8,128)(2,1)S(1)}, bf16[4,2,2,2,16,3200]{5,4,3,2,1,0:T(8,128)(2,1)}, u32[]{:S(2)}, u32[]{:S(2)}) collective-permute-start(bf16[4,2,2,2,16,3200]{5,4,3,2,1,0:T(8,128)(2,1)S(1)} %fusion.18), channel_id=1, source_target_pairs={{0,4},{4,0},{8,12},{12,8},{16,20},{20,16},{24,28},{28,24},{1,5},{5... | collective-permute-start | bytes 9830408 | tf_op jit(solution)/shard_map/ppermute | solution.py:133
  374.2 44.2 %collective-permute-start.58 = (bf16[4,2,2,2,16,4096]{5,4,3,2,1,0:T(8,128)(2,1)S(1)}, bf16[4,2,2,2,16,4096]{5,4,3,2,1,0:T(8,128)(2,1)}, u32[]{:S(2)}, u32[]{:S(2)}) collective-permute-start(bf16[4,2,2,2,16,4096]{5,4,3,2,1,0:T(8,128)(2,1)S(1)} %dynamic-slice_bitcast_fusion.1), channel_id=1, source_target_pairs={{0,4},{4,0},{8,12},{12,8},{16,20},{20,16},{24,28},{28,24},{1,5},{5... | collective-permute-start | bytes 12582920 | tf_op jit(solution)/shard_map/ppermute | solution.py:133
  387.5 41.1 %collective-permute-start.70 = (bf16[4,2,2,2,64,1024]{5,4,3,2,1,0:T(8,128)(2,1)S(1)}, bf16[4,2,2,2,64,1024]{5,4,3,2,1,0:T(8,128)(2,1)}, u32[]{:S(2)}, u32[]{:S(2)}) collective-permute-start(bf16[4,2,2,2,64,1024]{5,4,3,2,1,0:T(8,128)(2,1)S(1)} %dynamic-slice_bitcast_fusion), channel_id=1, source_target_pairs={{0,4},{4,0},{8,12},{12,8},{16,20},{20,16},{24,28},{28,24},{1,5},{5... | collective-permute-start | bytes 12582920 | tf_op jit(solution)/shard_map/ppermute | solution.py:133
  425.5 43.5 %collective-permute-start.59 = (bf16[4,2,16,4096]{3,2,0,1:T(8,128)(2,1)}, bf16[4,2,16,4096]{3,2,0,1:T(8,128)(2,1)}, u32[]{:S(2)}, u32[]{:S(2)}) collective-permute-start(bf16[4,2,16,4096]{3,2,0,1:T(8,128)(2,1)} %fusion.78), channel_id=1, source_target_pairs={{0,16},{4,20},{8,24},{12,28},{16,0},{20,4},{24,8},{28,12},{1,17},{... | collective-permute-start | bytes 3145736 | tf_op jit(solution)/shard_map/ppermute | solution.py:133
  427.6 44.1 %collective-permute-start.61 = (bf16[4,2,16,4096]{3,2,1,0:T(8,128)(2,1)}, bf16[4,2,16,4096]{3,2,1,0:T(8,128)(2,1)}, u32[]{:S(2)}, u32[]{:S(2)}) collective-permute-start(bf16[4,2,16,4096]{3,2,1,0:T(8,128)(2,1)} %fusion.76), channel_id=1, source_target_pairs={{0,8},{4,12},{8,0},{12,4},{16,24},{20,28},{24,16},{28,20},{1,9},{5... | collective-permute-start | bytes 3145736 | tf_op jit(solution)/shard_map/ppermute | solution.py:133
  464.0 26.0 %collective-permute-start.71 = (bf16[4,2,64,1024]{3,2,0,1:T(8,128)(2,1)S(1)}, bf16[4,2,64,1024]{3,2,0,1:T(8,128)(2,1)S(1)}, u32[]{:S(2)}, u32[]{:S(2)}) collective-permute-start(bf16[4,2,64,1024]{3,2,0,1:T(8,128)(2,1)S(1)} %fusion.79), channel_id=1, source_target_pairs={{0,16},{4,20},{8,24},{12,28},{16,0},{20,4},{24,8},{28,12},{1,17},{... | collective-permute-start | bytes 3145736 | tf_op jit(solution)/shard_map/ppermute | solution.py:133
  467.4 26.0 %collective-permute-start.73 = (bf16[4,2,64,1024]{3,2,1,0:T(8,128)(2,1)S(1)}, bf16[4,2,64,1024]{3,2,1,0:T(8,128)(2,1)S(1)}, u32[]{:S(2)}, u32[]{:S(2)}) collective-permute-start(bf16[4,2,64,1024]{3,2,1,0:T(8,128)(2,1)S(1)} %fusion.77), channel_id=1, source_target_pairs={{0,8},{4,12},{8,0},{12,4},{16,24},{20,28},{24,16},{28,20},{1,9},{5... | collective-permute-start | bytes 3145736 | tf_op jit(solution)/shard_map/ppermute | solution.py:133
  468.7 52.0 %collective-permute-start.45 = (bf16[2,2,2,16,3200]{4,3,2,1,0:T(8,128)(2,1)S(1)}, bf16[2,2,2,16,3200]{4,3,2,1,0:T(8,128)(2,1)S(1)}, u32[]{:S(2)}, u32[]{:S(2)}) collective-permute-start(bf16[2,2,2,16,3200]{4,3,2,1,0:T(8,128)(2,1)S(1)} %reverse_select_fusion.4), channel_id=1, source_target_pairs={{0,4},{4,0},{8,12},{12,8},{16,20},{20,16},{24,28},{28,24},{1,5},{5... | collective-permute-start | bytes 2457608 | tf_op jit(solution)/shard_map/ppermute | solution.py:118
  470.5 34.1 %collective-permute-start.60 = (bf16[4,16,4096]{2,1,0:T(8,128)(2,1)S(1)}, bf16[4,16,4096]{2,1,0:T(8,128)(2,1)S(1)}, u32[]{:S(2)}, u32[]{:S(2)}) collective-permute-start(bf16[4,16,4096]{2,1,0:T(8,128)(2,1)S(1)} %fusion.93), channel_id=1, source_target_pairs={{0,8},{4,12},{8,0},{12,4},{16,24},{20,28},{24,16},{28,20},{1,9},{5... | collective-permute-start | bytes 1572872 | tf_op jit(solution)/shard_map/ppermute | solution.py:133
  473.2 31.5 %collective-permute-start.62 = (bf16[4,16,4096]{2,1,0:T(8,128)(2,1)S(1)}, bf16[4,16,4096]{2,1,0:T(8,128)(2,1)S(1)}, u32[]{:S(2)}, u32[]{:S(2)}) collective-permute-start(bf16[4,16,4096]{2,1,0:T(8,128)(2,1)S(1)} %fusion.94), channel_id=1, source_target_pairs={{0,16},{4,20},{8,24},{12,28},{16,0},{20,4},{24,8},{28,12},{1,17},{... | collective-permute-start | bytes 1572872 | tf_op jit(solution)/shard_map/ppermute | solution.py:133
  490.4 24.4 %collective-permute-start.72 = (bf16[4,64,1024]{2,1,0:T(8,128)(2,1)S(1)}, bf16[4,64,1024]{2,1,0:T(8,128)(2,1)S(1)}, u32[]{:S(2)}, u32[]{:S(2)}) collective-permute-start(bf16[4,64,1024]{2,1,0:T(8,128)(2,1)S(1)} %fusion.95), channel_id=1, source_target_pairs={{0,8},{4,12},{8,0},{12,4},{16,24},{20,28},{24,16},{28,20},{1,9},{5... | collective-permute-start | bytes 1572872 | tf_op jit(solution)/shard_map/ppermute | solution.py:133
  (115 other events, 1136.2 us)
